TPU v7x, 32 devices: a whole 2x2x4 slice. The times are simulated.
32 devices in a mesh: out: 8 (over z, y), inp: 4 (over x, core).
Axes of the slice: x: 2, y: 2, z: 4, core: 2. Of those that a mesh axis runs over, the one named last changes fastest.
Arguments:
- weight: float32 [8, 512, 13824], P(None, 'out', 'inp'), may hold values from -6 to 6
- gradient: bfloat16 [8, 512, 13824], P(None, 'out', 'inp'), may hold values from -60 to 60
- momentum: bfloat16 [8, 512, 13824], P(None, 'out', 'inp'), may hold values from -6 to 6
Outputs:
- weight_next: float32 [8, 512, 13824], P(None, 'out', 'inp')
- momentum_next: bfloat16 [8, 512, 13824], P(None, 'out', 'inp')
All inputs are finite; a program needn't handle non-finite values.
Results may differ from a plain program's by a relative error of at most 0.0039.
Values may be sent and summed in bfloat16 or wider, within the bound.
No kernel may reach another device: no remote copies, remote signals or barrier semaphores. Data moves between devices by JAX's collectives and lax.ppermute only.
A program may use at most 64 MiB of HBM per device.

v0:
```python
import math

import jax
import jax.numpy as jnp
from jax import lax
from jax.sharding import PartitionSpec as P

ITERS = 5
COLS = 13824


BETA = 0.95
EPSILON = 1e-06
COEF_A = 3.4445
COEF_B = -4.775
COEF_C = 2.0315


def mult(former, latter):
    return jnp.einsum("kij,kjl->kil", former, latter, precision=lax.Precision.HIGHEST)


def on_device(weight, gradient, momentum):
    moment = BETA * momentum.astype(jnp.float32) + gradient.astype(jnp.float32)
    source = (gradient.astype(jnp.float32) + BETA * moment).astype(jnp.bfloat16)
    local_squares = jnp.einsum("kic,kic->k", source, source, preferred_element_type=jnp.float32)
    totals = lax.psum(local_squares, ("out", "inp")) + EPSILON
    regrouped = lax.all_to_all(source, "out", split_axis=0, concat_axis=1, tiled=True)
    held = regrouped.shape[0]
    width = regrouped.shape[1]
    partial_value = jnp.einsum(
        "kic,kjc->kij", regrouped, regrouped, preferred_element_type=jnp.float32
    )
    scale2 = lax.dynamic_slice_in_dim(totals, lax.axis_index("out") * held, held, 0)
    gram = lax.psum(partial_value.astype(jnp.bfloat16), "inp").astype(jnp.float32)
    current = gram / scale2[:, None, None]
    transform = jnp.broadcast_to(jnp.eye(width, dtype=jnp.float32), (held, width, width))
    for sweep in range(ITERS):
        poly_part = COEF_B * current + COEF_C * mult(current, current)
        transform = COEF_A * transform + mult(poly_part, transform)
        halfway = COEF_A * current + mult(poly_part, current)
        current = COEF_A * halfway + mult(halfway, poly_part)
    factor = (transform / jnp.sqrt(scale2)[:, None, None]).astype(jnp.bfloat16)
    orthogonal = jnp.einsum("kij,kjc->kic", factor, regrouped, preferred_element_type=jnp.float32)
    update = (0.2 * math.sqrt(COLS) * orthogonal).astype(jnp.bfloat16)
    returned = lax.all_to_all(update, "out", split_axis=1, concat_axis=0, tiled=True)
    weight_next = 0.9 * weight - 0.5 * returned.astype(jnp.float32)
    return (weight_next, moment.astype(jnp.bfloat16))


def solution(mesh):
    return jax.shard_map(
        on_device,
        mesh=mesh,
        in_specs=(P(None, "out", "inp"), P(None, "out", "inp"), P(None, "out", "inp")),
        out_specs=(P(None, "out", "inp"), P(None, "out", "inp")),
        check_vma=False,
    )
```

profile of v0, /device:TPU:0, one launch (start us, length us, event | category | flops | bytes accessed | tf_op | source)
XLA Modules:
  0.0 335.6 jit_solution(17814851323513137917)
XLA Ops:
  7.2 4.2 %fusion.1 = (f32[8]{0:T(128)S(1)}, bf16[8,64,3456]{2,1,0:T(8,128)(2,1)S(1)}) fusion(bf16[8,64,3456]{2,1,0:T(8,128)(2,1)} %param.5, bf16[8,64,3456]{2,1,0:T(8,128)(2,1)} %param.4), kind=kLoop, calls=%fused_computation.4 | loop fusion | flops 17694712 | bytes 10616864 | tf_op jit(solution)/shard_map/kic,kic->k/dot_general | solution.py:26
  11.4 86.6 %all_to_all.8 = bf16[8,64,3456]{2,1,0:T(8,128)(2,1)S(1)} all-to-all(bf16[8,64,3456]{2,1,0:T(8,128)(2,1)S(1)} %get-tuple-element.3), channel_id=1, replica_groups=mesh['out'=8,'inp'=4] {'out'}, dimensions={0} | all-to-all | bytes 7077888 | tf_op jit(solution)/shard_map/all_to_all | solution.py:28
  98.0 2.9 fusion.29
  100.9 38.8 %psum.15 = f32[8]{0:T(128)S(1)} all-reduce(f32[8]{0:T(128)S(1)} %get-tuple-element.2), channel_id=1, replica_groups=mesh['out'=8,'inp'=4] {'out','inp'}, use_global_device_ids=true, to_apply=%region_1.0 | all-reduce | flops 8 | bytes 64 | tf_op jit(solution)/shard_map/psum | solution.py:27
  141.1 4.1 %fusion.11 = f32[512,512]{1,0:T(8,128)S(1)} fusion(bf16[1,512,512]{2,1,0:T(8,128)(2,1)} %all-reduce.2.cloned.1.call-done, f32[]{:T(128)} %bitcast.4), kind=kOutput, calls=%fused_computation.35 | convolution fusion | flops 1612447744 | bytes 1572868 | tf_op jit(solution)/shard_map/kij,kjl->kil/dot_general | solution.py:20
  146.2 2.6 fusion.12
  148.8 1.8 fusion.13
  150.6 1.9 fusion.15
  152.5 1.8 fusion.16
  154.4 1.8 fusion.17
  156.2 2.1 fusion.19
  158.3 1.8 convolution_add_fusion.3
  160.2 1.8 fusion.20
  162.1 1.8 convolution_add_fusion.2
  163.9 1.8 fusion.21
  165.8 1.9 fusion.23
  167.7 1.8 fusion.24
  169.5 2.3 convolution_add_fusion.1
  171.8 1.8 fusion.25
  173.6 1.9 fusion.27
  175.5 1.9 fusion.28
  177.4 2.1 fusion.3
  179.6 19.5 %copy.14 = bf16[1,512,3456]{2,0,1:T(2,128)(2,1)} copy(bf16[1,512,3456]{2,1,0:T(8,128)(2,1)S(1)} %fusion.3) | data formatting | bytes 7077888 | tf_op jit(solution)/shard_map/convert_element_type | solution.py:45
  199.6 22.1 %reduce.2 = bf16[512,3456]{1,0:T(8,128)(2,1)S(1)} reduce(bf16[512,1,3456]{2,1,0:T(2,128)(2,1)} %bitcast.144, bf16[]{:T(256)} %broadcast.71), dimensions={1}, to_apply=%bitcast.143.reduce_sub_computation | reduce | bytes 7077890
  221.7 3.7 %reshape.156 = bf16[8,2,110592]{2,1,0:T(2,128)(2,1)} reshape(bf16[512,3456]{1,0:T(8,128)(2,1)S(1)} %reduce.2) | data formatting | bytes 7077888
  225.4 4.8 %all-to-all-start.1 = ((bf16[8,2,110592]{2,1,0:T(2,128)(2,1)}), bf16[8,2,110592]{2,1,0:T(2,128)(2,1)S(1)}, u32[]{:S(2)}, u32[]{:S(2)}) async-start(bf16[8,2,110592]{2,1,0:T(2,128)(2,1)} %reshape.156), calls=%async_computation.1 | async-start | bytes 7077888 | tf_op jit(solution)/shard_map/all_to_all | solution.py:46
  230.3 5.9 %fusion.2 = bf16[8,64,3456]{2,1,0:T(8,128)(2,1)} fusion(bf16[8,64,3456]{2,1,0:T(8,128)(2,1)} %param.4, bf16[8,64,3456]{2,1,0:T(8,128)(2,1)} %param.5), kind=kLoop, calls=%fused_computation.7 | loop fusion | flops 8847360 | bytes 10616832 | tf_op jit(solution)/shard_map/convert_element_type | solution.py:48
  236.2 72.2 %all-to-all-done.1 = bf16[8,2,110592]{2,1,0:T(2,128)(2,1)S(1)} async-done(((bf16[8,2,110592]{2,1,0:T(2,128)(2,1)}), bf16[8,2,110592]{2,1,0:T(2,128)(2,1)S(1)}, u32[]{:S(2)}, u32[]{:S(2)}) %all-to-all-start.1) | async-done | bytes 3538976 | tf_op jit(solution)/shard_map/all_to_all | solution.py:46
  308.4 5.5 %reshape.157 = bf16[512,1,3456]{2,1,0:T(2,128)(2,1)} reshape(bf16[8,2,110592]{2,1,0:T(2,128)(2,1)S(1)} %all-to-all-done.1) | data formatting | bytes 7077888
  313.9 9.0 %convert_multiply_fusion.1 = f32[1,512,3456]{2,0,1:T(1,128)S(1)} fusion(bf16[512,1,3456]{2,1,0:T(2,128)(2,1)} %reshape.157), kind=kLoop, calls=%fused_computation.5 | loop fusion | flops 3538944 | bytes 10616832 | tf_op jit(solution)/shard_map/mul | solution.py:47
  323.4 1.3 slice-done.1
  324.7 3.9 %multiply_subtract_fusion = f32[8,64,3456]{2,1,0:T(8,128)} fusion(f32[8,64,3456]{2,1,0:T(8,128)S(1)} %bitcast.145, f32[8,64,3456]{2,1,0:T(8,128)S(1)} %bitcast.147), kind=kLoop, calls=%fused_computation.8 | loop fusion | flops 3538944 | bytes 21233664 | tf_op jit(solution)/shard_map/sub | solution.py:47
  (14 shorter events, 2.6 us)
Async XLA Ops:
  7.2 133.9 %all-reduce.2.cloned.1.call-start = ((), (), s32[]{:S(2)}) async-start(), calls=%async_computation.2 | async-start | bytes 1048576 | tf_op jit(solution)/shard_map/psum | solution.py:35
  141.1 5.1 %copy-start = (bf16[1,512,512]{2,1,0:T(8,128)(2,1)S(1)}, bf16[1,512,512]{2,1,0:T(8,128)(2,1)}, u32[]{:S(2)}) copy-start(bf16[1,512,512]{2,1,0:T(8,128)(2,1)} %all-reduce.2.cloned.1.call-done) | copy-start | bytes 1572868
  225.4 82.9 %all-to-all-start.1 = ((bf16[8,2,110592]{2,1,0:T(2,128)(2,1)}), bf16[8,2,110592]{2,1,0:T(2,128)(2,1)S(1)}, u32[]{:S(2)}, u32[]{:S(2)}) async-start(bf16[8,2,110592]{2,1,0:T(2,128)(2,1)} %reshape.156), calls=%async_computation.1 | async-start | bytes 7077888 | tf_op jit(solution)/shard_map/all_to_all | solution.py:46
  313.9 9.5 %slice-start = ((s8[7077888]{0:T(1024)(128)(4,1)}), s8[4194304]{0:T(1024)(128)(4,1)S(1)}, s32[]{:S(2)}) async-start(s8[7077888]{0:T(1024)(128)(4,1)} %bitcast.146), calls=%async_computation.3 | async-start | bytes 8388608
  322.9 1.8 slice-start.1
Sparse Core Ops, SparseCore 0:
  101.0 32.1 all-reduce.1
where the time goes:
time: 339 us; the launch traced here: 336 us
  blocking collectives  125 us (37%)
  waiting for transfers between devices  72.2 us (21%)
  other arithmetic  45.2 us (13%)
  matrix products  41.2 us (12%)
  local copies, waits for them, and re-layouts  31.6 us (9%)
  between operations  15.2 us (4%)
  starting transfers between devices  4.87 us (1%)
    all_to_all x1, blocking collectives, on_device(): lax.all_to_all(source, 'out', split_axis=0, concat_axis=1, tiled=True)  86.6 us
    all_to_all x1, waiting for transfers between devices, on_device(): lax.all_to_all(update, 'out', split_axis=1, concat_axis=0, tiled=True)  72.2 us
    psum x1, blocking collectives, on_device(): totals = lax.psum(local_squares, ('out', 'inp')) + EPSILON  38.8 us
    dot_general x18, matrix products, mult(): jnp.einsum('kij,kjl->kil', former, latter, precision=lax.Precision.HIGHEST)  36.2 us
    unnamed x2, other arithmetic  22.1 us
    convert_element_type x1, local copies, waits for them, and re-layouts, on_device(): update = (0.2 * math.sqrt(COLS) * orthogonal).astype(jnp.bfloat16)  19.5 us
    unnamed x10, local copies, waits for them, and re-layouts  11.6 us
    mul x1, other arithmetic, on_device(): weight_next = 0.9 * weight - 0.5 * returned.astype(jnp.float32)  9.03 us
  transfers between devices with their start and end apart: 2, of which 1 were waited for; matrix products, arithmetic and copies ran while one was open for 2% of the time, Pallas kernels for 0%

commit v1 on v0

v1 whole, which is shorter than its diff:
```python
import functools
import math

import jax
import jax.numpy as jnp
from jax import lax
from jax.experimental import pallas as pl
from jax.experimental.pallas import tpu as pltpu
from jax.sharding import PartitionSpec as P

ITERS = 5
GROUPS = 2
SHARE = 2
LANE = 128

BETA = 0.95
EPSILON = 1e-06
COEF_A = 3.4445
COEF_B = -4.775
COEF_C = 2.0315

F32 = jnp.float32
BF16 = jnp.bfloat16
AXES = ("out", "inp")


def source_of(gradient, momentum):
    grads = gradient.astype(F32)
    moment = BETA * momentum.astype(F32) + grads
    return (grads + BETA * moment).astype(BF16)


def params(**kwargs):
    return pltpu.CompilerParams(vmem_limit_bytes=48 * 1024 * 1024, **kwargs)


def cost(flops, size):
    return pl.CostEstimate(flops=int(flops), bytes_accessed=int(size), transcendentals=0)


def pack(read, tiles, rows, first, put, lanes):
    for t in range(tiles):
        put(slice(t * rows, (t + 1) * rows), read(first + t))
    last = read(tiles)
    half = rows // 2
    low = lanes * (LANE // 2)
    piece = last[:, low : low + LANE // 2]
    put(slice(tiles * rows, tiles * rows + half), jnp.concatenate([piece[:half], piece[half:]], axis=1))


def source_body(grad_ref, mom_ref, out_ref, *, rows, tiles):
    source = source_of(grad_ref[0], mom_ref[0])

    def read(t):
        return source[:, t * LANE : (t + 1) * LANE]

    for side in range(SHARE):

        def put(where, value, side=side):
            out_ref[side, where, :] = value

        pack(read, tiles, rows, side * (tiles + 1), put, side)


def source_call(gradient, momentum, group, per_group, tiles):
    kernels, rows, width = gradient.shape
    packed = tiles * rows + rows // 2
    return pl.pallas_call(
        functools.partial(source_body, rows=rows, tiles=tiles),
        grid=(per_group,),
        in_specs=[
            pl.BlockSpec((1, rows, width), lambda k: (group * per_group + k, 0, 0)),
            pl.BlockSpec((1, rows, width), lambda k: (group * per_group + k, 0, 0)),
        ],
        out_specs=pl.BlockSpec((SHARE, packed, LANE), lambda k: (k, 0, 0)),
        out_shape=jax.ShapeDtypeStruct((per_group * SHARE, packed, LANE), BF16),
        compiler_params=params(),
        cost_estimate=cost(per_group * rows * width * 6, per_group * rows * width * 6),
        name=f"source{group}",
    )(gradient, momentum)


def gram_body(core_ref, in_ref, x_ref, keep_ref, send_ref, gram_ref, *, blocks, rows, tiles):
    half = rows // 2
    zeros = jnp.zeros((half, LANE // 2), BF16)
    for s in range(blocks):
        base = s * rows
        for t in range(tiles):
            x_ref[base : base + rows, t * LANE : (t + 1) * LANE] = in_ref[s, t * rows : (t + 1) * rows, :]
        last = in_ref[s, tiles * rows : tiles * rows + half, :]
        columns = slice(tiles * LANE, (tiles + 1) * LANE)
        x_ref[base : base + half, columns] = jnp.concatenate([last[:, : LANE // 2], zeros], axis=1)
        x_ref[base + half : base + rows, columns] = jnp.concatenate([last[:, LANE // 2 :], zeros], axis=1)
    x = x_ref[...]
    gram_ref[...] = lax.dot_general(x, x, (((1,), (1,)), ((), ())), preferred_element_type=F32)
    size = gram_ref.shape[0] // 2
    core = core_ref[0]
    keep_ref[...] = gram_ref[pl.ds(pl.multiple_of(core * size, size), size), :]
    send_ref[...] = gram_ref[pl.ds(pl.multiple_of((1 - core) * size, size), size), :].astype(BF16)


def vmem():
    return pl.BlockSpec(memory_space=pltpu.VMEM)


def smem():
    return pl.BlockSpec(memory_space=pltpu.SMEM)


def gram_call(core, received, rows, tiles, group):
    blocks = received.shape[0]
    size = blocks * rows
    columns = (tiles + 1) * LANE
    return pl.pallas_call(
        functools.partial(gram_body, blocks=blocks, rows=rows, tiles=tiles),
        in_specs=[smem(), vmem()],
        out_specs=[vmem(), vmem(), vmem()],
        out_shape=[
            jax.ShapeDtypeStruct((size, columns), BF16),
            jax.ShapeDtypeStruct((size // 2, size), F32),
            jax.ShapeDtypeStruct((size // 2, size), BF16),
        ],
        scratch_shapes=[pltpu.VMEM((size, size), F32)],
        compiler_params=params(),
        cost_estimate=cost(2 * size * size * columns, 4 * size * columns),
        name=f"gram{group}",
    )(core, received)


def split_body(chip_ref, keep_ref, got_ref, own_ref, *rest, piece):
    *send_refs, total_ref = rest
    total_ref[...] = keep_ref[...] + got_ref[...].astype(F32)
    chip = chip_ref[0]

    def rows_of(m):
        return total_ref[pl.ds(pl.multiple_of((chip ^ m) * piece, piece), piece), :]

    own_ref[...] = rows_of(0)
    for m, ref in enumerate(send_refs):
        ref[...] = rows_of(m + 1).astype(BF16)


def split_call(chip, keep, got, chips, group):
    half, size = keep.shape
    piece = half // chips
    return pl.pallas_call(
        functools.partial(split_body, piece=piece),
        in_specs=[smem(), vmem(), vmem()],
        out_specs=[vmem() for _ in range(chips)],
        out_shape=[jax.ShapeDtypeStruct((piece, size), F32 if m == 0 else BF16) for m in range(chips)],
        scratch_shapes=[pltpu.VMEM((half, size), F32)],
        compiler_params=params(),
        cost_estimate=cost(half * size * 4, half * size * 8),
        name=f"split{group}",
    )(chip, keep, got)


def add_body(own_ref, *refs):
    *got_refs, out_ref = refs
    total = own_ref[...]
    for ref in got_refs:
        total = total + ref[...].astype(F32)
    out_ref[...] = total.astype(BF16)


def add_call(own, got, group):
    return pl.pallas_call(
        add_body,
        in_specs=[vmem() for _ in range(1 + len(got))],
        out_specs=vmem(),
        out_shape=jax.ShapeDtypeStruct(own.shape, BF16),
        compiler_params=params(),
        cost_estimate=cost(own.size * 4, own.size * 8),
        name=f"add{group}",
    )(own, *got)


def join_body(chip_ref, *refs):
    *in_refs, out_ref = refs
    piece = in_refs[0].shape[0]
    for m, ref in enumerate(in_refs):
        out_ref[pl.ds(pl.multiple_of((chip_ref[0] ^ m) * piece, piece), piece), :] = ref[...]


def join_call(chip, pieces, group):
    piece, size = pieces[0].shape
    return pl.pallas_call(
        join_body,
        in_specs=[smem()] + [vmem() for _ in pieces],
        out_specs=vmem(),
        out_shape=jax.ShapeDtypeStruct((piece * len(pieces), size), BF16),
        compiler_params=params(),
        cost_estimate=cost(piece * len(pieces) * size, 4 * piece * len(pieces) * size),
        name=f"join{group}",
    )(chip, *pieces)


def newton_body(core_ref, own_ref, got_ref, out_ref, r_ref, q_ref, y_ref, r2_ref, p2_ref, q2_ref, y2_ref):
    half, size = own_ref.shape
    core = core_ref[0]
    r_ref[pl.ds(pl.multiple_of(core * half, half), half), :] = own_ref[...].astype(F32)
    r_ref[pl.ds(pl.multiple_of((1 - core) * half, half), half), :] = got_ref[...].astype(F32)
    row = lax.broadcasted_iota(jnp.int32, (size, size), 0)
    column = lax.broadcasted_iota(jnp.int32, (size, size), 1)
    eye = row == column
    gram = r_ref[...]
    scale2 = jnp.sum(jnp.where(eye, gram, 0.0)) + EPSILON
    r_ref[...] = gram / scale2

    def halves(ref, value):
        high = value.astype(BF16)
        ref[0] = high
        ref[1] = (value - high.astype(F32)).astype(BF16)

    def mult(left, right):
        def one(i, j):
            return jnp.dot(left[i], right[j], preferred_element_type=F32)

        return one(0, 0) + (one(0, 1) + one(1, 0))

    def poly():
        halves(r2_ref, r_ref[...])
        return COEF_B * r_ref[...] + COEF_C * mult(r2_ref, r2_ref)

    def advance():
        halfway = COEF_A * r_ref[...] + mult(p2_ref, r2_ref)
        halves(y2_ref, halfway)
        y_ref[...] = halfway
        r_ref[...] = COEF_A * y_ref[...] + mult(y2_ref, p2_ref)

    first = poly()
    halves(p2_ref, first)
    q_ref[...] = jnp.where(eye, COEF_A, 0.0) + first
    advance()

    def sweep(_, carry):
        halves(p2_ref, poly())
        halves(q2_ref, q_ref[...])
        q_ref[...] = COEF_A * q_ref[...] + mult(p2_ref, q2_ref)
        advance()
        return carry

    lax.fori_loop(1, ITERS - 1, sweep, 0)
    halves(p2_ref, poly())
    halves(q2_ref, q_ref[...])
    final = COEF_A * q_ref[...] + mult(p2_ref, q2_ref)
    out_ref[...] = (final / jnp.sqrt(scale2)).astype(BF16)


def newton_call(core, own, got, group):
    half, size = own.shape
    return pl.pallas_call(
        newton_body,
        in_specs=[smem(), vmem(), vmem()],
        out_specs=vmem(),
        out_shape=jax.ShapeDtypeStruct((size, size), BF16),
        scratch_shapes=[pltpu.VMEM((size, size), F32)] * 3 + [pltpu.VMEM((2, size, size), BF16)] * 4,
        compiler_params=params(),
        cost_estimate=cost(6 * 17 * size**3, 6 * size * size),
        name=f"newton{group}",
    )(core, own, got)


def update_body(factor_ref, x_ref, out_ref, *, blocks, rows, tiles, scale):
    half = rows // 2
    factor = factor_ref[...]
    step = 2
    for t in range(0, tiles + 1, step):
        part = jnp.dot(factor, x_ref[:, t * LANE : (t + step) * LANE], preferred_element_type=F32)
        part = (scale * part).astype(BF16)
        for u in range(t, min(t + step, tiles + 1)):
            tile = part[:, (u - t) * LANE : (u - t + 1) * LANE]
            for s in range(blocks):
                block = tile[s * rows : (s + 1) * rows, :]
                if u < tiles:
                    out_ref[s, u * rows : (u + 1) * rows, :] = block
                else:
                    low = block[:, : LANE // 2]
                    out_ref[s, tiles * rows : tiles * rows + half, :] = jnp.concatenate([low[:half], low[half:]], axis=1)


def update_call(factor, x, rows, tiles, scale, group):
    size = factor.shape[0]
    blocks = size // rows
    packed = tiles * rows + rows // 2
    return pl.pallas_call(
        functools.partial(update_body, blocks=blocks, rows=rows, tiles=tiles, scale=scale),
        in_specs=[vmem(), vmem()],
        out_specs=vmem(),
        out_shape=jax.ShapeDtypeStruct((blocks, packed, LANE), BF16),
        compiler_params=params(),
        cost_estimate=cost(2 * size * size * x.shape[1], 4 * x.size),
        name=f"update{group}",
    )(factor, x)


def finish_body(*refs, rows, tiles):
    got_ref, weight_ref, out_ref = refs[0], refs[1], refs[-1]
    half = rows // 2

    def put(where, update):
        out_ref[0, :, where] = 0.9 * weight_ref[0, :, where] - 0.5 * update.astype(F32)

    for side in range(SHARE):
        for t in range(tiles):
            column = side * (tiles + 1) + t
            put(slice(column * LANE, (column + 1) * LANE), got_ref[side, t * rows : (t + 1) * rows, :])
    left, right = (got_ref[side, tiles * rows : tiles * rows + half, :] for side in range(SHARE))
    middle = LANE // 2
    upper = jnp.concatenate([left[:, :middle], right[:, :middle]], axis=1)
    lower = jnp.concatenate([left[:, middle:], right[:, middle:]], axis=1)
    put(slice(tiles * LANE, (tiles + 1) * LANE), jnp.concatenate([upper, lower], axis=0))


def finish_call(returned, weight, base, group, per_group, tiles):
    kernels, rows, width = weight.shape
    packed = tiles * rows + rows // 2
    where = lambda k: (group * per_group + k, 0, 0)
    more = [] if base is None else [base]
    return pl.pallas_call(
        functools.partial(finish_body, rows=rows, tiles=tiles),
        grid=(per_group,),
        in_specs=[
            pl.BlockSpec((SHARE, packed, LANE), lambda k: (k, 0, 0)),
            pl.BlockSpec((1, rows, width), where),
        ]
        + [pl.BlockSpec(memory_space=pl.ANY) for _ in more],
        out_specs=pl.BlockSpec((1, rows, width), where),
        out_shape=jax.ShapeDtypeStruct(weight.shape, F32),
        input_output_aliases={2: 0} if more else {},
        compiler_params=params(),
        cost_estimate=cost(per_group * rows * width * 3, per_group * rows * width * 10),
        name=f"finish{group}",
    )(returned, weight, *more)


def exchange(value, bits, count):
    return lax.ppermute(value, AXES, [(i, i ^ bits) for i in range(count)])


def pipelined(weight, gradient, momentum, n, inner):
    kernels, rows, width = weight.shape
    per_group = kernels // GROUPS
    tiles = width // LANE // SHARE
    scale = 0.2 * math.sqrt(width * inner)
    devices = n * inner
    chips = SHARE * inner // 2
    index = lax.axis_index(AXES)
    core = (index % 2).astype(jnp.int32).reshape(1)
    chip = (index // 2 % chips).astype(jnp.int32).reshape(1)

    def regroup(value):
        return lax.all_to_all(value, "out", split_axis=0, concat_axis=0, tiled=True)

    def factor_of(received, group):
        x, keep, send = gram_call(core, received, rows, tiles, group)
        own, *send = split_call(chip, keep, exchange(send, 1, devices), chips, group)
        got = [exchange(value, 2 * (m + 1), devices) for m, value in enumerate(send)]
        piece = add_call(own, got, group)
        pieces = [piece] + [exchange(piece, 2 * m, devices) for m in range(1, chips)]
        half = join_call(chip, pieces, group)
        factor = newton_call(core, half, exchange(half, 1, devices), group)
        return update_call(factor, x, rows, tiles, scale, group)

    sent = [source_call(gradient, momentum, g, per_group, tiles) for g in range(GROUPS)]
    received = [regroup(value) for value in sent]
    moment = (BETA * momentum.astype(F32) + gradient.astype(F32)).astype(BF16)
    updates = [factor_of(value, g) for g, value in enumerate(received)]
    returned = [regroup(value) for value in updates]
    result = None
    for g, value in enumerate(returned):
        result = finish_call(value, weight, result, g, per_group, tiles)
    return (result, moment)


def mult(former, latter):
    return jnp.einsum("kij,kjl->kil", former, latter, precision=lax.Precision.HIGHEST)


def whole_kernels(weight, gradient, momentum, n, inner):
    moment = BETA * momentum.astype(F32) + gradient.astype(F32)
    source = source_of(gradient, momentum)
    kernels, rows, columns = source.shape
    held = kernels // n
    width = rows * n
    regrouped = lax.all_to_all(source, "out", split_axis=0, concat_axis=1, tiled=True)
    partial_value = jnp.einsum("kic,kjc->kij", regrouped, regrouped, preferred_element_type=F32)
    gram = lax.psum(partial_value.astype(BF16), "inp").astype(F32)
    scale2 = jnp.trace(gram, axis1=1, axis2=2) + EPSILON
    current = gram / scale2[:, None, None]
    transform = jnp.broadcast_to(jnp.eye(width, dtype=F32), (held, width, width))
    for sweep in range(ITERS):
        poly_part = COEF_B * current + COEF_C * mult(current, current)
        transform = COEF_A * transform + mult(poly_part, transform)
        halfway = COEF_A * current + mult(poly_part, current)
        current = COEF_A * halfway + mult(halfway, poly_part)
    factor = (transform / jnp.sqrt(scale2)[:, None, None]).astype(BF16)
    orthogonal = jnp.einsum("kij,kjc->kic", factor, regrouped, preferred_element_type=F32)
    update = (0.2 * math.sqrt(columns * inner) * orthogonal).astype(BF16)
    returned = lax.all_to_all(update, "out", split_axis=1, concat_axis=0, tiled=True)
    weight_next = 0.9 * weight - 0.5 * returned.astype(F32)
    return (weight_next, moment.astype(BF16))


def solution(mesh):
    n, inner = mesh.shape["out"], mesh.shape["inp"]

    def on_device(weight, gradient, momentum):
        kernels, rows, width = weight.shape
        chips = SHARE * inner // 2
        fits = (
            kernels % GROUPS == 0
            and n * GROUPS == kernels * SHARE
            and width % (SHARE * LANE) == LANE
            and rows % 32 == 0
            and inner >= 2
            and inner & (inner - 1) == 0
            and n * rows % (2 * chips * 16) == 0
        )
        run = pipelined if fits else whole_kernels
        return run(weight, gradient, momentum, n, inner)

    return jax.shard_map(
        on_device,
        mesh=mesh,
        in_specs=(P(None, "out", "inp"), P(None, "out", "inp"), P(None, "out", "inp")),
        out_specs=(P(None, "out", "inp"), P(None, "out", "inp")),
        check_vma=False,
    )
```

time: 339 us -> 224 us (0.66)
  blocking collectives: 125 us -> 0 us
  Pallas kernels: 0 us -> 57.6 us
  matrix products: 41.2 us -> 0 us
  other arithmetic: 45.2 us -> 4.83 us
  starting transfers between devices: 4.87 us -> 44.2 us
  waiting for transfers between devices: 72.2 us -> 106 us
  local copies, waits for them, and re-layouts: 31.6 us -> 9.95 us
  between operations: 15.2 us -> 0.82 us
    all_to_all x1 -> x0, blocking collectives: 86.6 us -> none  [on_device(): lax.all_to_all(source, 'out', split_axis=0, concat_axis=1, tiled=True)]
    pallas_call x0 -> x16, Pallas kernels: none -> 57.6 us  [the longest x2 31.7 us: newton_call(): pl.pallas_call(newton_body, in_specs=[smem(), vmem(), vmem()], out_specs=...]
    dot_general x20 -> x0, matrix products: 41.2 us -> none  [the longest x18 36.2 us: mult(): jnp.einsum('kij,kjl->kil', former, latter, precision=lax.Precision.HIGHEST)]
    psum x1 -> x0, blocking collectives: 38.8 us -> none  [on_device(): totals = lax.psum(local_squares, ('out', 'inp')) + EPSILON]
    ppermute x0 -> x16, waiting for transfers between devices: none -> 36.7 us  [exchange(): return lax.ppermute(value, AXES, [(i, i ^ bits) for i in range(count)])]
    all_to_all x1 -> x4, starting transfers between devices: 4.83 us -> 28.8 us  [regroup(): return lax.all_to_all(value, 'out', split_axis=0, concat_axis=0, tiled=True)]
    unnamed x2 -> x0, other arithmetic: 22.1 us -> none
    convert_element_type x1 -> x0, local copies, waits for them, and re-layouts: 19.5 us -> none  [on_device(): update = (0.2 * math.sqrt(COLS) * orthogonal).astype(jnp.bfloat16)]
  transfers between devices with their start and end apart: 2 -> 20, of which waited for: 1 -> 13; matrix products, arithmetic and copies ran while one was open for 2% -> 2% of each run, Pallas kernels for 0% -> 22%
where the time goes in v1:
time: 224 us; the launch traced here: 223 us
  waiting for transfers between devices  106 us (47%)
  Pallas kernels  57.6 us (26%)
  starting transfers between devices  44.2 us (20%)
  local copies, waits for them, and re-layouts  9.95 us (4%)
  other arithmetic  4.83 us (2%)
    all_to_all x4, waiting for transfers between devices, regroup(): return lax.all_to_all(value, 'out', split_axis=0, concat_axis=0, tiled=True)  69.1 us
    ppermute x16, waiting for transfers between devices, exchange(): return lax.ppermute(value, AXES, [(i, i ^ bits) for i in range(count)])  36.7 us
    pallas_call x2, Pallas kernels, newton_call(): pl.pallas_call(newton_body, in_specs=[smem(), vmem(), vmem()], out_specs=...  31.7 us
    all_to_all x4, starting transfers between devices, regroup(): return lax.all_to_all(value, 'out', split_axis=0, concat_axis=0, tiled=True)  28.8 us
    ppermute x16, starting transfers between devices, exchange(): return lax.ppermute(value, AXES, [(i, i ^ bits) for i in range(count)])  15.4 us
    unnamed x20, local copies, waits for them, and re-layouts  9.95 us
    pallas_call x2, Pallas kernels, finish_call(): pl.pallas_call(functools.partial(finish_body, rows=rows, tiles=tiles), gr...  9.73 us
    pallas_call x2, Pallas kernels, source_call(): pl.pallas_call(functools.partial(source_body, rows=rows, tiles=tiles), gr...  6.26 us
  transfers between devices with their start and end apart: 20, of which 13 were waited for; matrix products, arithmetic and copies ran while one was open for 2% of the time, Pallas kernels for 22%

profile of v1, /device:TPU:0, one launch (start us, length us, event | category | flops | bytes accessed | tf_op | source)
XLA Modules:
  0.0 223.1 jit_solution(14783741185447691631)
XLA Ops:
  0.6 2.0 copy-done
  2.6 3.1 %source0.1 = bf16[8,864,128]{2,1,0:T(8,128)(2,1)S(1)} custom-call(bf16[8,64,3456]{2,1,0:T(8,128)(2,1)S(1)} %copy-done, bf16[8,64,3456]{2,1,0:T(8,128)(2,1)} %mom_ref.3), custom_call_target="tpu_custom_call" | custom-call | flops 5308416 | bytes 5308416 | tf_op jit(solution)/shard_map/source0/pallas_call | solution.py:68
  7.0 7.6 %all-to-all-start.2 = ((bf16[8,864,128]{2,1,0:T(8,128)(2,1)}), bf16[8,864,128]{2,1,0:T(8,128)(2,1)}, u32[]{:S(2)}, u32[]{:S(2)}) async-start(bf16[8,864,128]{2,1,0:T(8,128)(2,1)} %copy-done.5), calls=%async_computation.2 | async-start | bytes 3538944 | tf_op jit(solution)/shard_map/all_to_all | solution.py:353
  14.6 3.1 %source1.1 = bf16[8,864,128]{2,1,0:T(8,128)(2,1)S(1)} custom-call(bf16[8,64,3456]{2,1,0:T(8,128)(2,1)S(1)} %copy-done.1, bf16[8,64,3456]{2,1,0:T(8,128)(2,1)} %mom_ref.3), custom_call_target="tpu_custom_call" | custom-call | flops 5308416 | bytes 5308416 | tf_op jit(solution)/shard_map/source1/pallas_call | solution.py:68
  18.9 37.0 %all-to-all-done.2.in_ref = bf16[8,864,128]{2,1,0:T(8,128)(2,1)} async-done(((bf16[8,864,128]{2,1,0:T(8,128)(2,1)}), bf16[8,864,128]{2,1,0:T(8,128)(2,1)}, u32[]{:S(2)}, u32[]{:S(2)}) %all-to-all-start.2) | async-done | bytes 1769504 | tf_op jit(solution)/shard_map/all_to_all | solution.py:353
  55.9 4.3 %all-to-all-start = ((bf16[8,864,128]{2,1,0:T(8,128)(2,1)}), bf16[8,864,128]{2,1,0:T(8,128)(2,1)}, u32[]{:S(2)}, u32[]{:S(2)}) async-start(bf16[8,864,128]{2,1,0:T(8,128)(2,1)} %copy-done.4), calls=%async_computation | async-start | bytes 3538944 | tf_op jit(solution)/shard_map/all_to_all | solution.py:353
  60.2 3.5 %gram0.1 = (bf16[512,1792]{1,0:T(8,128)(2,1)S(1)}, f32[256,512]{1,0:T(8,128)S(1)}, bf16[256,512]{1,0:T(8,128)(2,1)}) custom-call(s32[1]{0:T(128)} %bitcast.core_ref, bf16[8,864,128]{2,1,0:T(8,128)(2,1)} %all-to-all-done.2.in_ref), custom_call_target="tpu_custom_call" | custom-call | flops 939524096 | bytes 3670016 | tf_op jit(solution)/shard_map/gram0/pallas_call | solution.py:114
  65.7 1.9 collective-permute-done.8.got_ref
  69.7 1.9 collective-permute-start.10
  73.2 4.8 %collective-permute-done.10.refs_1_ = bf16[64,512]{1,0:T(8,128)(2,1)S(1)} collective-permute-done((bf16[64,512]{1,0:T(8,128)(2,1)S(1)}, bf16[64,512]{1,0:T(8,128)(2,1)S(1)}, u32[]{:S(2)}, u32[]{:S(2)}) %collective-permute-start.10) | collective-permute-done | bytes 65568 | tf_op jit(solution)/shard_map/ppermute | solution.py:338
  78.0 1.6 collective-permute-start.12
  79.6 2.5 %collective-permute-start.13 = (bf16[64,512]{1,0:T(8,128)(2,1)S(1)}, bf16[64,512]{1,0:T(8,128)(2,1)S(1)}, u32[]{:S(2)}, u32[]{:S(2)}) collective-permute-start(bf16[64,512]{1,0:T(8,128)(2,1)S(1)} %add0.1.refs_0_), channel_id=1, source_target_pairs={{0,4},{1,5},{2,6},{3,7},{4,0},{5,1},{6,2},{7,3},{8,12},{9,13},{10,... | collective-permute-start | bytes 196616 | tf_op jit(solution)/shard_map/ppermute | solution.py:338
  82.4 6.6 %collective-permute-done.13.refs_2_ = bf16[64,512]{1,0:T(8,128)(2,1)S(1)} collective-permute-done((bf16[64,512]{1,0:T(8,128)(2,1)S(1)}, bf16[64,512]{1,0:T(8,128)(2,1)S(1)}, u32[]{:S(2)}, u32[]{:S(2)}) %collective-permute-start.13) | collective-permute-done | bytes 65568 | tf_op jit(solution)/shard_map/ppermute | solution.py:338
  89.0 1.5 collective-permute-done.15.got_ref
  90.6 15.9 %newton0.1.factor_ref = bf16[512,512]{1,0:T(8,128)(2,1)S(1)} custom-call(s32[1]{0:T(128)} %bitcast.core_ref, bf16[256,512]{1,0:T(8,128)(2,1)S(1)} %join0.1.own_ref, bf16[256,512]{1,0:T(8,128)(2,1)S(1)} %collective-permute-done.15.got_ref), custom_call_target="tpu_custom_call" | custom-call | flops 13690208256 | bytes 1572864 | tf_op jit(solution)/shard_map/newton0/pallas_call | solution.py:252
  108.9 12.6 %all-to-all-start.3 = ((bf16[8,864,128]{2,1,0:T(8,128)(2,1)}), bf16[8,864,128]{2,1,0:T(8,128)(2,1)}, u32[]{:S(2)}, u32[]{:S(2)}) async-start(bf16[8,864,128]{2,1,0:T(8,128)(2,1)} %copy-done.2), calls=%async_computation.3 | async-start | bytes 3538944 | tf_op jit(solution)/shard_map/all_to_all | solution.py:353
  121.5 2.8 %gram1.1 = (bf16[512,1792]{1,0:T(8,128)(2,1)S(1)}, f32[256,512]{1,0:T(8,128)S(1)}, bf16[256,512]{1,0:T(8,128)(2,1)S(1)}) custom-call(s32[1]{0:T(128)} %bitcast.core_ref, bf16[8,864,128]{2,1,0:T(8,128)(2,1)} %all-to-all-done.in_ref), custom_call_target="tpu_custom_call" | custom-call | flops 939524096 | bytes 3670016 | tf_op jit(solution)/shard_map/gram1/pallas_call | solution.py:114
  124.3 1.5 collective-permute-done.got_ref
  125.9 1.5 collective-permute-start.1
  127.5 2.0 collective-permute-start.2
  130.3 9.6 %collective-permute-done.2.refs_1_ = bf16[64,512]{1,0:T(8,128)(2,1)S(1)} collective-permute-done((bf16[64,512]{1,0:T(8,128)(2,1)S(1)}, bf16[64,512]{1,0:T(8,128)(2,1)S(1)}, u32[]{:S(2)}, u32[]{:S(2)}) %collective-permute-start.2) | collective-permute-done | bytes 65568 | tf_op jit(solution)/shard_map/ppermute | solution.py:338
  139.9 1.5 collective-permute-start.4
  141.4 2.5 %collective-permute-start.5 = (bf16[64,512]{1,0:T(8,128)(2,1)S(1)}, bf16[64,512]{1,0:T(8,128)(2,1)S(1)}, u32[]{:S(2)}, u32[]{:S(2)}) collective-permute-start(bf16[64,512]{1,0:T(8,128)(2,1)S(1)} %add1.1.refs_0_), channel_id=1, source_target_pairs={{0,4},{1,5},{2,6},{3,7},{4,0},{5,1},{6,2},{7,3},{8,12},{9,13},{10,... | collective-permute-start | bytes 196616 | tf_op jit(solution)/shard_map/ppermute | solution.py:338
  144.2 8.0 %collective-permute-done.5.refs_2_ = bf16[64,512]{1,0:T(8,128)(2,1)S(1)} collective-permute-done((bf16[64,512]{1,0:T(8,128)(2,1)S(1)}, bf16[64,512]{1,0:T(8,128)(2,1)S(1)}, u32[]{:S(2)}, u32[]{:S(2)}) %collective-permute-start.5) | collective-permute-done | bytes 65568 | tf_op jit(solution)/shard_map/ppermute | solution.py:338
  152.3 1.5 collective-permute-done.7.got_ref
  153.9 15.8 %newton1.1.factor_ref = bf16[512,512]{1,0:T(8,128)(2,1)S(1)} custom-call(s32[1]{0:T(128)} %bitcast.core_ref, bf16[256,512]{1,0:T(8,128)(2,1)S(1)} %join1.1.own_ref, bf16[256,512]{1,0:T(8,128)(2,1)S(1)} %collective-permute-done.7.got_ref), custom_call_target="tpu_custom_call" | custom-call | flops 13690208256 | bytes 1572864 | tf_op jit(solution)/shard_map/newton1/pallas_call | solution.py:252
  170.9 1.2 copy-done.3
  172.2 4.3 %all-to-all-start.1 = ((bf16[8,864,128]{2,1,0:T(8,128)(2,1)}), bf16[8,864,128]{2,1,0:T(8,128)(2,1)}, u32[]{:S(2)}, u32[]{:S(2)}) async-start(bf16[8,864,128]{2,1,0:T(8,128)(2,1)} %copy-done.3), calls=%async_computation.1 | async-start | bytes 3538944 | tf_op jit(solution)/shard_map/all_to_all | solution.py:353
  176.5 4.8 %add_convert_fusion = bf16[8,64,3456]{2,1,0:T(8,128)(2,1)} fusion(bf16[8,64,3456]{2,1,0:T(8,128)(2,1)S(1)} %copy-done.1, bf16[8,64,3456]{2,1,0:T(8,128)(2,1)} %mom_ref.3), kind=kLoop, calls=%fused_computation | loop fusion | flops 8847360 | bytes 10616832 | tf_op jit(solution)/shard_map/convert_element_type | solution.py:367
  181.3 4.9 %finish0.1.refs_2_ = f32[8,64,3456]{2,1,0:T(8,128)} custom-call(bf16[8,864,128]{2,1,0:T(8,128)(2,1)} %all-to-all-done.3.refs_0_, f32[8,64,3456]{2,1,0:T(8,128)} %refs_1_.3), custom_call_target="tpu_custom_call" | custom-call | flops 2654208 | bytes 8847360 | tf_op jit(solution)/shard_map/finish0/pallas_call | solution.py:320
  186.2 32.1 %all-to-all-done.1.refs_0_ = bf16[8,864,128]{2,1,0:T(8,128)(2,1)} async-done(((bf16[8,864,128]{2,1,0:T(8,128)(2,1)}), bf16[8,864,128]{2,1,0:T(8,128)(2,1)}, u32[]{:S(2)}, u32[]{:S(2)}) %all-to-all-start.1) | async-done | bytes 1769504 | tf_op jit(solution)/shard_map/all_to_all | solution.py:353
  218.3 4.9 %finish1.1 = f32[8,64,3456]{2,1,0:T(8,128)} custom-call(bf16[8,864,128]{2,1,0:T(8,128)(2,1)} %all-to-all-done.1.refs_0_, f32[8,64,3456]{2,1,0:T(8,128)} %refs_1_.3, f32[8,64,3456]{2,1,0:T(8,128)} %finish0.1.refs_2_), custom_call_target="tpu_custom_call", output_to_operand_aliasing={{}: (2, {})} | custom-call | flops 2654208 | bytes 8847360 | tf_op jit(solution)/shard_map/finish1/pallas_call | solution.py:320
  (45 shorter events, 13.5 us)
Async XLA Ops:
  0.6 2.0 copy-start
  5.8 1.2 copy-start.5
  7.0 7.6 %copy-start.1 = (bf16[8,64,3456]{2,1,0:T(8,128)(2,1)S(1)}, bf16[8,64,3456]{2,1,0:T(8,128)(2,1)}, u32[]{:S(2)}) copy-start(bf16[8,64,3456]{2,1,0:T(8,128)(2,1)} %grad_ref.3) | copy-start | bytes 10616836
  7.0 48.9 %all-to-all-start.2 = ((bf16[8,864,128]{2,1,0:T(8,128)(2,1)}), bf16[8,864,128]{2,1,0:T(8,128)(2,1)}, u32[]{:S(2)}, u32[]{:S(2)}) async-start(bf16[8,864,128]{2,1,0:T(8,128)(2,1)} %copy-done.5), calls=%async_computation.2 | async-start | bytes 3538944 | tf_op jit(solution)/shard_map/all_to_all | solution.py:353
  17.7 1.2 copy-start.4
  55.9 53.0 %all-to-all-start = ((bf16[8,864,128]{2,1,0:T(8,128)(2,1)}), bf16[8,864,128]{2,1,0:T(8,128)(2,1)}, u32[]{:S(2)}, u32[]{:S(2)}) async-start(bf16[8,864,128]{2,1,0:T(8,128)(2,1)} %copy-done.4), calls=%async_computation | async-start | bytes 3538944 | tf_op jit(solution)/shard_map/all_to_all | solution.py:353
  63.7 1.2 copy-start.6
  64.9 0.8 copy-start.8
  65.7 1.9 collective-permute-start.8
  67.6 1.0 copy-start.9
  69.7 8.3 %collective-permute-start.10 = (bf16[64,512]{1,0:T(8,128)(2,1)S(1)}, bf16[64,512]{1,0:T(8,128)(2,1)S(1)}, u32[]{:S(2)}, u32[]{:S(2)}) collective-permute-start(bf16[64,512]{1,0:T(8,128)(2,1)S(1)} %get-tuple-element.27), channel_id=1, source_target_pairs={{0,4},{1,5},{2,6},{3,7},{4,0},{5,1},{6,2},{7,3},{8,12},{9,13},{10,... | collective-permute-start | bytes 196616 | tf_op jit(solution)/shard_map/ppermute | solution.py:338
  71.6 6.4 %collective-permute-start.11 = (bf16[64,512]{1,0:T(8,128)(2,1)S(1)}, bf16[64,512]{1,0:T(8,128)(2,1)S(1)}, u32[]{:S(2)}, u32[]{:S(2)}) collective-permute-start(bf16[64,512]{1,0:T(8,128)(2,1)S(1)} %get-tuple-element.28), channel_id=1, source_target_pairs={{0,6},{1,7},{2,4},{3,5},{4,2},{5,3},{6,0},{7,1},{8,14},{9,15},{10,... | collective-permute-start | bytes 196616 | tf_op jit(solution)/shard_map/ppermute | solution.py:338
  72.7 5.3 %collective-permute-start.9 = (bf16[64,512]{1,0:T(8,128)(2,1)S(1)}, bf16[64,512]{1,0:T(8,128)(2,1)S(1)}, u32[]{:S(2)}, u32[]{:S(2)}) collective-permute-start(bf16[64,512]{1,0:T(8,128)(2,1)S(1)} %get-tuple-element.26), channel_id=1, source_target_pairs={{0,2},{1,3},{2,0},{3,1},{4,6},{5,7},{6,4},{7,5},{8,10},{9,11},{10,... | collective-permute-start | bytes 196616 | tf_op jit(solution)/shard_map/ppermute | solution.py:338
  78.0 4.3 %collective-permute-start.12 = (bf16[64,512]{1,0:T(8,128)(2,1)S(1)}, bf16[64,512]{1,0:T(8,128)(2,1)S(1)}, u32[]{:S(2)}, u32[]{:S(2)}) collective-permute-start(bf16[64,512]{1,0:T(8,128)(2,1)S(1)} %add0.1.refs_0_), channel_id=1, source_target_pairs={{0,2},{1,3},{2,0},{3,1},{4,6},{5,7},{6,4},{7,5},{8,10},{9,11},{10,... | collective-permute-start | bytes 196616 | tf_op jit(solution)/shard_map/ppermute | solution.py:338
  79.6 9.3 %collective-permute-start.13 = (bf16[64,512]{1,0:T(8,128)(2,1)S(1)}, bf16[64,512]{1,0:T(8,128)(2,1)S(1)}, u32[]{:S(2)}, u32[]{:S(2)}) collective-permute-start(bf16[64,512]{1,0:T(8,128)(2,1)S(1)} %add0.1.refs_0_), channel_id=1, source_target_pairs={{0,4},{1,5},{2,6},{3,7},{4,0},{5,1},{6,2},{7,3},{8,12},{9,13},{10,... | collective-permute-start | bytes 196616 | tf_op jit(solution)/shard_map/ppermute | solution.py:338
  82.1 6.8 %collective-permute-start.14 = (bf16[64,512]{1,0:T(8,128)(2,1)S(1)}, bf16[64,512]{1,0:T(8,128)(2,1)S(1)}, u32[]{:S(2)}, u32[]{:S(2)}) collective-permute-start(bf16[64,512]{1,0:T(8,128)(2,1)S(1)} %add0.1.refs_0_), channel_id=1, source_target_pairs={{0,6},{1,7},{2,4},{3,5},{4,2},{5,3},{6,0},{7,1},{8,14},{9,15},{10,... | collective-permute-start | bytes 196616 | tf_op jit(solution)/shard_map/ppermute | solution.py:338
  89.0 17.5 %copy-start.7 = (bf16[512,1792]{1,0:T(8,128)(2,1)S(1)}, bf16[512,1792]{1,0:T(8,128)(2,1)}, u32[]{:S(2)}) copy-start(bf16[512,1792]{1,0:T(8,128)(2,1)} %copy-done.6) | copy-start | bytes 5505028
  89.0 1.6 collective-permute-start.15
  107.6 1.2 copy-start.2
  108.9 63.3 %all-to-all-start.3 = ((bf16[8,864,128]{2,1,0:T(8,128)(2,1)}), bf16[8,864,128]{2,1,0:T(8,128)(2,1)}, u32[]{:S(2)}, u32[]{:S(2)}) async-start(bf16[8,864,128]{2,1,0:T(8,128)(2,1)} %copy-done.2), calls=%async_computation.3 | async-start | bytes 3538944 | tf_op jit(solution)/shard_map/all_to_all | solution.py:353
  124.2 1.6 collective-permute-start
  125.9 4.3 %collective-permute-start.1 = (bf16[64,512]{1,0:T(8,128)(2,1)S(1)}, bf16[64,512]{1,0:T(8,128)(2,1)S(1)}, u32[]{:S(2)}, u32[]{:S(2)}) collective-permute-start(bf16[64,512]{1,0:T(8,128)(2,1)S(1)} %get-tuple-element.19), channel_id=1, source_target_pairs={{0,2},{1,3},{2,0},{3,1},{4,6},{5,7},{6,4},{7,5},{8,10},{9,11},{10,... | collective-permute-start | bytes 196616 | tf_op jit(solution)/shard_map/ppermute | solution.py:338
  127.5 12.4 %collective-permute-start.2 = (bf16[64,512]{1,0:T(8,128)(2,1)S(1)}, bf16[64,512]{1,0:T(8,128)(2,1)S(1)}, u32[]{:S(2)}, u32[]{:S(2)}) collective-permute-start(bf16[64,512]{1,0:T(8,128)(2,1)S(1)} %get-tuple-element.20), channel_id=1, source_target_pairs={{0,4},{1,5},{2,6},{3,7},{4,0},{5,1},{6,2},{7,3},{8,12},{9,13},{10,... | collective-permute-start | bytes 196616 | tf_op jit(solution)/shard_map/ppermute | solution.py:338
  129.5 10.3 %collective-permute-start.3 = (bf16[64,512]{1,0:T(8,128)(2,1)S(1)}, bf16[64,512]{1,0:T(8,128)(2,1)S(1)}, u32[]{:S(2)}, u32[]{:S(2)}) collective-permute-start(bf16[64,512]{1,0:T(8,128)(2,1)S(1)} %get-tuple-element.21), channel_id=1, source_target_pairs={{0,6},{1,7},{2,4},{3,5},{4,2},{5,3},{6,0},{7,1},{8,14},{9,15},{10,... | collective-permute-start | bytes 196616 | tf_op jit(solution)/shard_map/ppermute | solution.py:338
  139.9 4.3 %collective-permute-start.4 = (bf16[64,512]{1,0:T(8,128)(2,1)S(1)}, bf16[64,512]{1,0:T(8,128)(2,1)S(1)}, u32[]{:S(2)}, u32[]{:S(2)}) collective-permute-start(bf16[64,512]{1,0:T(8,128)(2,1)S(1)} %add1.1.refs_0_), channel_id=1, source_target_pairs={{0,2},{1,3},{2,0},{3,1},{4,6},{5,7},{6,4},{7,5},{8,10},{9,11},{10,... | collective-permute-start | bytes 196616 | tf_op jit(solution)/shard_map/ppermute | solution.py:338
  141.4 10.8 %collective-permute-start.5 = (bf16[64,512]{1,0:T(8,128)(2,1)S(1)}, bf16[64,512]{1,0:T(8,128)(2,1)S(1)}, u32[]{:S(2)}, u32[]{:S(2)}) collective-permute-start(bf16[64,512]{1,0:T(8,128)(2,1)S(1)} %add1.1.refs_0_), channel_id=1, source_target_pairs={{0,4},{1,5},{2,6},{3,7},{4,0},{5,1},{6,2},{7,3},{8,12},{9,13},{10,... | collective-permute-start | bytes 196616 | tf_op jit(solution)/shard_map/ppermute | solution.py:338
  143.9 8.3 %collective-permute-start.6 = (bf16[64,512]{1,0:T(8,128)(2,1)S(1)}, bf16[64,512]{1,0:T(8,128)(2,1)S(1)}, u32[]{:S(2)}, u32[]{:S(2)}) collective-permute-start(bf16[64,512]{1,0:T(8,128)(2,1)S(1)} %add1.1.refs_0_), channel_id=1, source_target_pairs={{0,6},{1,7},{2,4},{3,5},{4,2},{5,3},{6,0},{7,1},{8,14},{9,15},{10,... | collective-permute-start | bytes 196616 | tf_op jit(solution)/shard_map/ppermute | solution.py:338
  152.3 1.6 collective-permute-start.7
  170.9 1.2 copy-start.3
  172.2 46.1 %all-to-all-start.1 = ((bf16[8,864,128]{2,1,0:T(8,128)(2,1)}), bf16[8,864,128]{2,1,0:T(8,128)(2,1)}, u32[]{:S(2)}, u32[]{:S(2)}) async-start(bf16[8,864,128]{2,1,0:T(8,128)(2,1)} %copy-done.3), calls=%async_computation.1 | async-start | bytes 3538944 | tf_op jit(solution)/shard_map/all_to_all | solution.py:353

commit v2 on v0

v2 whole, which is shorter than its diff:
```python
import functools
import math

import jax
import jax.numpy as jnp
from jax import lax
from jax.experimental import pallas as pl
from jax.experimental.pallas import tpu as pltpu
from jax.sharding import PartitionSpec as P


ITERS = 5
GROUPS = 2
SHARE = 2
LANE = 128

BETA = 0.95
EPSILON = 1e-06
COEF_A = 3.4445
COEF_B = -4.775
COEF_C = 2.0315

F32 = jnp.float32
BF16 = jnp.bfloat16
AXES = ("out", "inp")


def sending(count):
    return list(reversed(range(count)))


def source_of(gradient, momentum):
    grads = gradient.astype(F32)
    moment = BETA * momentum.astype(F32) + grads
    return (grads + BETA * moment).astype(BF16)


def params(mib=20):
    return pltpu.CompilerParams(vmem_limit_bytes=mib * 1024 * 1024)


def cost(flops, size):
    return pl.CostEstimate(flops=int(flops), bytes_accessed=int(size), transcendentals=0)


def vmem():
    return pl.BlockSpec(memory_space=pltpu.VMEM)


def smem():
    return pl.BlockSpec(memory_space=pltpu.SMEM)


def lanes_at(tile):
    return pl.ds(pl.multiple_of(tile * LANE, LANE), LANE)


def source_body(kernel_ref, side_ref, grad_ref, mom_ref, *refs, rows, tiles):
    *out_refs, source_ref = refs
    source_ref[...] = source_of(grad_ref[0], mom_ref[0])
    half = rows // 2
    middle = LANE // 2
    last = source_ref[:, tiles * LANE : (tiles + 1) * LANE]
    for flip, out_ref in enumerate(out_refs):
        side = side_ref[0] ^ flip
        for t in range(tiles):
            out_ref[t * rows : (t + 1) * rows, :] = source_ref[:, lanes_at(side * (tiles + 1) + t)]
        left = jnp.concatenate([last[:half, :middle], last[half:, :middle]], axis=1)
        right = jnp.concatenate([last[:half, middle:], last[half:, middle:]], axis=1)
        out_ref[tiles * rows :, :] = jnp.where(side == 0, left, right)


def source_call(kernel, side, gradient, momentum, tiles, mib):
    rows, width = gradient.shape[1:]
    packed = tiles * rows + rows // 2
    block = pl.BlockSpec((1, rows, width), lambda i, kernel, side: (kernel[0], 0, 0))
    return pl.pallas_call(
        functools.partial(source_body, rows=rows, tiles=tiles),
        grid_spec=pltpu.PrefetchScalarGridSpec(
            num_scalar_prefetch=2,
            grid=(1,),
            in_specs=[block, block],
            out_specs=[pl.BlockSpec((packed, LANE), lambda i, kernel, side: (0, 0)) for _ in range(SHARE)],
            scratch_shapes=[pltpu.VMEM((rows, width), BF16)],
        ),
        out_shape=[jax.ShapeDtypeStruct((packed, LANE), BF16) for _ in range(SHARE)],
        compiler_params=params(mib=mib),
        cost_estimate=cost(rows * width * 6, rows * width * 6),
    )(kernel, side, gradient, momentum)


def unpack(side_ref, in_refs, x_ref, rows, tiles):
    half = rows // 2
    zeros = jnp.zeros((half, LANE // 2), BF16)
    columns = slice(tiles * LANE, (tiles + 1) * LANE)
    for s, in_ref in enumerate(in_refs):
        base = pl.multiple_of((s // SHARE * SHARE + (side_ref[0] ^ (s % SHARE))) * rows, rows)
        for t in range(tiles):
            x_ref[pl.ds(base, rows), t * LANE : (t + 1) * LANE] = in_ref[t * rows : (t + 1) * rows, :]
        last = in_ref[tiles * rows : tiles * rows + half, :]
        x_ref[pl.ds(base, half), columns] = jnp.concatenate([last[:, : LANE // 2], zeros], axis=1)
        x_ref[pl.ds(base + half, half), columns] = jnp.concatenate([last[:, LANE // 2 :], zeros], axis=1)


def gram_body(core_ref, side_ref, *refs, rows, tiles):
    *in_refs, keep_ref, send_ref, x_ref, gram_ref = refs
    unpack(side_ref, in_refs, x_ref, rows, tiles)
    x = x_ref[...]
    gram_ref[...] = lax.dot_general(x, x, (((1,), (1,)), ((), ())), preferred_element_type=F32)
    size = gram_ref.shape[0] // 2
    core = core_ref[0]
    keep_ref[...] = gram_ref[pl.ds(pl.multiple_of(core * size, size), size), :]
    send_ref[...] = gram_ref[pl.ds(pl.multiple_of((1 - core) * size, size), size), :].astype(BF16)


def gram_call(core, side, received, rows, tiles):
    size = len(received) * rows
    columns = (tiles + 1) * LANE
    return pl.pallas_call(
        functools.partial(gram_body, rows=rows, tiles=tiles),
        in_specs=[smem(), smem()] + [vmem() for _ in received],
        out_specs=[vmem(), vmem()],
        out_shape=[
            jax.ShapeDtypeStruct((size // 2, size), F32),
            jax.ShapeDtypeStruct((size // 2, size), BF16),
        ],
        scratch_shapes=[pltpu.VMEM((size, columns), BF16), pltpu.VMEM((size, size), F32)],
        compiler_params=params(),
        cost_estimate=cost(2 * size * size * columns, 4 * size * columns),
    )(core, side, *received)


def split_body(chip_ref, keep_ref, got_ref, own_ref, *rest, piece):
    *send_refs, total_ref = rest
    total_ref[...] = keep_ref[...] + got_ref[...].astype(F32)
    chip = chip_ref[0]

    def rows_of(m):
        return total_ref[pl.ds(pl.multiple_of((chip ^ m) * piece, piece), piece), :]

    own_ref[...] = rows_of(0)
    for m, ref in enumerate(send_refs):
        ref[...] = rows_of(m + 1).astype(BF16)


def split_call(chip, keep, got, chips):
    half, size = keep.shape
    piece = half // chips
    return pl.pallas_call(
        functools.partial(split_body, piece=piece),
        in_specs=[smem(), vmem(), vmem()],
        out_specs=[vmem() for _ in range(chips)],
        out_shape=[jax.ShapeDtypeStruct((piece, size), F32 if m == 0 else BF16) for m in range(chips)],
        scratch_shapes=[pltpu.VMEM((half, size), F32)],
        compiler_params=params(),
        cost_estimate=cost(half * size * 4, half * size * 8),
    )(chip, keep, got)


def add_body(own_ref, *refs):
    *got_refs, out_ref = refs
    total = own_ref[...]
    for ref in got_refs:
        total = total + ref[...].astype(F32)
    out_ref[...] = total.astype(BF16)


def add_call(own, got):
    return pl.pallas_call(
        add_body,
        in_specs=[vmem() for _ in range(1 + len(got))],
        out_specs=vmem(),
        out_shape=jax.ShapeDtypeStruct(own.shape, BF16),
        compiler_params=params(),
        cost_estimate=cost(own.size * 4, own.size * 8),
    )(own, *got)


def join_body(chip_ref, *refs):
    *in_refs, out_ref = refs
    piece = in_refs[0].shape[0]
    for m, ref in enumerate(in_refs):
        out_ref[pl.ds(pl.multiple_of((chip_ref[0] ^ m) * piece, piece), piece), :] = ref[...]


def join_call(chip, pieces):
    piece, size = pieces[0].shape
    return pl.pallas_call(
        join_body,
        in_specs=[smem()] + [vmem() for _ in pieces],
        out_specs=vmem(),
        out_shape=jax.ShapeDtypeStruct((piece * len(pieces), size), BF16),
        compiler_params=params(),
        cost_estimate=cost(piece * len(pieces) * size, 4 * piece * len(pieces) * size),
    )(chip, *pieces)


def newton_body(core_ref, own_ref, got_ref, out_ref, r_ref, q_ref, y_ref, r2_ref, p2_ref, q2_ref, y2_ref, beside):
    half, size = own_ref.shape
    core = core_ref[0]
    r_ref[pl.ds(pl.multiple_of(core * half, half), half), :] = own_ref[...].astype(F32)
    r_ref[pl.ds(pl.multiple_of((1 - core) * half, half), half), :] = got_ref[...].astype(F32)
    row = lax.broadcasted_iota(jnp.int32, (size, size), 0)
    column = lax.broadcasted_iota(jnp.int32, (size, size), 1)
    eye = row == column
    gram = r_ref[...]
    scale2 = jnp.sum(jnp.where(eye, gram, 0.0)) + EPSILON
    r_ref[...] = gram / scale2

    def halves(ref, value):
        high = value.astype(BF16)
        ref[0] = high
        ref[1] = (value - high.astype(F32)).astype(BF16)

    def mult(left, right, terms):
        first, *rest = [jnp.dot(left[i], right[j], preferred_element_type=F32) for i, j in terms]
        return functools.reduce(jnp.add, rest, first)

    fine = ((0, 0), (0, 1), (1, 0))

    def poly(exact):
        halves(r2_ref, r_ref[...])
        value = COEF_B * r_ref[...] + COEF_C * mult(r2_ref, r2_ref, fine if exact else fine[:1])
        if exact:
            halves(p2_ref, value)
        else:
            p2_ref[0] = value.astype(BF16)

    def transform(exact):
        halves(q2_ref, q_ref[...])
        return COEF_A * q_ref[...] + mult(p2_ref, q2_ref, fine if exact else fine[:2])

    def advance(exact):
        halfway = COEF_A * r_ref[...] + mult(p2_ref, r2_ref, fine if exact else fine[:2])
        halves(y2_ref, halfway)
        y_ref[...] = halfway
        r_ref[...] = COEF_A * y_ref[...] + mult(y2_ref, p2_ref, fine if exact else fine[::2])

    poly(False)
    q_ref[...] = jnp.where(eye, COEF_A, 0.0) + p2_ref[0].astype(F32)
    advance(False)

    def sweep(exact):
        poly(exact)
        q_ref[...] = transform(exact)
        advance(exact)

    sweep(False)

    def loop(_, carry):
        sweep(True)
        return carry

    lax.fori_loop(2, ITERS - 1, loop, 0)
    beside()
    poly(True)
    out_ref[...] = (transform(True) / jnp.sqrt(scale2)).astype(BF16)


def update_body(core_ref, side_ref, own_ref, got_ref, *refs, rows, tiles, scale, blocks):
    any_refs, out_refs = refs[:blocks], refs[blocks : 2 * blocks]
    factor_ref, in_ref, x_ref, part_ref, sem, *newton_refs = refs[2 * blocks :]
    copies = [pltpu.make_async_copy(ref, in_ref.at[s], sem.at[s]) for s, ref in enumerate(any_refs)]
    for copy in copies:
        copy.start()

    def beside():
        for copy in copies:
            copy.wait()
        unpack(side_ref, [in_ref.at[s] for s in range(blocks)], x_ref, rows, tiles)

    newton_body(core_ref, own_ref, got_ref, factor_ref, *newton_refs, beside)
    half = rows // 2
    middle = LANE // 2
    step = 2
    for t in range(0, tiles + 1, step):
        part = jnp.dot(factor_ref[...], x_ref[:, t * LANE : (t + step) * LANE], preferred_element_type=F32)
        part_ref[...] = (scale * part).astype(BF16)
        for s, out_ref in enumerate(out_refs):
            base = pl.multiple_of((s // SHARE * SHARE + (side_ref[0] ^ (s % SHARE))) * rows, rows)
            for u in range(t, min(t + step, tiles + 1)):
                block = part_ref[pl.ds(base, rows), (u - t) * LANE : (u - t + 1) * LANE]
                if u == tiles:
                    block = jnp.concatenate([block[:half, :middle], block[half:, :middle]], axis=1)
                out_ref[u * rows : u * rows + block.shape[0], :] = block


def update_call(core, side, own, got, received, rows, tiles, scale):
    size = own.shape[1]
    blocks = len(received)
    packed = tiles * rows + rows // 2
    columns = (tiles + 1) * LANE
    newton = [pltpu.VMEM((size, size), F32)] * 3 + [pltpu.VMEM((2, size, size), BF16)] * 4
    return pl.pallas_call(
        functools.partial(update_body, rows=rows, tiles=tiles, scale=scale, blocks=blocks),
        in_specs=[smem(), smem(), vmem(), vmem()] + [pl.BlockSpec(memory_space=pl.ANY) for _ in received],
        out_specs=[vmem() for _ in range(blocks)],
        out_shape=[jax.ShapeDtypeStruct((packed, LANE), BF16) for _ in range(blocks)],
        scratch_shapes=[
            pltpu.VMEM((size, size), BF16),
            pltpu.VMEM((blocks, packed, LANE), BF16),
            pltpu.VMEM((size, columns), BF16),
            pltpu.VMEM((size, 2 * LANE), BF16),
            pltpu.SemaphoreType.DMA((blocks,)),
        ]
        + newton,
        compiler_params=params(mib=28),
        cost_estimate=cost(2 * size * size * columns + 6 * 17 * size**3, 4 * size * columns),
    )(core, side, own, got, *received)


def finish_body(kernel_ref, side_ref, first_ref, second_ref, weight_ref, *refs, rows, tiles):
    out_ref = refs[-1]
    middle = LANE // 2
    side = side_ref[0]

    def put(where, update):
        out_ref[0, :, where] = 0.9 * weight_ref[0, :, where] - 0.5 * update.astype(F32)

    for flip, ref in enumerate((first_ref, second_ref)):
        for t in range(tiles):
            put(lanes_at((side ^ flip) * (tiles + 1) + t), ref[t * rows : (t + 1) * rows, :])
    one, two = first_ref[tiles * rows :, :], second_ref[tiles * rows :, :]
    left = jnp.where(side == 0, one, two)
    right = jnp.where(side == 0, two, one)
    upper = jnp.concatenate([left[:, :middle], right[:, :middle]], axis=1)
    lower = jnp.concatenate([left[:, middle:], right[:, middle:]], axis=1)
    put(slice(tiles * LANE, (tiles + 1) * LANE), jnp.concatenate([upper, lower], axis=0))


def finish_call(kernel, side, first, second, weight, base, tiles):
    rows, width = weight.shape[1:]
    packed = tiles * rows + rows // 2
    block = pl.BlockSpec((1, rows, width), lambda i, kernel, side: (kernel[0], 0, 0))
    half = pl.BlockSpec((packed, LANE), lambda i, kernel, side: (0, 0))
    more = [] if base is None else [base]
    return pl.pallas_call(
        functools.partial(finish_body, rows=rows, tiles=tiles),
        grid_spec=pltpu.PrefetchScalarGridSpec(
            num_scalar_prefetch=2,
            grid=(1,),
            in_specs=[half, half, block] + [pl.BlockSpec(memory_space=pl.ANY) for _ in more],
            out_specs=block,
        ),
        out_shape=jax.ShapeDtypeStruct(weight.shape, F32),
        input_output_aliases={5: 0} if more else {},
        compiler_params=params(),
        cost_estimate=cost(rows * width * 3, rows * width * 10),
    )(kernel, side, first, second, weight, *more)


def exchange(value, bits, count):
    return lax.ppermute(value, AXES, [(i, i ^ bits) for i in range(count)])


def pipelined(weight, gradient, momentum, n, inner):
    kernels, rows, width = weight.shape
    per_group = kernels // GROUPS
    tiles = width // LANE // SHARE
    scale = 0.2 * math.sqrt(width * inner)
    devices = n * inner
    chips = SHARE * inner // 2
    index = lax.axis_index(AXES)

    def scalar(value):
        return value.astype(jnp.int32).reshape(1)

    core = scalar(index % 2)
    chip = scalar(index // 2 % chips)
    outer = lax.axis_index("out")
    side = scalar(outer % SHARE)

    def kernel_of(group, far):
        return scalar(group * per_group + ((outer // SHARE) ^ far))

    def regroup(value, s):
        if s == 0:
            return value
        return lax.ppermute(value, "out", [(o, o ^ s) for o in range(n)])

    def factor_of(received):
        keep, send = gram_call(core, side, received, rows, tiles)
        own, *send = split_call(chip, keep, exchange(send, 1, devices), chips)
        got = [exchange(value, 2 * (m + 1), devices) for m, value in enumerate(send)]
        piece = add_call(own, got)
        pieces = [piece] + [exchange(piece, 2 * m, devices) for m in range(1, chips)]
        half = join_call(chip, pieces)
        got = exchange(half, 1, devices)
        return update_call(core, side, half, got, received, rows, tiles, scale)

    order = sending(per_group)
    received = []
    for g in range(GROUPS):
        blocks = {}
        for far in order:
            pair = source_call(kernel_of(g, far), side, gradient, momentum, tiles, 62)
            for flip, value in enumerate(pair):
                s = far * SHARE + flip
                blocks[s] = regroup(value, s)
        received.append([blocks[s] for s in range(n)])
    moment = (BETA * momentum.astype(F32) + gradient.astype(F32)).astype(BF16)
    updates = [factor_of(value) for value in received]
    returned = [[regroup(block, s) for s, block in enumerate(value)] for value in updates]
    result = None
    for g, value in enumerate(returned):
        for far in reversed(order):
            first, second = value[far * SHARE], value[far * SHARE + 1]
            result = finish_call(kernel_of(g, far), side, first, second, weight, result, tiles)
    return (result, moment)


def mult(former, latter):
    return jnp.einsum("kij,kjl->kil", former, latter, precision=lax.Precision.HIGHEST)


def whole_kernels(weight, gradient, momentum, n, inner):
    moment = BETA * momentum.astype(F32) + gradient.astype(F32)
    source = source_of(gradient, momentum)
    kernels, rows, columns = source.shape
    held = kernels // n
    width = rows * n
    regrouped = lax.all_to_all(source, "out", split_axis=0, concat_axis=1, tiled=True)
    partial_value = jnp.einsum("kic,kjc->kij", regrouped, regrouped, preferred_element_type=F32)
    gram = lax.psum(partial_value.astype(BF16), "inp").astype(F32)
    scale2 = jnp.trace(gram, axis1=1, axis2=2) + EPSILON
    current = gram / scale2[:, None, None]
    transform = jnp.broadcast_to(jnp.eye(width, dtype=F32), (held, width, width))
    for _ in range(ITERS):
        poly_part = COEF_B * current + COEF_C * mult(current, current)
        transform = COEF_A * transform + mult(poly_part, transform)
        halfway = COEF_A * current + mult(poly_part, current)
        current = COEF_A * halfway + mult(halfway, poly_part)
    factor = (transform / jnp.sqrt(scale2)[:, None, None]).astype(BF16)
    orthogonal = jnp.einsum("kij,kjc->kic", factor, regrouped, preferred_element_type=F32)
    update = (0.2 * math.sqrt(columns * inner) * orthogonal).astype(BF16)
    returned = lax.all_to_all(update, "out", split_axis=1, concat_axis=0, tiled=True)
    weight_next = 0.9 * weight - 0.5 * returned.astype(F32)
    return (weight_next, moment.astype(BF16))


def solution(mesh):
    n, inner = mesh.shape["out"], mesh.shape["inp"]

    def on_device(weight, gradient, momentum):
        kernels, rows, width = weight.shape
        chips = SHARE * inner // 2
        fits = (
            kernels % GROUPS == 0
            and n * GROUPS == kernels * SHARE
            and n & (n - 1) == 0
            and width % (SHARE * LANE) == LANE
            and rows % 32 == 0
            and inner >= 2
            and inner & (inner - 1) == 0
            and n * rows % (2 * chips * 16) == 0
        )
        if not fits:
            return whole_kernels(weight, gradient, momentum, n, inner)
        return pipelined(weight, gradient, momentum, n, inner)

    return jax.shard_map(
        on_device,
        mesh=mesh,
        in_specs=(P(None, "out", "inp"), P(None, "out", "inp"), P(None, "out", "inp")),
        out_specs=(P(None, "out", "inp"), P(None, "out", "inp")),
        check_vma=False,
    )
```

time: 339 us -> 223 us (0.66)
  the two profiles are of different devices: /device:TPU:0 before, /device:TPU:16 now
where the time goes in v2:
time: 223 us
  waiting for transfers between devices  98.1 us (44%)
  Pallas kernels  66 us (30%)
  starting transfers between devices  53.8 us (24%)
  other arithmetic  2.89 us (1%)
    ppermute x28, waiting for transfers between devices, regroup(): return lax.ppermute(value, 'out', [(o, o ^ s) for o in range(n)])  82.7 us
    ppermute x28, starting transfers between devices, regroup(): return lax.ppermute(value, 'out', [(o, o ^ s) for o in range(n)])  39.3 us
    pallas_call x2, Pallas kernels, update_call(): pl.pallas_call(functools.partial(update_body, rows=rows, tiles=tiles, sca...  33.3 us
    pallas_call x8, Pallas kernels, source_call(): pl.pallas_call(functools.partial(source_body, rows=rows, tiles=tiles), gr...  18.8 us
    ppermute x16, waiting for transfers between devices, exchange(): return lax.ppermute(value, AXES, [(i, i ^ bits) for i in range(count)])  15.4 us
    ppermute x16, starting transfers between devices, exchange(): return lax.ppermute(value, AXES, [(i, i ^ bits) for i in range(count)])  14.5 us
    pallas_call x8, Pallas kernels, finish_call(): pl.pallas_call(functools.partial(finish_body, rows=rows, tiles=tiles), gr...  8.38 us
    pallas_call x2, Pallas kernels, gram_call(): pl.pallas_call(functools.partial(gram_body, rows=rows, tiles=tiles), in_s...  5.19 us
  transfers between devices with their start and end apart: 44, of which 23 were waited for; matrix products, arithmetic and copies ran while one was open for 1% of the time, Pallas kernels for 28%

profile of v2, /device:TPU:16, one launch (start us, length us, event | category | flops | bytes accessed | tf_op | source)
XLA Modules:
  0.0 222.7 jit_solution(12063244919926070325)
XLA Ops:
  6.0 2.4 %shard_map.61 = (bf16[864,128]{1,0:T(8,128)(2,1)}, bf16[864,128]{1,0:T(8,128)(2,1)}) custom-call(s32[1]{0:T(128)} %bitcast.10.kernel_ref, s32[1]{0:T(128)} %bitcast.1.side_ref, bf16[8,64,3456]{2,1,0:T(8,128)(2,1)} %grad_ref.15, bf16[8,64,3456]{2,1,0:T(8,128)(2,1)} %mom_ref.15), custom_call_target="tpu_custom_call" | custom-call | flops 1327104 | bytes 1327104 | tf_op jit(solution)/shard_map/pallas_call | solution.py:77
  8.7 2.5 %collective-permute-start.26 = (bf16[864,128]{1,0:T(8,128)(2,1)}, bf16[864,128]{1,0:T(8,128)(2,1)S(1)}, u32[]{:S(2)}, u32[]{:S(2)}) collective-permute-start(bf16[864,128]{1,0:T(8,128)(2,1)} %get-tuple-element.73), channel_id=1, source_target_pairs={{0,20},{4,16},{8,28},{12,24},{16,4},{20,0},{24,12},{28,8},{1,21},{... | collective-permute-start | bytes 663560 | tf_op jit(solution)/shard_map/ppermute | solution.py:379
  11.2 2.3 %shard_map.62 = (bf16[864,128]{1,0:T(8,128)(2,1)}, bf16[864,128]{1,0:T(8,128)(2,1)}) custom-call(s32[1]{0:T(128)} %bitcast.7.kernel_ref, s32[1]{0:T(128)} %bitcast.1.side_ref, bf16[8,64,3456]{2,1,0:T(8,128)(2,1)} %grad_ref.15, bf16[8,64,3456]{2,1,0:T(8,128)(2,1)} %mom_ref.15), custom_call_target="tpu_custom_call" | custom-call | flops 1327104 | bytes 1327104 | tf_op jit(solution)/shard_map/pallas_call | solution.py:77
  14.0 2.4 %shard_map.59 = (bf16[864,128]{1,0:T(8,128)(2,1)}, bf16[864,128]{1,0:T(8,128)(2,1)}) custom-call(s32[1]{0:T(128)} %bitcast.8.kernel_ref, s32[1]{0:T(128)} %bitcast.1.side_ref, bf16[8,64,3456]{2,1,0:T(8,128)(2,1)} %grad_ref.15, bf16[8,64,3456]{2,1,0:T(8,128)(2,1)} %mom_ref.15), custom_call_target="tpu_custom_call" | custom-call | flops 1327104 | bytes 1327104 | tf_op jit(solution)/shard_map/pallas_call | solution.py:77
  16.4 2.3 %shard_map.51 = (bf16[864,128]{1,0:T(8,128)(2,1)}, bf16[864,128]{1,0:T(8,128)(2,1)}) custom-call(s32[1]{0:T(128)} %bitcast.5.kernel_ref, s32[1]{0:T(128)} %bitcast.1.side_ref, bf16[8,64,3456]{2,1,0:T(8,128)(2,1)} %grad_ref.15, bf16[8,64,3456]{2,1,0:T(8,128)(2,1)} %mom_ref.15), custom_call_target="tpu_custom_call" | custom-call | flops 1327104 | bytes 1327104 | tf_op jit(solution)/shard_map/pallas_call | solution.py:77
  18.7 2.5 %collective-permute-start.28 = (bf16[864,128]{1,0:T(8,128)(2,1)}, bf16[864,128]{1,0:T(8,128)(2,1)}, u32[]{:S(2)}, u32[]{:S(2)}) collective-permute-start(bf16[864,128]{1,0:T(8,128)(2,1)} %get-tuple-element.75), channel_id=1, source_target_pairs={{0,28},{4,24},{8,20},{12,16},{16,12},{20,8},{24,4},{28,0},{1,29},{... | collective-permute-start | bytes 663560 | tf_op jit(solution)/shard_map/ppermute | solution.py:379
  21.7 11.0 %collective-permute-done.25.refs_4_ = bf16[864,128]{1,0:T(8,128)(2,1)S(1)} collective-permute-done((bf16[864,128]{1,0:T(8,128)(2,1)}, bf16[864,128]{1,0:T(8,128)(2,1)S(1)}, u32[]{:S(2)}, u32[]{:S(2)}) %collective-permute-start.25) | collective-permute-done | bytes 221216 | tf_op jit(solution)/shard_map/ppermute | solution.py:379
  32.7 5.7 %collective-permute-start.1 = (bf16[864,128]{1,0:T(8,128)(2,1)}, bf16[864,128]{1,0:T(8,128)(2,1)S(1)}, u32[]{:S(2)}, u32[]{:S(2)}) collective-permute-start(bf16[864,128]{1,0:T(8,128)(2,1)} %get-tuple-element.48), channel_id=1, source_target_pairs={{0,8},{4,12},{8,0},{12,4},{16,24},{20,28},{24,16},{28,20},{1,9},{5... | collective-permute-start | bytes 663560 | tf_op jit(solution)/shard_map/ppermute | solution.py:379
  38.6 5.4 %collective-permute-start.2 = (bf16[864,128]{1,0:T(8,128)(2,1)}, bf16[864,128]{1,0:T(8,128)(2,1)S(1)}, u32[]{:S(2)}, u32[]{:S(2)}) collective-permute-start(bf16[864,128]{1,0:T(8,128)(2,1)} %get-tuple-element.49), channel_id=1, source_target_pairs={{0,12},{4,8},{8,4},{12,0},{16,28},{20,24},{24,20},{28,16},{1,13},{... | collective-permute-start | bytes 663560 | tf_op jit(solution)/shard_map/ppermute | solution.py:379
  44.0 2.4 %shard_map.52 = (bf16[864,128]{1,0:T(8,128)(2,1)}, bf16[864,128]{1,0:T(8,128)(2,1)}) custom-call(s32[1]{0:T(128)} %bitcast.6.kernel_ref, s32[1]{0:T(128)} %bitcast.1.side_ref, bf16[8,64,3456]{2,1,0:T(8,128)(2,1)} %grad_ref.15, bf16[8,64,3456]{2,1,0:T(8,128)(2,1)} %mom_ref.15), custom_call_target="tpu_custom_call" | custom-call | flops 1327104 | bytes 1327104 | tf_op jit(solution)/shard_map/pallas_call | solution.py:77
  46.3 2.4 %shard_map.53 = (bf16[864,128]{1,0:T(8,128)(2,1)}, bf16[864,128]{1,0:T(8,128)(2,1)}) custom-call(s32[1]{0:T(128)} %bitcast.kernel_ref, s32[1]{0:T(128)} %bitcast.1.side_ref, bf16[8,64,3456]{2,1,0:T(8,128)(2,1)} %grad_ref.15, bf16[8,64,3456]{2,1,0:T(8,128)(2,1)} %mom_ref.15), custom_call_target="tpu_custom_call" | custom-call | flops 1327104 | bytes 1327104 | tf_op jit(solution)/shard_map/pallas_call | solution.py:77
  51.1 12.0 %collective-permute-done.28.refs_7_ = bf16[864,128]{1,0:T(8,128)(2,1)} collective-permute-done((bf16[864,128]{1,0:T(8,128)(2,1)}, bf16[864,128]{1,0:T(8,128)(2,1)}, u32[]{:S(2)}, u32[]{:S(2)}) %collective-permute-start.28) | collective-permute-done | bytes 221216 | tf_op jit(solution)/shard_map/ppermute | solution.py:379
  63.1 2.9 %collective-permute-start.6 = (bf16[864,128]{1,0:T(8,128)(2,1)}, bf16[864,128]{1,0:T(8,128)(2,1)}, u32[]{:S(2)}, u32[]{:S(2)}) collective-permute-start(bf16[864,128]{1,0:T(8,128)(2,1)} %get-tuple-element.53), channel_id=1, source_target_pairs={{0,28},{4,24},{8,20},{12,16},{16,12},{20,8},{24,4},{28,0},{1,29},{... | collective-permute-start | bytes 663560 | tf_op jit(solution)/shard_map/ppermute | solution.py:379
  66.6 2.6 %shard_map.63 = (f32[256,512]{1,0:T(8,128)S(1)}, bf16[256,512]{1,0:T(8,128)(2,1)S(1)}) custom-call(s32[1]{0:T(128)} %bitcast.2.core_ref, s32[1]{0:T(128)} %bitcast.1.side_ref, bf16[864,128]{1,0:T(8,128)(2,1)S(1)} %copy-done, bf16[864,128]{1,0:T(8,128)(2,1)} %collective-permute-done.22.refs_1_, bf16[864,128]{1,0:T(8,128)(2,1)S(1)} %collective-permute-done.23.refs_2_, ...), custom_call_target="tpu_custom_call" | custom-call | flops 939524096 | bytes 3670016 | tf_op jit(solution)/shard_map/pallas_call | solution.py:119
  69.3 7.4 %collective-permute-done.4.refs_5_ = bf16[864,128]{1,0:T(8,128)(2,1)S(1)} collective-permute-done((bf16[864,128]{1,0:T(8,128)(2,1)}, bf16[864,128]{1,0:T(8,128)(2,1)S(1)}, u32[]{:S(2)}, u32[]{:S(2)}) %collective-permute-start.4) | collective-permute-done | bytes 221216 | tf_op jit(solution)/shard_map/ppermute | solution.py:379
  76.7 7.7 %collective-permute-done.5.refs_6_ = bf16[864,128]{1,0:T(8,128)(2,1)S(1)} collective-permute-done((bf16[864,128]{1,0:T(8,128)(2,1)}, bf16[864,128]{1,0:T(8,128)(2,1)S(1)}, u32[]{:S(2)}, u32[]{:S(2)}) %collective-permute-start.5) | collective-permute-done | bytes 221216 | tf_op jit(solution)/shard_map/ppermute | solution.py:379
  84.3 3.2 %collective-permute-done.6.refs_7_ = bf16[864,128]{1,0:T(8,128)(2,1)} collective-permute-done((bf16[864,128]{1,0:T(8,128)(2,1)}, bf16[864,128]{1,0:T(8,128)(2,1)}, u32[]{:S(2)}, u32[]{:S(2)}) %collective-permute-start.6) | collective-permute-done | bytes 221216 | tf_op jit(solution)/shard_map/ppermute | solution.py:379
  88.4 2.6 %shard_map.54 = (f32[256,512]{1,0:T(8,128)S(1)}, bf16[256,512]{1,0:T(8,128)(2,1)S(1)}) custom-call(s32[1]{0:T(128)} %bitcast.2.core_ref, s32[1]{0:T(128)} %bitcast.1.side_ref, bf16[864,128]{1,0:T(8,128)(2,1)S(1)} %copy-done.1, bf16[864,128]{1,0:T(8,128)(2,1)} %collective-permute-done.refs_1_, bf16[864,128]{1,0:T(8,128)(2,1)S(1)} %collective-permute-done.1.refs_2_, ...), custom_call_target="tpu_custom_call" | custom-call | flops 939524096 | bytes 3670016 | tf_op jit(solution)/shard_map/pallas_call | solution.py:119
  97.1 2.4 %collective-permute-done.32.refs_2_ = bf16[64,512]{1,0:T(8,128)(2,1)S(1)} collective-permute-done((bf16[64,512]{1,0:T(8,128)(2,1)S(1)}, bf16[64,512]{1,0:T(8,128)(2,1)S(1)}, u32[]{:S(2)}, u32[]{:S(2)}) %collective-permute-start.32) | collective-permute-done | bytes 65568 | tf_op jit(solution)/shard_map/ppermute | solution.py:353
  100.6 2.4 %collective-permute-start.35 = (bf16[64,512]{1,0:T(8,128)(2,1)S(1)}, bf16[64,512]{1,0:T(8,128)(2,1)S(1)}, u32[]{:S(2)}, u32[]{:S(2)}) collective-permute-start(bf16[64,512]{1,0:T(8,128)(2,1)S(1)} %shard_map.65.refs_0_), channel_id=1, source_target_pairs={{0,6},{1,7},{2,4},{3,5},{4,2},{5,3},{6,0},{7,1},{8,14},{9,15},{10,... | collective-permute-start | bytes 196616 | tf_op jit(solution)/shard_map/ppermute | solution.py:353
  106.0 2.5 %collective-permute-start.10 = (bf16[64,512]{1,0:T(8,128)(2,1)S(1)}, bf16[64,512]{1,0:T(8,128)(2,1)S(1)}, u32[]{:S(2)}, u32[]{:S(2)}) collective-permute-start(bf16[64,512]{1,0:T(8,128)(2,1)S(1)} %get-tuple-element.59), channel_id=1, source_target_pairs={{0,6},{1,7},{2,4},{3,5},{4,2},{5,3},{6,0},{7,1},{8,14},{9,15},{10,... | collective-permute-start | bytes 196616 | tf_op jit(solution)/shard_map/ppermute | solution.py:353
  121.2 16.7 %shard_map.67 = (bf16[864,128]{1,0:T(8,128)(2,1)S(1)}, bf16[864,128]{1,0:T(8,128)(2,1)S(1)}, bf16[864,128]{1,0:T(8,128)(2,1)S(1)}, bf16[864,128]{1,0:T(8,128)(2,...) custom-call(s32[1]{0:T(128)} %bitcast.2.core_ref, ...), custom_call_target="tpu_custom_call" | custom-call | flops 14629732352 | bytes 3670016 | tf_op jit(solution)/shard_map/pallas_call | solution.py:294
  138.9 2.5 %collective-permute-start.42 = (bf16[864,128]{1,0:T(8,128)(2,1)S(1)}, bf16[864,128]{1,0:T(8,128)(2,1)S(1)}, u32[]{:S(2)}, u32[]{:S(2)}) collective-permute-start(bf16[864,128]{1,0:T(8,128)(2,1)S(1)} %get-tuple-element.87), channel_id=1, source_target_pairs={{0,12},{4,8},{8,4},{12,0},{16,28},{20,24},{24,20},{28,16},{1,13},{... | collective-permute-start | bytes 663560 | tf_op jit(solution)/shard_map/ppermute | solution.py:379
  141.5 3.4 %collective-permute-start.40 = (bf16[864,128]{1,0:T(8,128)(2,1)S(1)}, bf16[864,128]{1,0:T(8,128)(2,1)S(1)}, u32[]{:S(2)}, u32[]{:S(2)}) collective-permute-start(bf16[864,128]{1,0:T(8,128)(2,1)S(1)} %get-tuple-element.85), channel_id=1, source_target_pairs={{0,20},{4,16},{8,28},{12,24},{16,4},{20,0},{24,12},{28,8},{1,21},{... | collective-permute-start | bytes 663560 | tf_op jit(solution)/shard_map/ppermute | solution.py:379
  144.9 16.7 %shard_map.58 = (bf16[864,128]{1,0:T(8,128)(2,1)S(1)}, bf16[864,128]{1,0:T(8,128)(2,1)S(1)}, bf16[864,128]{1,0:T(8,128)(2,1)S(1)}, bf16[864,128]{1,0:T(8,128)(2,...) custom-call(s32[1]{0:T(128)} %bitcast.2.core_ref, ...), custom_call_target="tpu_custom_call" | custom-call | flops 14629732352 | bytes 3670016 | tf_op jit(solution)/shard_map/pallas_call | solution.py:294
  161.6 2.5 %collective-permute-start.38 = (bf16[864,128]{1,0:T(8,128)(2,1)S(1)}, bf16[864,128]{1,0:T(8,128)(2,1)S(1)}, u32[]{:S(2)}, u32[]{:S(2)}) collective-permute-start(bf16[864,128]{1,0:T(8,128)(2,1)S(1)} %get-tuple-element.83), channel_id=1, source_target_pairs={{0,28},{4,24},{8,20},{12,16},{16,12},{20,8},{24,4},{28,0},{1,29},{... | collective-permute-start | bytes 663560 | tf_op jit(solution)/shard_map/ppermute | solution.py:379
  167.6 10.4 %collective-permute-done.37.first_ref = bf16[864,128]{1,0:T(8,128)(2,1)S(1)} collective-permute-done((bf16[864,128]{1,0:T(8,128)(2,1)S(1)}, bf16[864,128]{1,0:T(8,128)(2,1)S(1)}, u32[]{:S(2)}, u32[]{:S(2)}) %collective-permute-start.37) | collective-permute-done | bytes 221216 | tf_op jit(solution)/shard_map/ppermute | solution.py:379
  178.0 18.3 %collective-permute-done.38.second_ref = bf16[864,128]{1,0:T(8,128)(2,1)S(1)} collective-permute-done((bf16[864,128]{1,0:T(8,128)(2,1)S(1)}, bf16[864,128]{1,0:T(8,128)(2,1)S(1)}, u32[]{:S(2)}, u32[]{:S(2)}) %collective-permute-start.38) | collective-permute-done | bytes 221216 | tf_op jit(solution)/shard_map/ppermute | solution.py:379
  198.8 2.9 %add_convert_fusion = bf16[8,64,3456]{2,1,0:T(8,128)(2,1)} fusion(bf16[8,64,3456]{2,1,0:T(8,128)(2,1)S(1)} %copy-done.3, bf16[8,64,3456]{2,1,0:T(8,128)(2,1)S(1)} %copy-done.4), kind=kLoop, calls=%fused_computation | loop fusion | flops 8847360 | bytes 10616832 | tf_op jit(solution)/shard_map/convert_element_type | solution.py:401
  208.0 2.3 %collective-permute-done.18.second_ref = bf16[864,128]{1,0:T(8,128)(2,1)S(1)} collective-permute-done((bf16[864,128]{1,0:T(8,128)(2,1)S(1)}, bf16[864,128]{1,0:T(8,128)(2,1)S(1)}, u32[]{:S(2)}, u32[]{:S(2)}) %collective-permute-start.18) | collective-permute-done | bytes 221216 | tf_op jit(solution)/shard_map/ppermute | solution.py:379
  211.4 5.8 %collective-permute-done.15.first_ref = bf16[864,128]{1,0:T(8,128)(2,1)S(1)} collective-permute-done((bf16[864,128]{1,0:T(8,128)(2,1)S(1)}, bf16[864,128]{1,0:T(8,128)(2,1)S(1)}, u32[]{:S(2)}, u32[]{:S(2)}) %collective-permute-start.15) | collective-permute-done | bytes 221216 | tf_op jit(solution)/shard_map/ppermute | solution.py:379
  217.2 4.5 %collective-permute-done.16.second_ref = bf16[864,128]{1,0:T(8,128)(2,1)S(1)} collective-permute-done((bf16[864,128]{1,0:T(8,128)(2,1)S(1)}, bf16[864,128]{1,0:T(8,128)(2,1)S(1)}, u32[]{:S(2)}, u32[]{:S(2)}) %collective-permute-start.16) | collective-permute-done | bytes 221216 | tf_op jit(solution)/shard_map/ppermute | solution.py:379
  (98 shorter events, 48.9 us)
Async XLA Ops:
  3.0 15.7 %collective-permute-start.23 = (bf16[864,128]{1,0:T(8,128)(2,1)}, bf16[864,128]{1,0:T(8,128)(2,1)S(1)}, u32[]{:S(2)}, u32[]{:S(2)}) collective-permute-start(bf16[864,128]{1,0:T(8,128)(2,1)} %get-tuple-element.70), channel_id=1, source_target_pairs={{0,8},{4,12},{8,0},{12,4},{16,24},{20,28},{24,16},{28,20},{1,9},{5... | collective-permute-start | bytes 663560 | tf_op jit(solution)/shard_map/ppermute | solution.py:379
  4.6 16.7 %collective-permute-start.24 = (bf16[864,128]{1,0:T(8,128)(2,1)}, bf16[864,128]{1,0:T(8,128)(2,1)S(1)}, u32[]{:S(2)}, u32[]{:S(2)}) collective-permute-start(bf16[864,128]{1,0:T(8,128)(2,1)} %get-tuple-element.71), channel_id=1, source_target_pairs={{0,12},{4,8},{8,4},{12,0},{16,28},{20,24},{24,20},{28,16},{1,13},{... | collective-permute-start | bytes 663560 | tf_op jit(solution)/shard_map/ppermute | solution.py:379
  8.3 24.4 %collective-permute-start.25 = (bf16[864,128]{1,0:T(8,128)(2,1)}, bf16[864,128]{1,0:T(8,128)(2,1)S(1)}, u32[]{:S(2)}, u32[]{:S(2)}) collective-permute-start(bf16[864,128]{1,0:T(8,128)(2,1)} %get-tuple-element.72), channel_id=1, source_target_pairs={{0,16},{4,20},{8,24},{12,28},{16,0},{20,4},{24,8},{28,12},{1,17},{... | collective-permute-start | bytes 663560 | tf_op jit(solution)/shard_map/ppermute | solution.py:379
  8.7 29.9 %collective-permute-start.26 = (bf16[864,128]{1,0:T(8,128)(2,1)}, bf16[864,128]{1,0:T(8,128)(2,1)S(1)}, u32[]{:S(2)}, u32[]{:S(2)}) collective-permute-start(bf16[864,128]{1,0:T(8,128)(2,1)} %get-tuple-element.73), channel_id=1, source_target_pairs={{0,20},{4,16},{8,28},{12,24},{16,4},{20,0},{24,12},{28,8},{1,21},{... | collective-permute-start | bytes 663560 | tf_op jit(solution)/shard_map/ppermute | solution.py:379
  13.6 32.8 %collective-permute-start.27 = (bf16[864,128]{1,0:T(8,128)(2,1)}, bf16[864,128]{1,0:T(8,128)(2,1)S(1)}, u32[]{:S(2)}, u32[]{:S(2)}) collective-permute-start(bf16[864,128]{1,0:T(8,128)(2,1)} %get-tuple-element.74), channel_id=1, source_target_pairs={{0,24},{4,28},{8,16},{12,20},{16,8},{20,12},{24,0},{28,4},{1,25},{... | collective-permute-start | bytes 663560 | tf_op jit(solution)/shard_map/ppermute | solution.py:379
  18.7 44.4 %collective-permute-start.28 = (bf16[864,128]{1,0:T(8,128)(2,1)}, bf16[864,128]{1,0:T(8,128)(2,1)}, u32[]{:S(2)}, u32[]{:S(2)}) collective-permute-start(bf16[864,128]{1,0:T(8,128)(2,1)} %get-tuple-element.75), channel_id=1, source_target_pairs={{0,28},{4,24},{8,20},{12,16},{16,12},{20,8},{24,4},{28,0},{1,29},{... | collective-permute-start | bytes 663560 | tf_op jit(solution)/shard_map/ppermute | solution.py:379
  21.2 41.8 %collective-permute-start.22 = (bf16[864,128]{1,0:T(8,128)(2,1)}, bf16[864,128]{1,0:T(8,128)(2,1)}, u32[]{:S(2)}, u32[]{:S(2)}) collective-permute-start(bf16[864,128]{1,0:T(8,128)(2,1)} %get-tuple-element.69), channel_id=1, source_target_pairs={{0,4},{4,0},{8,12},{12,8},{16,20},{20,16},{24,28},{28,24},{1,5},{5... | collective-permute-start | bytes 663560 | tf_op jit(solution)/shard_map/ppermute | solution.py:379
  32.7 30.4 %collective-permute-start.1 = (bf16[864,128]{1,0:T(8,128)(2,1)}, bf16[864,128]{1,0:T(8,128)(2,1)S(1)}, u32[]{:S(2)}, u32[]{:S(2)}) collective-permute-start(bf16[864,128]{1,0:T(8,128)(2,1)} %get-tuple-element.48), channel_id=1, source_target_pairs={{0,8},{4,12},{8,0},{12,4},{16,24},{20,28},{24,16},{28,20},{1,9},{5... | collective-permute-start | bytes 663560 | tf_op jit(solution)/shard_map/ppermute | solution.py:379
  38.6 27.5 %collective-permute-start.2 = (bf16[864,128]{1,0:T(8,128)(2,1)}, bf16[864,128]{1,0:T(8,128)(2,1)S(1)}, u32[]{:S(2)}, u32[]{:S(2)}) collective-permute-start(bf16[864,128]{1,0:T(8,128)(2,1)} %get-tuple-element.49), channel_id=1, source_target_pairs={{0,12},{4,8},{8,4},{12,0},{16,28},{20,24},{24,20},{28,16},{1,13},{... | collective-permute-start | bytes 663560 | tf_op jit(solution)/shard_map/ppermute | solution.py:379
  46.3 22.9 %collective-permute-start.3 = (bf16[864,128]{1,0:T(8,128)(2,1)}, bf16[864,128]{1,0:T(8,128)(2,1)S(1)}, u32[]{:S(2)}, u32[]{:S(2)}) collective-permute-start(bf16[864,128]{1,0:T(8,128)(2,1)} %get-tuple-element.50), channel_id=1, source_target_pairs={{0,16},{4,20},{8,24},{12,28},{16,0},{20,4},{24,8},{28,12},{1,17},{... | collective-permute-start | bytes 663560 | tf_op jit(solution)/shard_map/ppermute | solution.py:379
  63.1 13.6 %collective-permute-start.4 = (bf16[864,128]{1,0:T(8,128)(2,1)}, bf16[864,128]{1,0:T(8,128)(2,1)S(1)}, u32[]{:S(2)}, u32[]{:S(2)}) collective-permute-start(bf16[864,128]{1,0:T(8,128)(2,1)} %get-tuple-element.51), channel_id=1, source_target_pairs={{0,20},{4,16},{8,28},{12,24},{16,4},{20,0},{24,12},{28,8},{1,21},{... | collective-permute-start | bytes 663560 | tf_op jit(solution)/shard_map/ppermute | solution.py:379
  63.1 21.3 %collective-permute-start.5 = (bf16[864,128]{1,0:T(8,128)(2,1)}, bf16[864,128]{1,0:T(8,128)(2,1)S(1)}, u32[]{:S(2)}, u32[]{:S(2)}) collective-permute-start(bf16[864,128]{1,0:T(8,128)(2,1)} %get-tuple-element.52), channel_id=1, source_target_pairs={{0,24},{4,28},{8,16},{12,20},{16,8},{20,12},{24,0},{28,4},{1,25},{... | collective-permute-start | bytes 663560 | tf_op jit(solution)/shard_map/ppermute | solution.py:379
  63.1 24.4 %collective-permute-start.6 = (bf16[864,128]{1,0:T(8,128)(2,1)}, bf16[864,128]{1,0:T(8,128)(2,1)}, u32[]{:S(2)}, u32[]{:S(2)}) collective-permute-start(bf16[864,128]{1,0:T(8,128)(2,1)} %get-tuple-element.53), channel_id=1, source_target_pairs={{0,28},{4,24},{8,20},{12,16},{16,12},{20,8},{24,4},{28,0},{1,29},{... | collective-permute-start | bytes 663560 | tf_op jit(solution)/shard_map/ppermute | solution.py:379
  66.1 21.4 %collective-permute-start = (bf16[864,128]{1,0:T(8,128)(2,1)}, bf16[864,128]{1,0:T(8,128)(2,1)}, u32[]{:S(2)}, u32[]{:S(2)}) collective-permute-start(bf16[864,128]{1,0:T(8,128)(2,1)} %get-tuple-element.47), channel_id=1, source_target_pairs={{0,4},{4,0},{8,12},{12,8},{16,20},{20,16},{24,28},{28,24},{1,5},{5... | collective-permute-start | bytes 663560 | tf_op jit(solution)/shard_map/ppermute | solution.py:379
  69.2 21.9 %collective-permute-start.29 = (bf16[256,512]{1,0:T(8,128)(2,1)S(1)}, bf16[256,512]{1,0:T(8,128)(2,1)S(1)}, u32[]{:S(2)}, u32[]{:S(2)}) collective-permute-start(bf16[256,512]{1,0:T(8,128)(2,1)S(1)} %get-tuple-element.77), channel_id=1, source_target_pairs={{0,1},{1,0},{2,3},{3,2},{4,5},{5,4},{6,7},{7,6},{8,9},{9,8},{10,11... | collective-permute-start | bytes 786440 | tf_op jit(solution)/shard_map/ppermute | solution.py:353
  91.0 14.8 %collective-permute-start.7 = (bf16[256,512]{1,0:T(8,128)(2,1)S(1)}, bf16[256,512]{1,0:T(8,128)(2,1)S(1)}, u32[]{:S(2)}, u32[]{:S(2)}) collective-permute-start(bf16[256,512]{1,0:T(8,128)(2,1)S(1)} %get-tuple-element.55), channel_id=1, source_target_pairs={{0,1},{1,0},{2,3},{3,2},{4,5},{5,4},{6,7},{7,6},{8,9},{9,8},{10,11... | collective-permute-start | bytes 786440 | tf_op jit(solution)/shard_map/ppermute | solution.py:353
  105.8 15.4 %collective-permute-start.36 = (bf16[256,512]{1,0:T(8,128)(2,1)S(1)}, bf16[256,512]{1,0:T(8,128)(2,1)S(1)}, u32[]{:S(2)}, u32[]{:S(2)}) collective-permute-start(bf16[256,512]{1,0:T(8,128)(2,1)S(1)} %shard_map.66.own_ref), channel_id=1, source_target_pairs={{0,1},{1,0},{2,3},{3,2},{4,5},{5,4},{6,7},{7,6},{8,9},{9,8},{10,11... | collective-permute-start | bytes 786440 | tf_op jit(solution)/shard_map/ppermute | solution.py:353
  121.1 20.3 %collective-permute-start.14 = (bf16[256,512]{1,0:T(8,128)(2,1)S(1)}, bf16[256,512]{1,0:T(8,128)(2,1)S(1)}, u32[]{:S(2)}, u32[]{:S(2)}) collective-permute-start(bf16[256,512]{1,0:T(8,128)(2,1)S(1)} %shard_map.57.own_ref), channel_id=1, source_target_pairs={{0,1},{1,0},{2,3},{3,2},{4,5},{5,4},{6,7},{7,6},{8,9},{9,8},{10,11... | collective-permute-start | bytes 786440 | tf_op jit(solution)/shard_map/ppermute | solution.py:353
  137.9 23.7 %collective-permute-start.43 = (bf16[864,128]{1,0:T(8,128)(2,1)S(1)}, bf16[864,128]{1,0:T(8,128)(2,1)S(1)}, u32[]{:S(2)}, u32[]{:S(2)}) collective-permute-start(bf16[864,128]{1,0:T(8,128)(2,1)S(1)} %get-tuple-element.89), channel_id=1, source_target_pairs={{0,4},{4,0},{8,12},{12,8},{16,20},{20,16},{24,28},{28,24},{1,5},{5... | collective-permute-start | bytes 663560 | tf_op jit(solution)/shard_map/ppermute | solution.py:379
  138.9 22.7 %collective-permute-start.41 = (bf16[864,128]{1,0:T(8,128)(2,1)S(1)}, bf16[864,128]{1,0:T(8,128)(2,1)S(1)}, u32[]{:S(2)}, u32[]{:S(2)}) collective-permute-start(bf16[864,128]{1,0:T(8,128)(2,1)S(1)} %get-tuple-element.86), channel_id=1, source_target_pairs={{0,8},{4,12},{8,0},{12,4},{16,24},{20,28},{24,16},{28,20},{1,9},{5... | collective-permute-start | bytes 663560 | tf_op jit(solution)/shard_map/ppermute | solution.py:379
  138.9 25.2 %collective-permute-start.42 = (bf16[864,128]{1,0:T(8,128)(2,1)S(1)}, bf16[864,128]{1,0:T(8,128)(2,1)S(1)}, u32[]{:S(2)}, u32[]{:S(2)}) collective-permute-start(bf16[864,128]{1,0:T(8,128)(2,1)S(1)} %get-tuple-element.87), channel_id=1, source_target_pairs={{0,12},{4,8},{8,4},{12,0},{16,28},{20,24},{24,20},{28,16},{1,13},{... | collective-permute-start | bytes 663560 | tf_op jit(solution)/shard_map/ppermute | solution.py:379
  141.4 23.7 %collective-permute-start.39 = (bf16[864,128]{1,0:T(8,128)(2,1)S(1)}, bf16[864,128]{1,0:T(8,128)(2,1)S(1)}, u32[]{:S(2)}, u32[]{:S(2)}) collective-permute-start(bf16[864,128]{1,0:T(8,128)(2,1)S(1)} %get-tuple-element.84), channel_id=1, source_target_pairs={{0,16},{4,20},{8,24},{12,28},{16,0},{20,4},{24,8},{28,12},{1,17},{... | collective-permute-start | bytes 663560 | tf_op jit(solution)/shard_map/ppermute | solution.py:379
  141.5 25.4 %collective-permute-start.40 = (bf16[864,128]{1,0:T(8,128)(2,1)S(1)}, bf16[864,128]{1,0:T(8,128)(2,1)S(1)}, u32[]{:S(2)}, u32[]{:S(2)}) collective-permute-start(bf16[864,128]{1,0:T(8,128)(2,1)S(1)} %get-tuple-element.85), channel_id=1, source_target_pairs={{0,20},{4,16},{8,28},{12,24},{16,4},{20,0},{24,12},{28,8},{1,21},{... | collective-permute-start | bytes 663560 | tf_op jit(solution)/shard_map/ppermute | solution.py:379
  161.5 16.5 %collective-permute-start.37 = (bf16[864,128]{1,0:T(8,128)(2,1)S(1)}, bf16[864,128]{1,0:T(8,128)(2,1)S(1)}, u32[]{:S(2)}, u32[]{:S(2)}) collective-permute-start(bf16[864,128]{1,0:T(8,128)(2,1)S(1)} %get-tuple-element.82), channel_id=1, source_target_pairs={{0,24},{4,28},{8,16},{12,20},{16,8},{20,12},{24,0},{28,4},{1,25},{... | collective-permute-start | bytes 663560 | tf_op jit(solution)/shard_map/ppermute | solution.py:379
  161.6 34.7 %collective-permute-start.38 = (bf16[864,128]{1,0:T(8,128)(2,1)S(1)}, bf16[864,128]{1,0:T(8,128)(2,1)S(1)}, u32[]{:S(2)}, u32[]{:S(2)}) collective-permute-start(bf16[864,128]{1,0:T(8,128)(2,1)S(1)} %get-tuple-element.83), channel_id=1, source_target_pairs={{0,28},{4,24},{8,20},{12,16},{16,12},{20,8},{24,4},{28,0},{1,29},{... | collective-permute-start | bytes 663560 | tf_op jit(solution)/shard_map/ppermute | solution.py:379
  164.1 32.2 %collective-permute-start.21 = (bf16[864,128]{1,0:T(8,128)(2,1)S(1)}, bf16[864,128]{1,0:T(8,128)(2,1)S(1)}, u32[]{:S(2)}, u32[]{:S(2)}) collective-permute-start(bf16[864,128]{1,0:T(8,128)(2,1)S(1)} %get-tuple-element.67), channel_id=1, source_target_pairs={{0,4},{4,0},{8,12},{12,8},{16,20},{20,16},{24,28},{28,24},{1,5},{5... | collective-permute-start | bytes 663560 | tf_op jit(solution)/shard_map/ppermute | solution.py:379
  165.1 31.6 %collective-permute-start.19 = (bf16[864,128]{1,0:T(8,128)(2,1)S(1)}, bf16[864,128]{1,0:T(8,128)(2,1)S(1)}, u32[]{:S(2)}, u32[]{:S(2)}) collective-permute-start(bf16[864,128]{1,0:T(8,128)(2,1)S(1)} %get-tuple-element.64), channel_id=1, source_target_pairs={{0,8},{4,12},{8,0},{12,4},{16,24},{20,28},{24,16},{28,20},{1,9},{5... | collective-permute-start | bytes 663560 | tf_op jit(solution)/shard_map/ppermute | solution.py:379
  166.9 40.0 %collective-permute-start.20 = (bf16[864,128]{1,0:T(8,128)(2,1)S(1)}, bf16[864,128]{1,0:T(8,128)(2,1)S(1)}, u32[]{:S(2)}, u32[]{:S(2)}) collective-permute-start(bf16[864,128]{1,0:T(8,128)(2,1)S(1)} %get-tuple-element.65), channel_id=1, source_target_pairs={{0,12},{4,8},{8,4},{12,0},{16,28},{20,24},{24,20},{28,16},{1,13},{... | collective-permute-start | bytes 663560 | tf_op jit(solution)/shard_map/ppermute | solution.py:379
  178.0 30.0 %collective-permute-start.17 = (bf16[864,128]{1,0:T(8,128)(2,1)S(1)}, bf16[864,128]{1,0:T(8,128)(2,1)S(1)}, u32[]{:S(2)}, u32[]{:S(2)}) collective-permute-start(bf16[864,128]{1,0:T(8,128)(2,1)S(1)} %get-tuple-element.62), channel_id=1, source_target_pairs={{0,16},{4,20},{8,24},{12,28},{16,0},{20,4},{24,8},{28,12},{1,17},{... | collective-permute-start | bytes 663560 | tf_op jit(solution)/shard_map/ppermute | solution.py:379
  196.3 14.0 %collective-permute-start.18 = (bf16[864,128]{1,0:T(8,128)(2,1)S(1)}, bf16[864,128]{1,0:T(8,128)(2,1)S(1)}, u32[]{:S(2)}, u32[]{:S(2)}) collective-permute-start(bf16[864,128]{1,0:T(8,128)(2,1)S(1)} %get-tuple-element.63), channel_id=1, source_target_pairs={{0,20},{4,16},{8,28},{12,24},{16,4},{20,0},{24,12},{28,8},{1,21},{... | collective-permute-start | bytes 663560 | tf_op jit(solution)/shard_map/ppermute | solution.py:379
  196.3 20.8 %collective-permute-start.15 = (bf16[864,128]{1,0:T(8,128)(2,1)S(1)}, bf16[864,128]{1,0:T(8,128)(2,1)S(1)}, u32[]{:S(2)}, u32[]{:S(2)}) collective-permute-start(bf16[864,128]{1,0:T(8,128)(2,1)S(1)} %get-tuple-element.60), channel_id=1, source_target_pairs={{0,24},{4,28},{8,16},{12,20},{16,8},{20,12},{24,0},{28,4},{1,25},{... | collective-permute-start | bytes 663560 | tf_op jit(solution)/shard_map/ppermute | solution.py:379
  196.7 25.0 %collective-permute-start.16 = (bf16[864,128]{1,0:T(8,128)(2,1)S(1)}, bf16[864,128]{1,0:T(8,128)(2,1)S(1)}, u32[]{:S(2)}, u32[]{:S(2)}) collective-permute-start(bf16[864,128]{1,0:T(8,128)(2,1)S(1)} %get-tuple-element.61), channel_id=1, source_target_pairs={{0,28},{4,24},{8,20},{12,16},{16,12},{20,8},{24,4},{28,0},{1,29},{... | collective-permute-start | bytes 663560 | tf_op jit(solution)/shard_map/ppermute | solution.py:379
  (19 other events, 336.5 us)

commit v3 on v2

--- a/solution.py
+++ b/solution.py
@@ -198,47 +198,45 @@
 def newton_body(core_ref, own_ref, got_ref, out_ref, r_ref, q_ref, y_ref, r2_ref, p2_ref, q2_ref, y2_ref, beside):
     half, size = own_ref.shape
     core = core_ref[0]
-    r_ref[pl.ds(pl.multiple_of(core * half, half), half), :] = own_ref[...].astype(F32)
-    r_ref[pl.ds(pl.multiple_of((1 - core) * half, half), half), :] = got_ref[...].astype(F32)
+    r2_ref[0, pl.ds(pl.multiple_of(core * half, half), half), :] = own_ref[...]
+    r2_ref[0, pl.ds(pl.multiple_of((1 - core) * half, half), half), :] = got_ref[...]
     row = lax.broadcasted_iota(jnp.int32, (size, size), 0)
     column = lax.broadcasted_iota(jnp.int32, (size, size), 1)
     eye = row == column
-    gram = r_ref[...]
-    scale2 = jnp.sum(jnp.where(eye, gram, 0.0)) + EPSILON
-    r_ref[...] = gram / scale2
-
-    def halves(ref, value):
+    scale2 = jnp.sum(jnp.where(eye, r2_ref[0].astype(F32), 0.0)) + EPSILON
+
+    def halves(ref, value, exact):
         high = value.astype(BF16)
         ref[0] = high
-        ref[1] = (value - high.astype(F32)).astype(BF16)
-
-    def mult(left, right, terms):
+        if exact:
+            ref[1] = (value - high.astype(F32)).astype(BF16)
+
+    def mult(left, right, exact):
+        terms = ((0, 0), (0, 1), (1, 0)) if exact else ((0, 0),)
         first, *rest = [jnp.dot(left[i], right[j], preferred_element_type=F32) for i, j in terms]
         return functools.reduce(jnp.add, rest, first)
 
-    fine = ((0, 0), (0, 1), (1, 0))
-
     def poly(exact):
-        halves(r2_ref, r_ref[...])
-        value = COEF_B * r_ref[...] + COEF_C * mult(r2_ref, r2_ref, fine if exact else fine[:1])
-        if exact:
-            halves(p2_ref, value)
-        else:
-            p2_ref[0] = value.astype(BF16)
+        halves(r2_ref, r_ref[...], exact)
+        halves(p2_ref, COEF_B * r_ref[...] + COEF_C * mult(r2_ref, r2_ref, exact), exact)
 
     def transform(exact):
-        halves(q2_ref, q_ref[...])
-        return COEF_A * q_ref[...] + mult(p2_ref, q2_ref, fine if exact else fine[:2])
-
-    def advance(exact):
-        halfway = COEF_A * r_ref[...] + mult(p2_ref, r2_ref, fine if exact else fine[:2])
-        halves(y2_ref, halfway)
+        halves(q2_ref, q_ref[...], exact)
+        return COEF_A * q_ref[...] + mult(p2_ref, q2_ref, exact)
+
+    def advance(exact, product=None):
+        product = mult(p2_ref, r2_ref, exact) if product is None else product
+        halfway = COEF_A * r_ref[...] + product
+        halves(y2_ref, halfway, exact)
         y_ref[...] = halfway
-        r_ref[...] = COEF_A * y_ref[...] + mult(y2_ref, p2_ref, fine if exact else fine[::2])
-
-    poly(False)
+        r_ref[...] = COEF_A * y_ref[...] + mult(y2_ref, p2_ref, exact)
+
+    ratio = 1.0 / scale2
+    r_ref[...] = r2_ref[0].astype(F32) * ratio
+    squared = (mult(r2_ref, r2_ref, False) * ratio) * ratio
+    p2_ref[0] = (COEF_B * r_ref[...] + COEF_C * squared).astype(BF16)
     q_ref[...] = jnp.where(eye, COEF_A, 0.0) + p2_ref[0].astype(F32)
-    advance(False)
+    advance(False, mult(p2_ref, r2_ref, False) * ratio)
 
     def sweep(exact):
         poly(exact)

time: 223 us -> 220 us (0.987)
  starting transfers between devices: 53.8 us -> 58.1 us
  waiting for transfers between devices: 98.1 us -> 94.3 us
  Pallas kernels: 66 us -> 62.7 us
    ppermute x28, starting transfers between devices: 39.3 us -> 43.6 us  [regroup(): return lax.ppermute(value, 'out', [(o, o ^ s) for o in range(n)])]
    ppermute x28, waiting for transfers between devices: 82.7 us -> 78.9 us  [regroup(): return lax.ppermute(value, 'out', [(o, o ^ s) for o in range(n)])]
    pallas_call x2, Pallas kernels: 33.3 us -> 30 us  [update_call(): pl.pallas_call(functools.partial(update_body, rows=rows, tiles=tiles, sca...]
  transfers between devices with their start and end apart: 44 -> 44, of which waited for: 23 -> 25; matrix products, arithmetic and copies ran while one was open for 1% -> 1% of each run, Pallas kernels for 28% -> 27%
where the time goes in v3:
time: 220 us
  waiting for transfers between devices  94.3 us (43%)
  Pallas kernels  62.7 us (28%)
  starting transfers between devices  58.1 us (26%)
  other arithmetic  2.89 us (1%)
    ppermute x28, waiting for transfers between devices, regroup(): return lax.ppermute(value, 'out', [(o, o ^ s) for o in range(n)])  78.9 us
    ppermute x28, starting transfers between devices, regroup(): return lax.ppermute(value, 'out', [(o, o ^ s) for o in range(n)])  43.6 us
    pallas_call x2, Pallas kernels, update_call(): pl.pallas_call(functools.partial(update_body, rows=rows, tiles=tiles, sca...  30 us
    pallas_call x8, Pallas kernels, source_call(): pl.pallas_call(functools.partial(source_body, rows=rows, tiles=tiles), gr...  18.8 us
    ppermute x16, waiting for transfers between devices, exchange(): return lax.ppermute(value, AXES, [(i, i ^ bits) for i in range(count)])  15.4 us
    ppermute x16, starting transfers between devices, exchange(): return lax.ppermute(value, AXES, [(i, i ^ bits) for i in range(count)])  14.5 us
    pallas_call x8, Pallas kernels, finish_call(): pl.pallas_call(functools.partial(finish_body, rows=rows, tiles=tiles), gr...  8.38 us
    pallas_call x2, Pallas kernels, gram_call(): pl.pallas_call(functools.partial(gram_body, rows=rows, tiles=tiles), in_s...  5.19 us
  transfers between devices with their start and end apart: 44, of which 25 were waited for; matrix products, arithmetic and copies ran while one was open for 1% of the time, Pallas kernels for 27%

profile of v3, /device:TPU:16, one launch (start us, length us, event | category | flops | bytes accessed | tf_op | source)
XLA Modules:
  0.0 219.9 jit_solution(9662502341050613276)
XLA Ops:
  6.0 2.4 %shard_map.61 = (bf16[864,128]{1,0:T(8,128)(2,1)}, bf16[864,128]{1,0:T(8,128)(2,1)}) custom-call(s32[1]{0:T(128)} %bitcast.10.kernel_ref, s32[1]{0:T(128)} %bitcast.1.side_ref, bf16[8,64,3456]{2,1,0:T(8,128)(2,1)} %grad_ref.15, bf16[8,64,3456]{2,1,0:T(8,128)(2,1)} %mom_ref.15), custom_call_target="tpu_custom_call" | custom-call | flops 1327104 | bytes 1327104 | tf_op jit(solution)/shard_map/pallas_call | solution.py:77
  8.7 2.5 %collective-permute-start.26 = (bf16[864,128]{1,0:T(8,128)(2,1)}, bf16[864,128]{1,0:T(8,128)(2,1)S(1)}, u32[]{:S(2)}, u32[]{:S(2)}) collective-permute-start(bf16[864,128]{1,0:T(8,128)(2,1)} %get-tuple-element.73), channel_id=1, source_target_pairs={{0,20},{4,16},{8,28},{12,24},{16,4},{20,0},{24,12},{28,8},{1,21},{... | collective-permute-start | bytes 663560 | tf_op jit(solution)/shard_map/ppermute | solution.py:377
  18.7 2.5 %collective-permute-start.28 = (bf16[864,128]{1,0:T(8,128)(2,1)}, bf16[864,128]{1,0:T(8,128)(2,1)}, u32[]{:S(2)}, u32[]{:S(2)}) collective-permute-start(bf16[864,128]{1,0:T(8,128)(2,1)} %get-tuple-element.75), channel_id=1, source_target_pairs={{0,28},{4,24},{8,20},{12,16},{16,12},{20,8},{24,4},{28,0},{1,29},{... | collective-permute-start | bytes 663560 | tf_op jit(solution)/shard_map/ppermute | solution.py:377
  21.7 11.0 %collective-permute-done.25.refs_4_ = bf16[864,128]{1,0:T(8,128)(2,1)S(1)} collective-permute-done((bf16[864,128]{1,0:T(8,128)(2,1)}, bf16[864,128]{1,0:T(8,128)(2,1)S(1)}, u32[]{:S(2)}, u32[]{:S(2)}) %collective-permute-start.25) | collective-permute-done | bytes 221216 | tf_op jit(solution)/shard_map/ppermute | solution.py:377
  32.7 5.7 %collective-permute-start.1 = (bf16[864,128]{1,0:T(8,128)(2,1)}, bf16[864,128]{1,0:T(8,128)(2,1)S(1)}, u32[]{:S(2)}, u32[]{:S(2)}) collective-permute-start(bf16[864,128]{1,0:T(8,128)(2,1)} %get-tuple-element.48), channel_id=1, source_target_pairs={{0,8},{4,12},{8,0},{12,4},{16,24},{20,28},{24,16},{28,20},{1,9},{5... | collective-permute-start | bytes 663560 | tf_op jit(solution)/shard_map/ppermute | solution.py:377
  38.6 5.4 %collective-permute-start.2 = (bf16[864,128]{1,0:T(8,128)(2,1)}, bf16[864,128]{1,0:T(8,128)(2,1)S(1)}, u32[]{:S(2)}, u32[]{:S(2)}) collective-permute-start(bf16[864,128]{1,0:T(8,128)(2,1)} %get-tuple-element.49), channel_id=1, source_target_pairs={{0,12},{4,8},{8,4},{12,0},{16,28},{20,24},{24,20},{28,16},{1,13},{... | collective-permute-start | bytes 663560 | tf_op jit(solution)/shard_map/ppermute | solution.py:377
  44.0 2.4 %shard_map.52 = (bf16[864,128]{1,0:T(8,128)(2,1)}, bf16[864,128]{1,0:T(8,128)(2,1)}) custom-call(s32[1]{0:T(128)} %bitcast.6.kernel_ref, s32[1]{0:T(128)} %bitcast.1.side_ref, bf16[8,64,3456]{2,1,0:T(8,128)(2,1)} %grad_ref.15, bf16[8,64,3456]{2,1,0:T(8,128)(2,1)} %mom_ref.15), custom_call_target="tpu_custom_call" | custom-call | flops 1327104 | bytes 1327104 | tf_op jit(solution)/shard_map/pallas_call | solution.py:77
  46.3 2.4 %shard_map.53 = (bf16[864,128]{1,0:T(8,128)(2,1)}, bf16[864,128]{1,0:T(8,128)(2,1)}) custom-call(s32[1]{0:T(128)} %bitcast.kernel_ref, s32[1]{0:T(128)} %bitcast.1.side_ref, bf16[8,64,3456]{2,1,0:T(8,128)(2,1)} %grad_ref.15, bf16[8,64,3456]{2,1,0:T(8,128)(2,1)} %mom_ref.15), custom_call_target="tpu_custom_call" | custom-call | flops 1327104 | bytes 1327104 | tf_op jit(solution)/shard_map/pallas_call | solution.py:77
  51.1 12.0 %collective-permute-done.28.refs_7_ = bf16[864,128]{1,0:T(8,128)(2,1)} collective-permute-done((bf16[864,128]{1,0:T(8,128)(2,1)}, bf16[864,128]{1,0:T(8,128)(2,1)}, u32[]{:S(2)}, u32[]{:S(2)}) %collective-permute-start.28) | collective-permute-done | bytes 221216 | tf_op jit(solution)/shard_map/ppermute | solution.py:377
  63.1 2.9 %collective-permute-start.6 = (bf16[864,128]{1,0:T(8,128)(2,1)}, bf16[864,128]{1,0:T(8,128)(2,1)}, u32[]{:S(2)}, u32[]{:S(2)}) collective-permute-start(bf16[864,128]{1,0:T(8,128)(2,1)} %get-tuple-element.53), channel_id=1, source_target_pairs={{0,28},{4,24},{8,20},{12,16},{16,12},{20,8},{24,4},{28,0},{1,29},{... | collective-permute-start | bytes 663560 | tf_op jit(solution)/shard_map/ppermute | solution.py:377
  66.6 2.6 %shard_map.63 = (f32[256,512]{1,0:T(8,128)S(1)}, bf16[256,512]{1,0:T(8,128)(2,1)S(1)}) custom-call(s32[1]{0:T(128)} %bitcast.2.core_ref, s32[1]{0:T(128)} %bitcast.1.side_ref, bf16[864,128]{1,0:T(8,128)(2,1)S(1)} %copy-done, bf16[864,128]{1,0:T(8,128)(2,1)} %collective-permute-done.22.refs_1_, bf16[864,128]{1,0:T(8,128)(2,1)S(1)} %collective-permute-done.23.refs_2_, ...), custom_call_target="tpu_custom_call" | custom-call | flops 939524096 | bytes 3670016 | tf_op jit(solution)/shard_map/pallas_call | solution.py:119
  69.3 7.4 %collective-permute-done.4.refs_5_ = bf16[864,128]{1,0:T(8,128)(2,1)S(1)} collective-permute-done((bf16[864,128]{1,0:T(8,128)(2,1)}, bf16[864,128]{1,0:T(8,128)(2,1)S(1)}, u32[]{:S(2)}, u32[]{:S(2)}) %collective-permute-start.4) | collective-permute-done | bytes 221216 | tf_op jit(solution)/shard_map/ppermute | solution.py:377
  76.7 7.7 %collective-permute-done.5.refs_6_ = bf16[864,128]{1,0:T(8,128)(2,1)S(1)} collective-permute-done((bf16[864,128]{1,0:T(8,128)(2,1)}, bf16[864,128]{1,0:T(8,128)(2,1)S(1)}, u32[]{:S(2)}, u32[]{:S(2)}) %collective-permute-start.5) | collective-permute-done | bytes 221216 | tf_op jit(solution)/shard_map/ppermute | solution.py:377
  84.3 3.2 %collective-permute-done.6.refs_7_ = bf16[864,128]{1,0:T(8,128)(2,1)} collective-permute-done((bf16[864,128]{1,0:T(8,128)(2,1)}, bf16[864,128]{1,0:T(8,128)(2,1)}, u32[]{:S(2)}, u32[]{:S(2)}) %collective-permute-start.6) | collective-permute-done | bytes 221216 | tf_op jit(solution)/shard_map/ppermute | solution.py:377
  88.4 2.6 %shard_map.54 = (f32[256,512]{1,0:T(8,128)S(1)}, bf16[256,512]{1,0:T(8,128)(2,1)S(1)}) custom-call(s32[1]{0:T(128)} %bitcast.2.core_ref, s32[1]{0:T(128)} %bitcast.1.side_ref, bf16[864,128]{1,0:T(8,128)(2,1)S(1)} %copy-done.1, bf16[864,128]{1,0:T(8,128)(2,1)} %collective-permute-done.refs_1_, bf16[864,128]{1,0:T(8,128)(2,1)S(1)} %collective-permute-done.1.refs_2_, ...), custom_call_target="tpu_custom_call" | custom-call | flops 939524096 | bytes 3670016 | tf_op jit(solution)/shard_map/pallas_call | solution.py:119
  97.1 2.4 %collective-permute-done.32.refs_2_ = bf16[64,512]{1,0:T(8,128)(2,1)S(1)} collective-permute-done((bf16[64,512]{1,0:T(8,128)(2,1)S(1)}, bf16[64,512]{1,0:T(8,128)(2,1)S(1)}, u32[]{:S(2)}, u32[]{:S(2)}) %collective-permute-start.32) | collective-permute-done | bytes 65568 | tf_op jit(solution)/shard_map/ppermute | solution.py:351
  100.6 2.4 %collective-permute-start.35 = (bf16[64,512]{1,0:T(8,128)(2,1)S(1)}, bf16[64,512]{1,0:T(8,128)(2,1)S(1)}, u32[]{:S(2)}, u32[]{:S(2)}) collective-permute-start(bf16[64,512]{1,0:T(8,128)(2,1)S(1)} %shard_map.65.refs_0_), channel_id=1, source_target_pairs={{0,6},{1,7},{2,4},{3,5},{4,2},{5,3},{6,0},{7,1},{8,14},{9,15},{10,... | collective-permute-start | bytes 196616 | tf_op jit(solution)/shard_map/ppermute | solution.py:351
  106.0 2.5 %collective-permute-start.10 = (bf16[64,512]{1,0:T(8,128)(2,1)S(1)}, bf16[64,512]{1,0:T(8,128)(2,1)S(1)}, u32[]{:S(2)}, u32[]{:S(2)}) collective-permute-start(bf16[64,512]{1,0:T(8,128)(2,1)S(1)} %get-tuple-element.59), channel_id=1, source_target_pairs={{0,6},{1,7},{2,4},{3,5},{4,2},{5,3},{6,0},{7,1},{8,14},{9,15},{10,... | collective-permute-start | bytes 196616 | tf_op jit(solution)/shard_map/ppermute | solution.py:351
  121.2 15.0 %shard_map.67 = (bf16[864,128]{1,0:T(8,128)(2,1)S(1)}, bf16[864,128]{1,0:T(8,128)(2,1)S(1)}, bf16[864,128]{1,0:T(8,128)(2,1)S(1)}, bf16[864,128]{1,0:T(8,128)(2,...) custom-call(s32[1]{0:T(128)} %bitcast.2.core_ref, ...), custom_call_target="tpu_custom_call" | custom-call | flops 14629732352 | bytes 3670016 | tf_op jit(solution)/shard_map/pallas_call | solution.py:292
  137.3 2.5 %collective-permute-start.42 = (bf16[864,128]{1,0:T(8,128)(2,1)S(1)}, bf16[864,128]{1,0:T(8,128)(2,1)S(1)}, u32[]{:S(2)}, u32[]{:S(2)}) collective-permute-start(bf16[864,128]{1,0:T(8,128)(2,1)S(1)} %get-tuple-element.87), channel_id=1, source_target_pairs={{0,12},{4,8},{8,4},{12,0},{16,28},{20,24},{24,20},{28,16},{1,13},{... | collective-permute-start | bytes 663560 | tf_op jit(solution)/shard_map/ppermute | solution.py:377
  139.8 3.4 %collective-permute-start.40 = (bf16[864,128]{1,0:T(8,128)(2,1)S(1)}, bf16[864,128]{1,0:T(8,128)(2,1)S(1)}, u32[]{:S(2)}, u32[]{:S(2)}) collective-permute-start(bf16[864,128]{1,0:T(8,128)(2,1)S(1)} %get-tuple-element.85), channel_id=1, source_target_pairs={{0,20},{4,16},{8,28},{12,24},{16,4},{20,0},{24,12},{28,8},{1,21},{... | collective-permute-start | bytes 663560 | tf_op jit(solution)/shard_map/ppermute | solution.py:377
  143.2 15.0 %shard_map.58 = (bf16[864,128]{1,0:T(8,128)(2,1)S(1)}, bf16[864,128]{1,0:T(8,128)(2,1)S(1)}, bf16[864,128]{1,0:T(8,128)(2,1)S(1)}, bf16[864,128]{1,0:T(8,128)(2,...) custom-call(s32[1]{0:T(128)} %bitcast.2.core_ref, ...), custom_call_target="tpu_custom_call" | custom-call | flops 14629732352 | bytes 3670016 | tf_op jit(solution)/shard_map/pallas_call | solution.py:292
  158.3 2.5 %collective-permute-start.38 = (bf16[864,128]{1,0:T(8,128)(2,1)S(1)}, bf16[864,128]{1,0:T(8,128)(2,1)S(1)}, u32[]{:S(2)}, u32[]{:S(2)}) collective-permute-start(bf16[864,128]{1,0:T(8,128)(2,1)S(1)} %get-tuple-element.83), channel_id=1, source_target_pairs={{0,28},{4,24},{8,20},{12,16},{16,12},{20,8},{24,4},{28,0},{1,29},{... | collective-permute-start | bytes 663560 | tf_op jit(solution)/shard_map/ppermute | solution.py:377
  163.6 3.8 %collective-permute-done.40.second_ref = bf16[864,128]{1,0:T(8,128)(2,1)S(1)} collective-permute-done((bf16[864,128]{1,0:T(8,128)(2,1)S(1)}, bf16[864,128]{1,0:T(8,128)(2,1)S(1)}, u32[]{:S(2)}, u32[]{:S(2)}) %collective-permute-start.40) | collective-permute-done | bytes 221216 | tf_op jit(solution)/shard_map/ppermute | solution.py:377
  167.4 4.9 %collective-permute-start.20 = (bf16[864,128]{1,0:T(8,128)(2,1)S(1)}, bf16[864,128]{1,0:T(8,128)(2,1)S(1)}, u32[]{:S(2)}, u32[]{:S(2)}) collective-permute-start(bf16[864,128]{1,0:T(8,128)(2,1)S(1)} %get-tuple-element.65), channel_id=1, source_target_pairs={{0,12},{4,8},{8,4},{12,0},{16,28},{20,24},{24,20},{28,16},{1,13},{... | collective-permute-start | bytes 663560 | tf_op jit(solution)/shard_map/ppermute | solution.py:377
  172.3 3.3 %collective-permute-done.37.first_ref = bf16[864,128]{1,0:T(8,128)(2,1)S(1)} collective-permute-done((bf16[864,128]{1,0:T(8,128)(2,1)S(1)}, bf16[864,128]{1,0:T(8,128)(2,1)S(1)}, u32[]{:S(2)}, u32[]{:S(2)}) %collective-permute-start.37) | collective-permute-done | bytes 221216 | tf_op jit(solution)/shard_map/ppermute | solution.py:377
  175.6 10.8 %collective-permute-done.38.second_ref = bf16[864,128]{1,0:T(8,128)(2,1)S(1)} collective-permute-done((bf16[864,128]{1,0:T(8,128)(2,1)S(1)}, bf16[864,128]{1,0:T(8,128)(2,1)S(1)}, u32[]{:S(2)}, u32[]{:S(2)}) %collective-permute-start.38) | collective-permute-done | bytes 221216 | tf_op jit(solution)/shard_map/ppermute | solution.py:377
  188.9 2.9 %add_convert_fusion = bf16[8,64,3456]{2,1,0:T(8,128)(2,1)} fusion(bf16[8,64,3456]{2,1,0:T(8,128)(2,1)S(1)} %copy-done.3, bf16[8,64,3456]{2,1,0:T(8,128)(2,1)S(1)} %copy-done.4), kind=kLoop, calls=%fused_computation | loop fusion | flops 8847360 | bytes 10616832 | tf_op jit(solution)/shard_map/convert_element_type | solution.py:399
  198.1 4.5 %collective-permute-done.17.first_ref = bf16[864,128]{1,0:T(8,128)(2,1)S(1)} collective-permute-done((bf16[864,128]{1,0:T(8,128)(2,1)S(1)}, bf16[864,128]{1,0:T(8,128)(2,1)S(1)}, u32[]{:S(2)}, u32[]{:S(2)}) %collective-permute-start.17) | collective-permute-done | bytes 221216 | tf_op jit(solution)/shard_map/ppermute | solution.py:377
  202.6 4.7 %collective-permute-done.18.second_ref = bf16[864,128]{1,0:T(8,128)(2,1)S(1)} collective-permute-done((bf16[864,128]{1,0:T(8,128)(2,1)S(1)}, bf16[864,128]{1,0:T(8,128)(2,1)S(1)}, u32[]{:S(2)}, u32[]{:S(2)}) %collective-permute-start.18) | collective-permute-done | bytes 221216 | tf_op jit(solution)/shard_map/ppermute | solution.py:377
  208.4 6.0 %collective-permute-done.15.first_ref = bf16[864,128]{1,0:T(8,128)(2,1)S(1)} collective-permute-done((bf16[864,128]{1,0:T(8,128)(2,1)S(1)}, bf16[864,128]{1,0:T(8,128)(2,1)S(1)}, u32[]{:S(2)}, u32[]{:S(2)}) %collective-permute-start.15) | collective-permute-done | bytes 221216 | tf_op jit(solution)/shard_map/ppermute | solution.py:377
  214.4 4.4 %collective-permute-done.16.second_ref = bf16[864,128]{1,0:T(8,128)(2,1)S(1)} collective-permute-done((bf16[864,128]{1,0:T(8,128)(2,1)S(1)}, bf16[864,128]{1,0:T(8,128)(2,1)S(1)}, u32[]{:S(2)}, u32[]{:S(2)}) %collective-permute-start.16) | collective-permute-done | bytes 221216 | tf_op jit(solution)/shard_map/ppermute | solution.py:377
  (98 shorter events, 55.3 us)
Async XLA Ops:
  3.0 15.7 %collective-permute-start.23 = (bf16[864,128]{1,0:T(8,128)(2,1)}, bf16[864,128]{1,0:T(8,128)(2,1)S(1)}, u32[]{:S(2)}, u32[]{:S(2)}) collective-permute-start(bf16[864,128]{1,0:T(8,128)(2,1)} %get-tuple-element.70), channel_id=1, source_target_pairs={{0,8},{4,12},{8,0},{12,4},{16,24},{20,28},{24,16},{28,20},{1,9},{5... | collective-permute-start | bytes 663560 | tf_op jit(solution)/shard_map/ppermute | solution.py:377
  4.6 16.7 %collective-permute-start.24 = (bf16[864,128]{1,0:T(8,128)(2,1)}, bf16[864,128]{1,0:T(8,128)(2,1)S(1)}, u32[]{:S(2)}, u32[]{:S(2)}) collective-permute-start(bf16[864,128]{1,0:T(8,128)(2,1)} %get-tuple-element.71), channel_id=1, source_target_pairs={{0,12},{4,8},{8,4},{12,0},{16,28},{20,24},{24,20},{28,16},{1,13},{... | collective-permute-start | bytes 663560 | tf_op jit(solution)/shard_map/ppermute | solution.py:377
  8.3 24.4 %collective-permute-start.25 = (bf16[864,128]{1,0:T(8,128)(2,1)}, bf16[864,128]{1,0:T(8,128)(2,1)S(1)}, u32[]{:S(2)}, u32[]{:S(2)}) collective-permute-start(bf16[864,128]{1,0:T(8,128)(2,1)} %get-tuple-element.72), channel_id=1, source_target_pairs={{0,16},{4,20},{8,24},{12,28},{16,0},{20,4},{24,8},{28,12},{1,17},{... | collective-permute-start | bytes 663560 | tf_op jit(solution)/shard_map/ppermute | solution.py:377
  8.7 29.9 %collective-permute-start.26 = (bf16[864,128]{1,0:T(8,128)(2,1)}, bf16[864,128]{1,0:T(8,128)(2,1)S(1)}, u32[]{:S(2)}, u32[]{:S(2)}) collective-permute-start(bf16[864,128]{1,0:T(8,128)(2,1)} %get-tuple-element.73), channel_id=1, source_target_pairs={{0,20},{4,16},{8,28},{12,24},{16,4},{20,0},{24,12},{28,8},{1,21},{... | collective-permute-start | bytes 663560 | tf_op jit(solution)/shard_map/ppermute | solution.py:377
  13.6 32.8 %collective-permute-start.27 = (bf16[864,128]{1,0:T(8,128)(2,1)}, bf16[864,128]{1,0:T(8,128)(2,1)S(1)}, u32[]{:S(2)}, u32[]{:S(2)}) collective-permute-start(bf16[864,128]{1,0:T(8,128)(2,1)} %get-tuple-element.74), channel_id=1, source_target_pairs={{0,24},{4,28},{8,16},{12,20},{16,8},{20,12},{24,0},{28,4},{1,25},{... | collective-permute-start | bytes 663560 | tf_op jit(solution)/shard_map/ppermute | solution.py:377
  18.7 44.4 %collective-permute-start.28 = (bf16[864,128]{1,0:T(8,128)(2,1)}, bf16[864,128]{1,0:T(8,128)(2,1)}, u32[]{:S(2)}, u32[]{:S(2)}) collective-permute-start(bf16[864,128]{1,0:T(8,128)(2,1)} %get-tuple-element.75), channel_id=1, source_target_pairs={{0,28},{4,24},{8,20},{12,16},{16,12},{20,8},{24,4},{28,0},{1,29},{... | collective-permute-start | bytes 663560 | tf_op jit(solution)/shard_map/ppermute | solution.py:377
  21.2 41.8 %collective-permute-start.22 = (bf16[864,128]{1,0:T(8,128)(2,1)}, bf16[864,128]{1,0:T(8,128)(2,1)}, u32[]{:S(2)}, u32[]{:S(2)}) collective-permute-start(bf16[864,128]{1,0:T(8,128)(2,1)} %get-tuple-element.69), channel_id=1, source_target_pairs={{0,4},{4,0},{8,12},{12,8},{16,20},{20,16},{24,28},{28,24},{1,5},{5... | collective-permute-start | bytes 663560 | tf_op jit(solution)/shard_map/ppermute | solution.py:377
  32.7 30.4 %collective-permute-start.1 = (bf16[864,128]{1,0:T(8,128)(2,1)}, bf16[864,128]{1,0:T(8,128)(2,1)S(1)}, u32[]{:S(2)}, u32[]{:S(2)}) collective-permute-start(bf16[864,128]{1,0:T(8,128)(2,1)} %get-tuple-element.48), channel_id=1, source_target_pairs={{0,8},{4,12},{8,0},{12,4},{16,24},{20,28},{24,16},{28,20},{1,9},{5... | collective-permute-start | bytes 663560 | tf_op jit(solution)/shard_map/ppermute | solution.py:377
  38.6 27.5 %collective-permute-start.2 = (bf16[864,128]{1,0:T(8,128)(2,1)}, bf16[864,128]{1,0:T(8,128)(2,1)S(1)}, u32[]{:S(2)}, u32[]{:S(2)}) collective-permute-start(bf16[864,128]{1,0:T(8,128)(2,1)} %get-tuple-element.49), channel_id=1, source_target_pairs={{0,12},{4,8},{8,4},{12,0},{16,28},{20,24},{24,20},{28,16},{1,13},{... | collective-permute-start | bytes 663560 | tf_op jit(solution)/shard_map/ppermute | solution.py:377
  46.3 22.9 %collective-permute-start.3 = (bf16[864,128]{1,0:T(8,128)(2,1)}, bf16[864,128]{1,0:T(8,128)(2,1)S(1)}, u32[]{:S(2)}, u32[]{:S(2)}) collective-permute-start(bf16[864,128]{1,0:T(8,128)(2,1)} %get-tuple-element.50), channel_id=1, source_target_pairs={{0,16},{4,20},{8,24},{12,28},{16,0},{20,4},{24,8},{28,12},{1,17},{... | collective-permute-start | bytes 663560 | tf_op jit(solution)/shard_map/ppermute | solution.py:377
  63.1 13.6 %collective-permute-start.4 = (bf16[864,128]{1,0:T(8,128)(2,1)}, bf16[864,128]{1,0:T(8,128)(2,1)S(1)}, u32[]{:S(2)}, u32[]{:S(2)}) collective-permute-start(bf16[864,128]{1,0:T(8,128)(2,1)} %get-tuple-element.51), channel_id=1, source_target_pairs={{0,20},{4,16},{8,28},{12,24},{16,4},{20,0},{24,12},{28,8},{1,21},{... | collective-permute-start | bytes 663560 | tf_op jit(solution)/shard_map/ppermute | solution.py:377
  63.1 21.3 %collective-permute-start.5 = (bf16[864,128]{1,0:T(8,128)(2,1)}, bf16[864,128]{1,0:T(8,128)(2,1)S(1)}, u32[]{:S(2)}, u32[]{:S(2)}) collective-permute-start(bf16[864,128]{1,0:T(8,128)(2,1)} %get-tuple-element.52), channel_id=1, source_target_pairs={{0,24},{4,28},{8,16},{12,20},{16,8},{20,12},{24,0},{28,4},{1,25},{... | collective-permute-start | bytes 663560 | tf_op jit(solution)/shard_map/ppermute | solution.py:377
  63.1 24.4 %collective-permute-start.6 = (bf16[864,128]{1,0:T(8,128)(2,1)}, bf16[864,128]{1,0:T(8,128)(2,1)}, u32[]{:S(2)}, u32[]{:S(2)}) collective-permute-start(bf16[864,128]{1,0:T(8,128)(2,1)} %get-tuple-element.53), channel_id=1, source_target_pairs={{0,28},{4,24},{8,20},{12,16},{16,12},{20,8},{24,4},{28,0},{1,29},{... | collective-permute-start | bytes 663560 | tf_op jit(solution)/shard_map/ppermute | solution.py:377
  66.1 21.4 %collective-permute-start = (bf16[864,128]{1,0:T(8,128)(2,1)}, bf16[864,128]{1,0:T(8,128)(2,1)}, u32[]{:S(2)}, u32[]{:S(2)}) collective-permute-start(bf16[864,128]{1,0:T(8,128)(2,1)} %get-tuple-element.47), channel_id=1, source_target_pairs={{0,4},{4,0},{8,12},{12,8},{16,20},{20,16},{24,28},{28,24},{1,5},{5... | collective-permute-start | bytes 663560 | tf_op jit(solution)/shard_map/ppermute | solution.py:377
  69.2 21.9 %collective-permute-start.29 = (bf16[256,512]{1,0:T(8,128)(2,1)S(1)}, bf16[256,512]{1,0:T(8,128)(2,1)S(1)}, u32[]{:S(2)}, u32[]{:S(2)}) collective-permute-start(bf16[256,512]{1,0:T(8,128)(2,1)S(1)} %get-tuple-element.77), channel_id=1, source_target_pairs={{0,1},{1,0},{2,3},{3,2},{4,5},{5,4},{6,7},{7,6},{8,9},{9,8},{10,11... | collective-permute-start | bytes 786440 | tf_op jit(solution)/shard_map/ppermute | solution.py:351
  91.0 14.8 %collective-permute-start.7 = (bf16[256,512]{1,0:T(8,128)(2,1)S(1)}, bf16[256,512]{1,0:T(8,128)(2,1)S(1)}, u32[]{:S(2)}, u32[]{:S(2)}) collective-permute-start(bf16[256,512]{1,0:T(8,128)(2,1)S(1)} %get-tuple-element.55), channel_id=1, source_target_pairs={{0,1},{1,0},{2,3},{3,2},{4,5},{5,4},{6,7},{7,6},{8,9},{9,8},{10,11... | collective-permute-start | bytes 786440 | tf_op jit(solution)/shard_map/ppermute | solution.py:351
  105.8 15.4 %collective-permute-start.36 = (bf16[256,512]{1,0:T(8,128)(2,1)S(1)}, bf16[256,512]{1,0:T(8,128)(2,1)S(1)}, u32[]{:S(2)}, u32[]{:S(2)}) collective-permute-start(bf16[256,512]{1,0:T(8,128)(2,1)S(1)} %shard_map.66.own_ref), channel_id=1, source_target_pairs={{0,1},{1,0},{2,3},{3,2},{4,5},{5,4},{6,7},{7,6},{8,9},{9,8},{10,11... | collective-permute-start | bytes 786440 | tf_op jit(solution)/shard_map/ppermute | solution.py:351
  121.1 18.7 %collective-permute-start.14 = (bf16[256,512]{1,0:T(8,128)(2,1)S(1)}, bf16[256,512]{1,0:T(8,128)(2,1)S(1)}, u32[]{:S(2)}, u32[]{:S(2)}) collective-permute-start(bf16[256,512]{1,0:T(8,128)(2,1)S(1)} %shard_map.57.own_ref), channel_id=1, source_target_pairs={{0,1},{1,0},{2,3},{3,2},{4,5},{5,4},{6,7},{7,6},{8,9},{9,8},{10,11... | collective-permute-start | bytes 786440 | tf_op jit(solution)/shard_map/ppermute | solution.py:351
  136.2 22.0 %collective-permute-start.43 = (bf16[864,128]{1,0:T(8,128)(2,1)S(1)}, bf16[864,128]{1,0:T(8,128)(2,1)S(1)}, u32[]{:S(2)}, u32[]{:S(2)}) collective-permute-start(bf16[864,128]{1,0:T(8,128)(2,1)S(1)} %get-tuple-element.89), channel_id=1, source_target_pairs={{0,4},{4,0},{8,12},{12,8},{16,20},{20,16},{24,28},{28,24},{1,5},{5... | collective-permute-start | bytes 663560 | tf_op jit(solution)/shard_map/ppermute | solution.py:377
  137.3 21.0 %collective-permute-start.41 = (bf16[864,128]{1,0:T(8,128)(2,1)S(1)}, bf16[864,128]{1,0:T(8,128)(2,1)S(1)}, u32[]{:S(2)}, u32[]{:S(2)}) collective-permute-start(bf16[864,128]{1,0:T(8,128)(2,1)S(1)} %get-tuple-element.86), channel_id=1, source_target_pairs={{0,8},{4,12},{8,0},{12,4},{16,24},{20,28},{24,16},{28,20},{1,9},{5... | collective-permute-start | bytes 663560 | tf_op jit(solution)/shard_map/ppermute | solution.py:377
  137.3 23.6 %collective-permute-start.42 = (bf16[864,128]{1,0:T(8,128)(2,1)S(1)}, bf16[864,128]{1,0:T(8,128)(2,1)S(1)}, u32[]{:S(2)}, u32[]{:S(2)}) collective-permute-start(bf16[864,128]{1,0:T(8,128)(2,1)S(1)} %get-tuple-element.87), channel_id=1, source_target_pairs={{0,12},{4,8},{8,4},{12,0},{16,28},{20,24},{24,20},{28,16},{1,13},{... | collective-permute-start | bytes 663560 | tf_op jit(solution)/shard_map/ppermute | solution.py:377
  139.8 22.0 %collective-permute-start.39 = (bf16[864,128]{1,0:T(8,128)(2,1)S(1)}, bf16[864,128]{1,0:T(8,128)(2,1)S(1)}, u32[]{:S(2)}, u32[]{:S(2)}) collective-permute-start(bf16[864,128]{1,0:T(8,128)(2,1)S(1)} %get-tuple-element.84), channel_id=1, source_target_pairs={{0,16},{4,20},{8,24},{12,28},{16,0},{20,4},{24,8},{28,12},{1,17},{... | collective-permute-start | bytes 663560 | tf_op jit(solution)/shard_map/ppermute | solution.py:377
  139.8 27.6 %collective-permute-start.40 = (bf16[864,128]{1,0:T(8,128)(2,1)S(1)}, bf16[864,128]{1,0:T(8,128)(2,1)S(1)}, u32[]{:S(2)}, u32[]{:S(2)}) collective-permute-start(bf16[864,128]{1,0:T(8,128)(2,1)S(1)} %get-tuple-element.85), channel_id=1, source_target_pairs={{0,20},{4,16},{8,28},{12,24},{16,4},{20,0},{24,12},{28,8},{1,21},{... | collective-permute-start | bytes 663560 | tf_op jit(solution)/shard_map/ppermute | solution.py:377
  158.2 17.3 %collective-permute-start.37 = (bf16[864,128]{1,0:T(8,128)(2,1)S(1)}, bf16[864,128]{1,0:T(8,128)(2,1)S(1)}, u32[]{:S(2)}, u32[]{:S(2)}) collective-permute-start(bf16[864,128]{1,0:T(8,128)(2,1)S(1)} %get-tuple-element.82), channel_id=1, source_target_pairs={{0,24},{4,28},{8,16},{12,20},{16,8},{20,12},{24,0},{28,4},{1,25},{... | collective-permute-start | bytes 663560 | tf_op jit(solution)/shard_map/ppermute | solution.py:377
  158.3 28.0 %collective-permute-start.38 = (bf16[864,128]{1,0:T(8,128)(2,1)S(1)}, bf16[864,128]{1,0:T(8,128)(2,1)S(1)}, u32[]{:S(2)}, u32[]{:S(2)}) collective-permute-start(bf16[864,128]{1,0:T(8,128)(2,1)S(1)} %get-tuple-element.83), channel_id=1, source_target_pairs={{0,28},{4,24},{8,20},{12,16},{16,12},{20,8},{24,4},{28,0},{1,29},{... | collective-permute-start | bytes 663560 | tf_op jit(solution)/shard_map/ppermute | solution.py:377
  160.8 25.5 %collective-permute-start.21 = (bf16[864,128]{1,0:T(8,128)(2,1)S(1)}, bf16[864,128]{1,0:T(8,128)(2,1)S(1)}, u32[]{:S(2)}, u32[]{:S(2)}) collective-permute-start(bf16[864,128]{1,0:T(8,128)(2,1)S(1)} %get-tuple-element.67), channel_id=1, source_target_pairs={{0,4},{4,0},{8,12},{12,8},{16,20},{20,16},{24,28},{28,24},{1,5},{5... | collective-permute-start | bytes 663560 | tf_op jit(solution)/shard_map/ppermute | solution.py:377
  161.8 24.8 %collective-permute-start.19 = (bf16[864,128]{1,0:T(8,128)(2,1)S(1)}, bf16[864,128]{1,0:T(8,128)(2,1)S(1)}, u32[]{:S(2)}, u32[]{:S(2)}) collective-permute-start(bf16[864,128]{1,0:T(8,128)(2,1)S(1)} %get-tuple-element.64), channel_id=1, source_target_pairs={{0,8},{4,12},{8,0},{12,4},{16,24},{20,28},{24,16},{28,20},{1,9},{5... | collective-permute-start | bytes 663560 | tf_op jit(solution)/shard_map/ppermute | solution.py:377
  167.4 29.6 %collective-permute-start.20 = (bf16[864,128]{1,0:T(8,128)(2,1)S(1)}, bf16[864,128]{1,0:T(8,128)(2,1)S(1)}, u32[]{:S(2)}, u32[]{:S(2)}) collective-permute-start(bf16[864,128]{1,0:T(8,128)(2,1)S(1)} %get-tuple-element.65), channel_id=1, source_target_pairs={{0,12},{4,8},{8,4},{12,0},{16,28},{20,24},{24,20},{28,16},{1,13},{... | collective-permute-start | bytes 663560 | tf_op jit(solution)/shard_map/ppermute | solution.py:377
  175.6 27.1 %collective-permute-start.17 = (bf16[864,128]{1,0:T(8,128)(2,1)S(1)}, bf16[864,128]{1,0:T(8,128)(2,1)S(1)}, u32[]{:S(2)}, u32[]{:S(2)}) collective-permute-start(bf16[864,128]{1,0:T(8,128)(2,1)S(1)} %get-tuple-element.62), channel_id=1, source_target_pairs={{0,16},{4,20},{8,24},{12,28},{16,0},{20,4},{24,8},{28,12},{1,17},{... | collective-permute-start | bytes 663560 | tf_op jit(solution)/shard_map/ppermute | solution.py:377
  186.3 21.0 %collective-permute-start.18 = (bf16[864,128]{1,0:T(8,128)(2,1)S(1)}, bf16[864,128]{1,0:T(8,128)(2,1)S(1)}, u32[]{:S(2)}, u32[]{:S(2)}) collective-permute-start(bf16[864,128]{1,0:T(8,128)(2,1)S(1)} %get-tuple-element.63), channel_id=1, source_target_pairs={{0,20},{4,16},{8,28},{12,24},{16,4},{20,0},{24,12},{28,8},{1,21},{... | collective-permute-start | bytes 663560 | tf_op jit(solution)/shard_map/ppermute | solution.py:377
  186.3 28.0 %collective-permute-start.15 = (bf16[864,128]{1,0:T(8,128)(2,1)S(1)}, bf16[864,128]{1,0:T(8,128)(2,1)S(1)}, u32[]{:S(2)}, u32[]{:S(2)}) collective-permute-start(bf16[864,128]{1,0:T(8,128)(2,1)S(1)} %get-tuple-element.60), channel_id=1, source_target_pairs={{0,24},{4,28},{8,16},{12,20},{16,8},{20,12},{24,0},{28,4},{1,25},{... | collective-permute-start | bytes 663560 | tf_op jit(solution)/shard_map/ppermute | solution.py:377
  186.6 32.3 %collective-permute-start.16 = (bf16[864,128]{1,0:T(8,128)(2,1)S(1)}, bf16[864,128]{1,0:T(8,128)(2,1)S(1)}, u32[]{:S(2)}, u32[]{:S(2)}) collective-permute-start(bf16[864,128]{1,0:T(8,128)(2,1)S(1)} %get-tuple-element.61), channel_id=1, source_target_pairs={{0,28},{4,24},{8,20},{12,16},{16,12},{20,8},{24,4},{28,0},{1,29},{... | collective-permute-start | bytes 663560 | tf_op jit(solution)/shard_map/ppermute | solution.py:377
  (19 other events, 301.9 us)

commit v4 on v3

--- a/solution.py
+++ b/solution.py
@@ -13,6 +13,7 @@
 GROUPS = 2
 SHARE = 2
 LANE = 128
+CHUNKS = 2
 
 BETA = 0.95
 EPSILON = 1e-06
@@ -27,6 +28,11 @@
 
 def sending(count):
     return list(reversed(range(count)))
+
+
+def arriving(count):
+    order = sending(count)
+    return order[::-1][: count // 2] + order[: count // 2]
 
 
 def source_of(gradient, momentum):
@@ -195,7 +201,7 @@
     )(chip, *pieces)
 
 
-def newton_body(core_ref, own_ref, got_ref, out_ref, r_ref, q_ref, y_ref, r2_ref, p2_ref, q2_ref, y2_ref, beside):
+def newton_body(core_ref, own_ref, got_ref, out_ref, r_ref, q_ref, y_ref, r2_ref, p2_ref, q2_ref, y2_ref):
     half, size = own_ref.shape
     core = core_ref[0]
     r2_ref[0, pl.ds(pl.multiple_of(core * half, half), half), :] = own_ref[...]
@@ -205,79 +211,105 @@
     eye = row == column
     scale2 = jnp.sum(jnp.where(eye, r2_ref[0].astype(F32), 0.0)) + EPSILON
 
-    def halves(ref, value, exact):
+    part = size // CHUNKS
+    slices = [slice(i * part, (i + 1) * part) for i in range(CHUNKS)]
+
+    def halves(ref, where, value, exact):
         high = value.astype(BF16)
-        ref[0] = high
+        ref[0, where, :] = high
         if exact:
-            ref[1] = (value - high.astype(F32)).astype(BF16)
-
-    def mult(left, right, exact):
+            ref[1, where, :] = (value - high.astype(F32)).astype(BF16)
+
+    def mult(left, where, right, exact):
         terms = ((0, 0), (0, 1), (1, 0)) if exact else ((0, 0),)
-        first, *rest = [jnp.dot(left[i], right[j], preferred_element_type=F32) for i, j in terms]
+        first, *rest = [jnp.dot(left[i, where, :], right[j], preferred_element_type=F32) for i, j in terms]
         return functools.reduce(jnp.add, rest, first)
 
-    def poly(exact):
-        halves(r2_ref, r_ref[...], exact)
-        halves(p2_ref, COEF_B * r_ref[...] + COEF_C * mult(r2_ref, r2_ref, exact), exact)
-
-    def transform(exact):
-        halves(q2_ref, q_ref[...], exact)
-        return COEF_A * q_ref[...] + mult(p2_ref, q2_ref, exact)
-
-    def advance(exact, product=None):
-        product = mult(p2_ref, r2_ref, exact) if product is None else product
-        halfway = COEF_A * r_ref[...] + product
-        halves(y2_ref, halfway, exact)
-        y_ref[...] = halfway
-        r_ref[...] = COEF_A * y_ref[...] + mult(y2_ref, p2_ref, exact)
+    def poly(exact, ratio=None):
+        for where in slices:
+            product = mult(r2_ref, where, r2_ref, exact)
+            product = product if ratio is None else (product * ratio) * ratio
+            halves(p2_ref, where, COEF_B * r_ref[where, :] + COEF_C * product, exact)
+
+    def transform(where, exact):
+        return COEF_A * q_ref[where, :] + mult(p2_ref, where, q2_ref, exact)
+
+    def advance(exact, following, ratio=None):
+        for where in slices:
+            product = mult(p2_ref, where, r2_ref, exact)
+            halfway = COEF_A * r_ref[where, :] + (product if ratio is None else product * ratio)
+            halves(y2_ref, where, halfway, exact)
+            y_ref[where, :] = halfway
+        for where in slices:
+            value = COEF_A * y_ref[where, :] + mult(y2_ref, where, p2_ref, exact)
+            r_ref[where, :] = value
+            halves(r2_ref, where, value, following)
 
     ratio = 1.0 / scale2
     r_ref[...] = r2_ref[0].astype(F32) * ratio
-    squared = (mult(r2_ref, r2_ref, False) * ratio) * ratio
-    p2_ref[0] = (COEF_B * r_ref[...] + COEF_C * squared).astype(BF16)
+    poly(False, ratio)
     q_ref[...] = jnp.where(eye, COEF_A, 0.0) + p2_ref[0].astype(F32)
-    advance(False, mult(p2_ref, r2_ref, False) * ratio)
-
-    def sweep(exact):
+    advance(False, False, ratio)
+
+    def sweep(exact, following):
+        for where in slices:
+            halves(q2_ref, where, q_ref[where, :], exact)
         poly(exact)
-        q_ref[...] = transform(exact)
-        advance(exact)
-
-    sweep(False)
+        for where in slices:
+            q_ref[where, :] = transform(where, exact)
+        advance(exact, following)
+
+    sweep(False, True)
 
     def loop(_, carry):
-        sweep(True)
+        sweep(True, True)
         return carry
 
     lax.fori_loop(2, ITERS - 1, loop, 0)
-    beside()
+    for where in slices:
+        halves(q2_ref, where, q_ref[where, :], True)
     poly(True)
-    out_ref[...] = (transform(True) / jnp.sqrt(scale2)).astype(BF16)
+    for where in slices:
+        out_ref[where, :] = (transform(where, True) / jnp.sqrt(scale2)).astype(BF16)
 
 
 def update_body(core_ref, side_ref, own_ref, got_ref, *refs, rows, tiles, scale, blocks):
     any_refs, out_refs = refs[:blocks], refs[blocks : 2 * blocks]
-    factor_ref, in_ref, x_ref, part_ref, sem, *newton_refs = refs[2 * blocks :]
+    factor_ref, order_ref, in_ref, sem, *newton_refs = refs[2 * blocks :]
     copies = [pltpu.make_async_copy(ref, in_ref.at[s], sem.at[s]) for s, ref in enumerate(any_refs)]
     for copy in copies:
         copy.start()
-
-    def beside():
-        for copy in copies:
-            copy.wait()
-        unpack(side_ref, [in_ref.at[s] for s in range(blocks)], x_ref, rows, tiles)
-
-    newton_body(core_ref, own_ref, got_ref, factor_ref, *newton_refs, beside)
+    newton_body(core_ref, own_ref, got_ref, factor_ref, *newton_refs)
+    side = side_ref[0]
+    for s in range(blocks):
+        base = pl.multiple_of((s // SHARE * SHARE + (side ^ (s % SHARE))) * rows, rows)
+        order_ref[s * rows : (s + 1) * rows, :] = factor_ref[pl.ds(base, rows), :]
+    for copy in copies:
+        copy.wait()
     half = rows // 2
     middle = LANE // 2
+    zeros = jnp.zeros((rows, middle), BF16)
+
+    def read(t):
+        found = []
+        for p in range(blocks):
+            block = in_ref.at[p // SHARE * SHARE + (side ^ (p % SHARE))]
+            if t < tiles:
+                found.append(block[t * rows : (t + 1) * rows, :])
+            else:
+                last = block[tiles * rows : tiles * rows + half, :]
+                last = jnp.concatenate([last[:, :middle], last[:, middle:]], axis=0)
+                found.append(jnp.concatenate([last, zeros], axis=1))
+        return jnp.concatenate(found, axis=0)
+
     step = 2
     for t in range(0, tiles + 1, step):
-        part = jnp.dot(factor_ref[...], x_ref[:, t * LANE : (t + step) * LANE], preferred_element_type=F32)
-        part_ref[...] = (scale * part).astype(BF16)
+        tile = jnp.concatenate([read(u) for u in range(t, t + step)], axis=1)
+        part = jnp.dot(order_ref[...], tile, preferred_element_type=F32)
+        part = (scale * part).astype(BF16)
         for s, out_ref in enumerate(out_refs):
-            base = pl.multiple_of((s // SHARE * SHARE + (side_ref[0] ^ (s % SHARE))) * rows, rows)
-            for u in range(t, min(t + step, tiles + 1)):
-                block = part_ref[pl.ds(base, rows), (u - t) * LANE : (u - t + 1) * LANE]
+            for u in range(t, t + step):
+                block = part[s * rows : (s + 1) * rows, (u - t) * LANE : (u - t + 1) * LANE]
                 if u == tiles:
                     block = jnp.concatenate([block[:half, :middle], block[half:, :middle]], axis=1)
                 out_ref[u * rows : u * rows + block.shape[0], :] = block
@@ -296,9 +328,8 @@
         out_shape=[jax.ShapeDtypeStruct((packed, LANE), BF16) for _ in range(blocks)],
         scratch_shapes=[
             pltpu.VMEM((size, size), BF16),
+            pltpu.VMEM((size, size), BF16),
             pltpu.VMEM((blocks, packed, LANE), BF16),
-            pltpu.VMEM((size, columns), BF16),
-            pltpu.VMEM((size, 2 * LANE), BF16),
             pltpu.SemaphoreType.DMA((blocks,)),
         ]
         + newton,
@@ -401,7 +432,7 @@
     returned = [[regroup(block, s) for s, block in enumerate(value)] for value in updates]
     result = None
     for g, value in enumerate(returned):
-        for far in reversed(order):
+        for far in arriving(per_group):
             first, second = value[far * SHARE], value[far * SHARE + 1]
             result = finish_call(kernel_of(g, far), side, first, second, weight, result, tiles)
     return (result, moment)
@@ -446,7 +477,7 @@
             kernels % GROUPS == 0
             and n * GROUPS == kernels * SHARE
             and n & (n - 1) == 0
-            and width % (SHARE * LANE) == LANE
+            and width % (2 * SHARE * LANE) == 3 * LANE
             and rows % 32 == 0
             and inner >= 2
             and inner & (inner - 1) == 0

time: 220 us -> 223 us (1.014)
  the two profiles are of different devices: /device:TPU:16 before, /device:TPU:0 now
where the time goes in v4:
time: 223 us; the launch traced here: 222 us
  starting transfers between devices  89.9 us (40%)
  waiting for transfers between devices  65.8 us (30%)
  Pallas kernels  61.9 us (28%)
  other arithmetic  2.89 us (1%)
    ppermute x28, starting transfers between devices, regroup(): return lax.ppermute(value, 'out', [(o, o ^ s) for o in range(n)])  75.4 us
    ppermute x28, waiting for transfers between devices, regroup(): return lax.ppermute(value, 'out', [(o, o ^ s) for o in range(n)])  50.7 us
    pallas_call x2, Pallas kernels, update_call(): pl.pallas_call(functools.partial(update_body, rows=rows, tiles=tiles, sca...  29.2 us
    pallas_call x8, Pallas kernels, source_call(): pl.pallas_call(functools.partial(source_body, rows=rows, tiles=tiles), gr...  18.8 us
    ppermute x16, waiting for transfers between devices, exchange(): return lax.ppermute(value, AXES, [(i, i ^ bits) for i in range(count)])  15.1 us
    ppermute x16, starting transfers between devices, exchange(): return lax.ppermute(value, AXES, [(i, i ^ bits) for i in range(count)])  14.5 us
    pallas_call x8, Pallas kernels, finish_call(): pl.pallas_call(functools.partial(finish_body, rows=rows, tiles=tiles), gr...  8.38 us
    pallas_call x2, Pallas kernels, gram_call(): pl.pallas_call(functools.partial(gram_body, rows=rows, tiles=tiles), in_s...  5.19 us
  transfers between devices with their start and end apart: 44, of which 21 were waited for; matrix products, arithmetic and copies ran while one was open for 1% of the time, Pallas kernels for 26%

profile of v4, /device:TPU:0, one launch (start us, length us, event | category | flops | bytes accessed | tf_op | source)
XLA Modules:
  0.0 222.4 jit_solution(12124068735128294068)
XLA Ops:
  0.7 2.3 %shard_map.60 = (bf16[864,128]{1,0:T(8,128)(2,1)}, bf16[864,128]{1,0:T(8,128)(2,1)}) custom-call(s32[1]{0:T(128)} %bitcast.9.kernel_ref, s32[1]{0:T(128)} %bitcast.1.side_ref, bf16[8,64,3456]{2,1,0:T(8,128)(2,1)} %grad_ref.15, bf16[8,64,3456]{2,1,0:T(8,128)(2,1)} %mom_ref.15), custom_call_target="tpu_custom_call" | custom-call | flops 1327104 | bytes 1327104 | tf_op jit(solution)/shard_map/pallas_call | solution.py:83
  3.0 3.1 %collective-permute-start.23 = (bf16[864,128]{1,0:T(8,128)(2,1)}, bf16[864,128]{1,0:T(8,128)(2,1)S(1)}, u32[]{:S(2)}, u32[]{:S(2)}) collective-permute-start(bf16[864,128]{1,0:T(8,128)(2,1)} %get-tuple-element.70), channel_id=1, source_target_pairs={{0,8},{4,12},{8,0},{12,4},{16,24},{20,28},{24,16},{28,20},{1,9},{5... | collective-permute-start | bytes 663560 | tf_op jit(solution)/shard_map/ppermute | solution.py:408
  7.5 2.4 %shard_map.61 = (bf16[864,128]{1,0:T(8,128)(2,1)}, bf16[864,128]{1,0:T(8,128)(2,1)}) custom-call(s32[1]{0:T(128)} %bitcast.7.kernel_ref, s32[1]{0:T(128)} %bitcast.1.side_ref, bf16[8,64,3456]{2,1,0:T(8,128)(2,1)} %grad_ref.15, bf16[8,64,3456]{2,1,0:T(8,128)(2,1)} %mom_ref.15), custom_call_target="tpu_custom_call" | custom-call | flops 1327104 | bytes 1327104 | tf_op jit(solution)/shard_map/pallas_call | solution.py:83
  9.8 2.6 %collective-permute-start.25 = (bf16[864,128]{1,0:T(8,128)(2,1)}, bf16[864,128]{1,0:T(8,128)(2,1)S(1)}, u32[]{:S(2)}, u32[]{:S(2)}) collective-permute-start(bf16[864,128]{1,0:T(8,128)(2,1)} %get-tuple-element.72), channel_id=1, source_target_pairs={{0,16},{4,20},{8,24},{12,28},{16,0},{20,4},{24,8},{28,12},{1,17},{... | collective-permute-start | bytes 663560 | tf_op jit(solution)/shard_map/ppermute | solution.py:408
  12.4 2.3 %shard_map.62 = (bf16[864,128]{1,0:T(8,128)(2,1)}, bf16[864,128]{1,0:T(8,128)(2,1)}) custom-call(s32[1]{0:T(128)} %bitcast.10.kernel_ref, s32[1]{0:T(128)} %bitcast.1.side_ref, bf16[8,64,3456]{2,1,0:T(8,128)(2,1)} %grad_ref.15, bf16[8,64,3456]{2,1,0:T(8,128)(2,1)} %mom_ref.15), custom_call_target="tpu_custom_call" | custom-call | flops 1327104 | bytes 1327104 | tf_op jit(solution)/shard_map/pallas_call | solution.py:83
  14.8 3.9 %collective-permute-start.27 = (bf16[864,128]{1,0:T(8,128)(2,1)}, bf16[864,128]{1,0:T(8,128)(2,1)S(1)}, u32[]{:S(2)}, u32[]{:S(2)}) collective-permute-start(bf16[864,128]{1,0:T(8,128)(2,1)} %get-tuple-element.74), channel_id=1, source_target_pairs={{0,24},{4,28},{8,16},{12,20},{16,8},{20,12},{24,0},{28,4},{1,25},{... | collective-permute-start | bytes 663560 | tf_op jit(solution)/shard_map/ppermute | solution.py:408
  18.6 2.4 %shard_map.59 = (bf16[864,128]{1,0:T(8,128)(2,1)}, bf16[864,128]{1,0:T(8,128)(2,1)}) custom-call(s32[1]{0:T(128)} %bitcast.8.kernel_ref, s32[1]{0:T(128)} %bitcast.1.side_ref, bf16[8,64,3456]{2,1,0:T(8,128)(2,1)} %grad_ref.15, bf16[8,64,3456]{2,1,0:T(8,128)(2,1)} %mom_ref.15), custom_call_target="tpu_custom_call" | custom-call | flops 1327104 | bytes 1327104 | tf_op jit(solution)/shard_map/pallas_call | solution.py:83
  21.0 2.3 %shard_map.51 = (bf16[864,128]{1,0:T(8,128)(2,1)}, bf16[864,128]{1,0:T(8,128)(2,1)}) custom-call(s32[1]{0:T(128)} %bitcast.5.kernel_ref, s32[1]{0:T(128)} %bitcast.1.side_ref, bf16[8,64,3456]{2,1,0:T(8,128)(2,1)} %grad_ref.15, bf16[8,64,3456]{2,1,0:T(8,128)(2,1)} %mom_ref.15), custom_call_target="tpu_custom_call" | custom-call | flops 1327104 | bytes 1327104 | tf_op jit(solution)/shard_map/pallas_call | solution.py:83
  24.9 12.7 %collective-permute-done.25.refs_4_ = bf16[864,128]{1,0:T(8,128)(2,1)S(1)} collective-permute-done((bf16[864,128]{1,0:T(8,128)(2,1)}, bf16[864,128]{1,0:T(8,128)(2,1)S(1)}, u32[]{:S(2)}, u32[]{:S(2)}) %collective-permute-start.25) | collective-permute-done | bytes 221216 | tf_op jit(solution)/shard_map/ppermute | solution.py:408
  39.1 3.5 %collective-permute-done.26.refs_5_ = bf16[864,128]{1,0:T(8,128)(2,1)S(1)} collective-permute-done((bf16[864,128]{1,0:T(8,128)(2,1)}, bf16[864,128]{1,0:T(8,128)(2,1)S(1)}, u32[]{:S(2)}, u32[]{:S(2)}) %collective-permute-start.26) | collective-permute-done | bytes 221216 | tf_op jit(solution)/shard_map/ppermute | solution.py:408
  43.8 2.4 %shard_map.52 = (bf16[864,128]{1,0:T(8,128)(2,1)}, bf16[864,128]{1,0:T(8,128)(2,1)}) custom-call(s32[1]{0:T(128)} %bitcast.kernel_ref, s32[1]{0:T(128)} %bitcast.1.side_ref, bf16[8,64,3456]{2,1,0:T(8,128)(2,1)} %grad_ref.15, bf16[8,64,3456]{2,1,0:T(8,128)(2,1)} %mom_ref.15), custom_call_target="tpu_custom_call" | custom-call | flops 1327104 | bytes 1327104 | tf_op jit(solution)/shard_map/pallas_call | solution.py:83
  46.2 4.2 %collective-permute-start.3 = (bf16[864,128]{1,0:T(8,128)(2,1)}, bf16[864,128]{1,0:T(8,128)(2,1)S(1)}, u32[]{:S(2)}, u32[]{:S(2)}) collective-permute-start(bf16[864,128]{1,0:T(8,128)(2,1)} %get-tuple-element.50), channel_id=1, source_target_pairs={{0,16},{4,20},{8,24},{12,28},{16,0},{20,4},{24,8},{28,12},{1,17},{... | collective-permute-start | bytes 663560 | tf_op jit(solution)/shard_map/ppermute | solution.py:408
  50.4 2.4 %shard_map.53 = (bf16[864,128]{1,0:T(8,128)(2,1)}, bf16[864,128]{1,0:T(8,128)(2,1)}) custom-call(s32[1]{0:T(128)} %bitcast.6.kernel_ref, s32[1]{0:T(128)} %bitcast.1.side_ref, bf16[8,64,3456]{2,1,0:T(8,128)(2,1)} %grad_ref.15, bf16[8,64,3456]{2,1,0:T(8,128)(2,1)} %mom_ref.15), custom_call_target="tpu_custom_call" | custom-call | flops 1327104 | bytes 1327104 | tf_op jit(solution)/shard_map/pallas_call | solution.py:83
  52.8 2.3 %shard_map.50 = (bf16[864,128]{1,0:T(8,128)(2,1)}, bf16[864,128]{1,0:T(8,128)(2,1)}) custom-call(s32[1]{0:T(128)} %bitcast.4.kernel_ref, s32[1]{0:T(128)} %bitcast.1.side_ref, bf16[8,64,3456]{2,1,0:T(8,128)(2,1)} %grad_ref.15, bf16[8,64,3456]{2,1,0:T(8,128)(2,1)} %mom_ref.15), custom_call_target="tpu_custom_call" | custom-call | flops 1327104 | bytes 1327104 | tf_op jit(solution)/shard_map/pallas_call | solution.py:83
  55.1 12.9 %collective-permute-start.4 = (bf16[864,128]{1,0:T(8,128)(2,1)}, bf16[864,128]{1,0:T(8,128)(2,1)S(1)}, u32[]{:S(2)}, u32[]{:S(2)}) collective-permute-start(bf16[864,128]{1,0:T(8,128)(2,1)} %get-tuple-element.51), channel_id=1, source_target_pairs={{0,20},{4,16},{8,28},{12,24},{16,4},{20,0},{24,12},{28,8},{1,21},{... | collective-permute-start | bytes 663560 | tf_op jit(solution)/shard_map/ppermute | solution.py:408
  68.1 3.8 %collective-permute-start.6 = (bf16[864,128]{1,0:T(8,128)(2,1)}, bf16[864,128]{1,0:T(8,128)(2,1)}, u32[]{:S(2)}, u32[]{:S(2)}) collective-permute-start(bf16[864,128]{1,0:T(8,128)(2,1)} %get-tuple-element.53), channel_id=1, source_target_pairs={{0,28},{4,24},{8,20},{12,16},{16,12},{20,8},{24,4},{28,0},{1,29},{... | collective-permute-start | bytes 663560 | tf_op jit(solution)/shard_map/ppermute | solution.py:408
  73.4 2.6 %shard_map.63 = (f32[256,512]{1,0:T(8,128)S(1)}, bf16[256,512]{1,0:T(8,128)(2,1)S(1)}) custom-call(s32[1]{0:T(128)} %bitcast.2.core_ref, s32[1]{0:T(128)} %bitcast.1.side_ref, bf16[864,128]{1,0:T(8,128)(2,1)S(1)} %copy-done, bf16[864,128]{1,0:T(8,128)(2,1)} %collective-permute-done.22.refs_1_, bf16[864,128]{1,0:T(8,128)(2,1)S(1)} %collective-permute-done.23.refs_2_, ...), custom_call_target="tpu_custom_call" | custom-call | flops 939524096 | bytes 3670016 | tf_op jit(solution)/shard_map/pallas_call | solution.py:125
  76.1 5.6 %collective-permute-done.4.refs_5_ = bf16[864,128]{1,0:T(8,128)(2,1)S(1)} collective-permute-done((bf16[864,128]{1,0:T(8,128)(2,1)}, bf16[864,128]{1,0:T(8,128)(2,1)S(1)}, u32[]{:S(2)}, u32[]{:S(2)}) %collective-permute-start.4) | collective-permute-done | bytes 221216 | tf_op jit(solution)/shard_map/ppermute | solution.py:408
  83.0 2.6 %shard_map.54 = (f32[256,512]{1,0:T(8,128)S(1)}, bf16[256,512]{1,0:T(8,128)(2,1)S(1)}) custom-call(s32[1]{0:T(128)} %bitcast.2.core_ref, s32[1]{0:T(128)} %bitcast.1.side_ref, bf16[864,128]{1,0:T(8,128)(2,1)S(1)} %copy-done.1, bf16[864,128]{1,0:T(8,128)(2,1)} %collective-permute-done.refs_1_, bf16[864,128]{1,0:T(8,128)(2,1)S(1)} %collective-permute-done.1.refs_2_, ...), custom_call_target="tpu_custom_call" | custom-call | flops 939524096 | bytes 3670016 | tf_op jit(solution)/shard_map/pallas_call | solution.py:125
  111.9 2.2 collective-permute-done.12.refs_2_
  115.5 14.6 %shard_map.67 = (bf16[864,128]{1,0:T(8,128)(2,1)S(1)}, bf16[864,128]{1,0:T(8,128)(2,1)S(1)}, bf16[864,128]{1,0:T(8,128)(2,1)S(1)}, bf16[864,128]{1,0:T(8,128)(2,...) custom-call(s32[1]{0:T(128)} %bitcast.2.core_ref, ...), custom_call_target="tpu_custom_call" | custom-call | flops 14629732352 | bytes 3670016 | tf_op jit(solution)/shard_map/pallas_call | solution.py:324
  131.2 7.8 %collective-permute-start.41 = (bf16[864,128]{1,0:T(8,128)(2,1)S(1)}, bf16[864,128]{1,0:T(8,128)(2,1)S(1)}, u32[]{:S(2)}, u32[]{:S(2)}) collective-permute-start(bf16[864,128]{1,0:T(8,128)(2,1)S(1)} %get-tuple-element.86), channel_id=1, source_target_pairs={{0,8},{4,12},{8,0},{12,4},{16,24},{20,28},{24,16},{28,20},{1,9},{5... | collective-permute-start | bytes 663560 | tf_op jit(solution)/shard_map/ppermute | solution.py:408
  139.4 3.5 %collective-permute-start.39 = (bf16[864,128]{1,0:T(8,128)(2,1)S(1)}, bf16[864,128]{1,0:T(8,128)(2,1)S(1)}, u32[]{:S(2)}, u32[]{:S(2)}) collective-permute-start(bf16[864,128]{1,0:T(8,128)(2,1)S(1)} %get-tuple-element.84), channel_id=1, source_target_pairs={{0,24},{4,28},{8,16},{12,20},{16,8},{20,12},{24,0},{28,4},{1,25},{... | collective-permute-start | bytes 663560 | tf_op jit(solution)/shard_map/ppermute | solution.py:408
  143.7 14.6 %shard_map.58 = (bf16[864,128]{1,0:T(8,128)(2,1)S(1)}, bf16[864,128]{1,0:T(8,128)(2,1)S(1)}, bf16[864,128]{1,0:T(8,128)(2,1)S(1)}, bf16[864,128]{1,0:T(8,128)(2,...) custom-call(s32[1]{0:T(128)} %bitcast.2.core_ref, ...), custom_call_target="tpu_custom_call" | custom-call | flops 14629732352 | bytes 3670016 | tf_op jit(solution)/shard_map/pallas_call | solution.py:324
  158.4 2.3 %collective-permute-start.37 = (bf16[864,128]{1,0:T(8,128)(2,1)S(1)}, bf16[864,128]{1,0:T(8,128)(2,1)S(1)}, u32[]{:S(2)}, u32[]{:S(2)}) collective-permute-start(bf16[864,128]{1,0:T(8,128)(2,1)S(1)} %get-tuple-element.82), channel_id=1, source_target_pairs={{0,16},{4,20},{8,24},{12,28},{16,0},{20,4},{24,8},{28,12},{1,17},{... | collective-permute-start | bytes 663560 | tf_op jit(solution)/shard_map/ppermute | solution.py:408
  164.5 11.4 %collective-permute-start.20 = (bf16[864,128]{1,0:T(8,128)(2,1)S(1)}, bf16[864,128]{1,0:T(8,128)(2,1)S(1)}, u32[]{:S(2)}, u32[]{:S(2)}) collective-permute-start(bf16[864,128]{1,0:T(8,128)(2,1)S(1)} %get-tuple-element.65), channel_id=1, source_target_pairs={{0,12},{4,8},{8,4},{12,0},{16,28},{20,24},{24,20},{28,16},{1,13},{... | collective-permute-start | bytes 663560 | tf_op jit(solution)/shard_map/ppermute | solution.py:408
  175.9 3.4 %collective-permute-done.37.first_ref = bf16[864,128]{1,0:T(8,128)(2,1)S(1)} collective-permute-done((bf16[864,128]{1,0:T(8,128)(2,1)S(1)}, bf16[864,128]{1,0:T(8,128)(2,1)S(1)}, u32[]{:S(2)}, u32[]{:S(2)}) %collective-permute-start.37) | collective-permute-done | bytes 221216 | tf_op jit(solution)/shard_map/ppermute | solution.py:408
  181.0 15.2 %collective-permute-done.38.second_ref = bf16[864,128]{1,0:T(8,128)(2,1)S(1)} collective-permute-done((bf16[864,128]{1,0:T(8,128)(2,1)S(1)}, bf16[864,128]{1,0:T(8,128)(2,1)S(1)}, u32[]{:S(2)}, u32[]{:S(2)}) %collective-permute-start.38) | collective-permute-done | bytes 221216 | tf_op jit(solution)/shard_map/ppermute | solution.py:408
  198.4 3.2 %collective-permute-start.16 = (bf16[864,128]{1,0:T(8,128)(2,1)S(1)}, bf16[864,128]{1,0:T(8,128)(2,1)S(1)}, u32[]{:S(2)}, u32[]{:S(2)}) collective-permute-start(bf16[864,128]{1,0:T(8,128)(2,1)S(1)} %get-tuple-element.61), channel_id=1, source_target_pairs={{0,20},{4,16},{8,28},{12,24},{16,4},{20,0},{24,12},{28,8},{1,21},{... | collective-permute-start | bytes 663560 | tf_op jit(solution)/shard_map/ppermute | solution.py:408
  201.7 2.9 %add_convert_fusion = bf16[8,64,3456]{2,1,0:T(8,128)(2,1)} fusion(bf16[8,64,3456]{2,1,0:T(8,128)(2,1)S(1)} %copy-done.3, bf16[8,64,3456]{2,1,0:T(8,128)(2,1)S(1)} %copy-done.4), kind=kLoop, calls=%fused_computation | loop fusion | flops 8847360 | bytes 10616832 | tf_op jit(solution)/shard_map/convert_element_type | solution.py:430
  211.9 5.2 %collective-permute-done.15.first_ref = bf16[864,128]{1,0:T(8,128)(2,1)S(1)} collective-permute-done((bf16[864,128]{1,0:T(8,128)(2,1)S(1)}, bf16[864,128]{1,0:T(8,128)(2,1)S(1)}, u32[]{:S(2)}, u32[]{:S(2)}) %collective-permute-start.15) | collective-permute-done | bytes 221216 | tf_op jit(solution)/shard_map/ppermute | solution.py:408
  217.1 4.2 %collective-permute-done.16.second_ref = bf16[864,128]{1,0:T(8,128)(2,1)S(1)} collective-permute-done((bf16[864,128]{1,0:T(8,128)(2,1)S(1)}, bf16[864,128]{1,0:T(8,128)(2,1)S(1)}, u32[]{:S(2)}, u32[]{:S(2)}) %collective-permute-start.16) | collective-permute-done | bytes 221216 | tf_op jit(solution)/shard_map/ppermute | solution.py:408
  (98 shorter events, 54.6 us)
Async XLA Ops:
  3.0 20.3 %collective-permute-start.23 = (bf16[864,128]{1,0:T(8,128)(2,1)}, bf16[864,128]{1,0:T(8,128)(2,1)S(1)}, u32[]{:S(2)}, u32[]{:S(2)}) collective-permute-start(bf16[864,128]{1,0:T(8,128)(2,1)} %get-tuple-element.70), channel_id=1, source_target_pairs={{0,8},{4,12},{8,0},{12,4},{16,24},{20,28},{24,16},{28,20},{1,9},{5... | collective-permute-start | bytes 663560 | tf_op jit(solution)/shard_map/ppermute | solution.py:408
  6.0 18.5 %collective-permute-start.24 = (bf16[864,128]{1,0:T(8,128)(2,1)}, bf16[864,128]{1,0:T(8,128)(2,1)S(1)}, u32[]{:S(2)}, u32[]{:S(2)}) collective-permute-start(bf16[864,128]{1,0:T(8,128)(2,1)} %get-tuple-element.71), channel_id=1, source_target_pairs={{0,12},{4,8},{8,4},{12,0},{16,28},{20,24},{24,20},{28,16},{1,13},{... | collective-permute-start | bytes 663560 | tf_op jit(solution)/shard_map/ppermute | solution.py:408
  9.8 27.9 %collective-permute-start.25 = (bf16[864,128]{1,0:T(8,128)(2,1)}, bf16[864,128]{1,0:T(8,128)(2,1)S(1)}, u32[]{:S(2)}, u32[]{:S(2)}) collective-permute-start(bf16[864,128]{1,0:T(8,128)(2,1)} %get-tuple-element.72), channel_id=1, source_target_pairs={{0,16},{4,20},{8,24},{12,28},{16,0},{20,4},{24,8},{28,12},{1,17},{... | collective-permute-start | bytes 663560 | tf_op jit(solution)/shard_map/ppermute | solution.py:408
  12.4 30.2 %collective-permute-start.26 = (bf16[864,128]{1,0:T(8,128)(2,1)}, bf16[864,128]{1,0:T(8,128)(2,1)S(1)}, u32[]{:S(2)}, u32[]{:S(2)}) collective-permute-start(bf16[864,128]{1,0:T(8,128)(2,1)} %get-tuple-element.73), channel_id=1, source_target_pairs={{0,20},{4,16},{8,28},{12,24},{16,4},{20,0},{24,12},{28,8},{1,21},{... | collective-permute-start | bytes 663560 | tf_op jit(solution)/shard_map/ppermute | solution.py:408
  14.8 31.4 %collective-permute-start.27 = (bf16[864,128]{1,0:T(8,128)(2,1)}, bf16[864,128]{1,0:T(8,128)(2,1)S(1)}, u32[]{:S(2)}, u32[]{:S(2)}) collective-permute-start(bf16[864,128]{1,0:T(8,128)(2,1)} %get-tuple-element.74), channel_id=1, source_target_pairs={{0,24},{4,28},{8,16},{12,20},{16,8},{20,12},{24,0},{28,4},{1,25},{... | collective-permute-start | bytes 663560 | tf_op jit(solution)/shard_map/ppermute | solution.py:408
  23.3 31.8 %collective-permute-start.28 = (bf16[864,128]{1,0:T(8,128)(2,1)}, bf16[864,128]{1,0:T(8,128)(2,1)}, u32[]{:S(2)}, u32[]{:S(2)}) collective-permute-start(bf16[864,128]{1,0:T(8,128)(2,1)} %get-tuple-element.75), channel_id=1, source_target_pairs={{0,28},{4,24},{8,20},{12,16},{16,12},{20,8},{24,4},{28,0},{1,29},{... | collective-permute-start | bytes 663560 | tf_op jit(solution)/shard_map/ppermute | solution.py:408
  24.5 43.6 %collective-permute-start.22 = (bf16[864,128]{1,0:T(8,128)(2,1)}, bf16[864,128]{1,0:T(8,128)(2,1)}, u32[]{:S(2)}, u32[]{:S(2)}) collective-permute-start(bf16[864,128]{1,0:T(8,128)(2,1)} %get-tuple-element.69), channel_id=1, source_target_pairs={{0,4},{4,0},{8,12},{12,8},{16,20},{20,16},{24,28},{28,24},{1,5},{5... | collective-permute-start | bytes 663560 | tf_op jit(solution)/shard_map/ppermute | solution.py:408
  37.7 30.4 %collective-permute-start.1 = (bf16[864,128]{1,0:T(8,128)(2,1)}, bf16[864,128]{1,0:T(8,128)(2,1)S(1)}, u32[]{:S(2)}, u32[]{:S(2)}) collective-permute-start(bf16[864,128]{1,0:T(8,128)(2,1)} %get-tuple-element.48), channel_id=1, source_target_pairs={{0,8},{4,12},{8,0},{12,4},{16,24},{20,28},{24,16},{28,20},{1,9},{5... | collective-permute-start | bytes 663560 | tf_op jit(solution)/shard_map/ppermute | solution.py:408
  42.6 29.3 %collective-permute-start.2 = (bf16[864,128]{1,0:T(8,128)(2,1)}, bf16[864,128]{1,0:T(8,128)(2,1)S(1)}, u32[]{:S(2)}, u32[]{:S(2)}) collective-permute-start(bf16[864,128]{1,0:T(8,128)(2,1)} %get-tuple-element.49), channel_id=1, source_target_pairs={{0,12},{4,8},{8,4},{12,0},{16,28},{20,24},{24,20},{28,16},{1,13},{... | collective-permute-start | bytes 663560 | tf_op jit(solution)/shard_map/ppermute | solution.py:408
  46.2 29.8 %collective-permute-start.3 = (bf16[864,128]{1,0:T(8,128)(2,1)}, bf16[864,128]{1,0:T(8,128)(2,1)S(1)}, u32[]{:S(2)}, u32[]{:S(2)}) collective-permute-start(bf16[864,128]{1,0:T(8,128)(2,1)} %get-tuple-element.50), channel_id=1, source_target_pairs={{0,16},{4,20},{8,24},{12,28},{16,0},{20,4},{24,8},{28,12},{1,17},{... | collective-permute-start | bytes 663560 | tf_op jit(solution)/shard_map/ppermute | solution.py:408
  55.1 26.5 %collective-permute-start.4 = (bf16[864,128]{1,0:T(8,128)(2,1)}, bf16[864,128]{1,0:T(8,128)(2,1)S(1)}, u32[]{:S(2)}, u32[]{:S(2)}) collective-permute-start(bf16[864,128]{1,0:T(8,128)(2,1)} %get-tuple-element.51), channel_id=1, source_target_pairs={{0,20},{4,16},{8,28},{12,24},{16,4},{20,0},{24,12},{28,8},{1,21},{... | collective-permute-start | bytes 663560 | tf_op jit(solution)/shard_map/ppermute | solution.py:408
  68.1 13.6 %collective-permute-start.5 = (bf16[864,128]{1,0:T(8,128)(2,1)}, bf16[864,128]{1,0:T(8,128)(2,1)S(1)}, u32[]{:S(2)}, u32[]{:S(2)}) collective-permute-start(bf16[864,128]{1,0:T(8,128)(2,1)} %get-tuple-element.52), channel_id=1, source_target_pairs={{0,24},{4,28},{8,16},{12,20},{16,8},{20,12},{24,0},{28,4},{1,25},{... | collective-permute-start | bytes 663560 | tf_op jit(solution)/shard_map/ppermute | solution.py:408
  68.1 13.6 %collective-permute-start.6 = (bf16[864,128]{1,0:T(8,128)(2,1)}, bf16[864,128]{1,0:T(8,128)(2,1)}, u32[]{:S(2)}, u32[]{:S(2)}) collective-permute-start(bf16[864,128]{1,0:T(8,128)(2,1)} %get-tuple-element.53), channel_id=1, source_target_pairs={{0,28},{4,24},{8,20},{12,16},{16,12},{20,8},{24,4},{28,0},{1,29},{... | collective-permute-start | bytes 663560 | tf_op jit(solution)/shard_map/ppermute | solution.py:408
  71.9 10.2 %collective-permute-start = (bf16[864,128]{1,0:T(8,128)(2,1)}, bf16[864,128]{1,0:T(8,128)(2,1)}, u32[]{:S(2)}, u32[]{:S(2)}) collective-permute-start(bf16[864,128]{1,0:T(8,128)(2,1)} %get-tuple-element.47), channel_id=1, source_target_pairs={{0,4},{4,0},{8,12},{12,8},{16,20},{20,16},{24,28},{28,24},{1,5},{5... | collective-permute-start | bytes 663560 | tf_op jit(solution)/shard_map/ppermute | solution.py:408
  76.0 9.7 %collective-permute-start.29 = (bf16[256,512]{1,0:T(8,128)(2,1)S(1)}, bf16[256,512]{1,0:T(8,128)(2,1)S(1)}, u32[]{:S(2)}, u32[]{:S(2)}) collective-permute-start(bf16[256,512]{1,0:T(8,128)(2,1)S(1)} %get-tuple-element.77), channel_id=1, source_target_pairs={{0,1},{1,0},{2,3},{3,2},{4,5},{5,4},{6,7},{7,6},{8,9},{9,8},{10,11... | collective-permute-start | bytes 786440 | tf_op jit(solution)/shard_map/ppermute | solution.py:382
  85.6 14.8 %collective-permute-start.7 = (bf16[256,512]{1,0:T(8,128)(2,1)S(1)}, bf16[256,512]{1,0:T(8,128)(2,1)S(1)}, u32[]{:S(2)}, u32[]{:S(2)}) collective-permute-start(bf16[256,512]{1,0:T(8,128)(2,1)S(1)} %get-tuple-element.55), channel_id=1, source_target_pairs={{0,1},{1,0},{2,3},{3,2},{4,5},{5,4},{6,7},{7,6},{8,9},{9,8},{10,11... | collective-permute-start | bytes 786440 | tf_op jit(solution)/shard_map/ppermute | solution.py:382
  100.4 15.1 %collective-permute-start.36 = (bf16[256,512]{1,0:T(8,128)(2,1)S(1)}, bf16[256,512]{1,0:T(8,128)(2,1)S(1)}, u32[]{:S(2)}, u32[]{:S(2)}) collective-permute-start(bf16[256,512]{1,0:T(8,128)(2,1)S(1)} %shard_map.66.own_ref), channel_id=1, source_target_pairs={{0,1},{1,0},{2,3},{3,2},{4,5},{5,4},{6,7},{7,6},{8,9},{9,8},{10,11... | collective-permute-start | bytes 786440 | tf_op jit(solution)/shard_map/ppermute | solution.py:382
  115.4 27.5 %collective-permute-start.14 = (bf16[256,512]{1,0:T(8,128)(2,1)S(1)}, bf16[256,512]{1,0:T(8,128)(2,1)S(1)}, u32[]{:S(2)}, u32[]{:S(2)}) collective-permute-start(bf16[256,512]{1,0:T(8,128)(2,1)S(1)} %shard_map.57.own_ref), channel_id=1, source_target_pairs={{0,1},{1,0},{2,3},{3,2},{4,5},{5,4},{6,7},{7,6},{8,9},{9,8},{10,11... | collective-permute-start | bytes 786440 | tf_op jit(solution)/shard_map/ppermute | solution.py:382
  130.1 28.2 %collective-permute-start.43 = (bf16[864,128]{1,0:T(8,128)(2,1)S(1)}, bf16[864,128]{1,0:T(8,128)(2,1)S(1)}, u32[]{:S(2)}, u32[]{:S(2)}) collective-permute-start(bf16[864,128]{1,0:T(8,128)(2,1)S(1)} %get-tuple-element.89), channel_id=1, source_target_pairs={{0,4},{4,0},{8,12},{12,8},{16,20},{20,16},{24,28},{28,24},{1,5},{5... | collective-permute-start | bytes 663560 | tf_op jit(solution)/shard_map/ppermute | solution.py:408
  131.2 29.5 %collective-permute-start.41 = (bf16[864,128]{1,0:T(8,128)(2,1)S(1)}, bf16[864,128]{1,0:T(8,128)(2,1)S(1)}, u32[]{:S(2)}, u32[]{:S(2)}) collective-permute-start(bf16[864,128]{1,0:T(8,128)(2,1)S(1)} %get-tuple-element.86), channel_id=1, source_target_pairs={{0,8},{4,12},{8,0},{12,4},{16,24},{20,28},{24,16},{28,20},{1,9},{5... | collective-permute-start | bytes 663560 | tf_op jit(solution)/shard_map/ppermute | solution.py:408
  138.9 22.9 %collective-permute-start.42 = (bf16[864,128]{1,0:T(8,128)(2,1)S(1)}, bf16[864,128]{1,0:T(8,128)(2,1)S(1)}, u32[]{:S(2)}, u32[]{:S(2)}) collective-permute-start(bf16[864,128]{1,0:T(8,128)(2,1)S(1)} %get-tuple-element.87), channel_id=1, source_target_pairs={{0,12},{4,8},{8,4},{12,0},{16,28},{20,24},{24,20},{28,16},{1,13},{... | collective-permute-start | bytes 663560 | tf_op jit(solution)/shard_map/ppermute | solution.py:408
  139.4 23.4 %collective-permute-start.39 = (bf16[864,128]{1,0:T(8,128)(2,1)S(1)}, bf16[864,128]{1,0:T(8,128)(2,1)S(1)}, u32[]{:S(2)}, u32[]{:S(2)}) collective-permute-start(bf16[864,128]{1,0:T(8,128)(2,1)S(1)} %get-tuple-element.84), channel_id=1, source_target_pairs={{0,24},{4,28},{8,16},{12,20},{16,8},{20,12},{24,0},{28,4},{1,25},{... | collective-permute-start | bytes 663560 | tf_op jit(solution)/shard_map/ppermute | solution.py:408
  142.9 21.5 %collective-permute-start.40 = (bf16[864,128]{1,0:T(8,128)(2,1)S(1)}, bf16[864,128]{1,0:T(8,128)(2,1)S(1)}, u32[]{:S(2)}, u32[]{:S(2)}) collective-permute-start(bf16[864,128]{1,0:T(8,128)(2,1)S(1)} %get-tuple-element.85), channel_id=1, source_target_pairs={{0,28},{4,24},{8,20},{12,16},{16,12},{20,8},{24,4},{28,0},{1,29},{... | collective-permute-start | bytes 663560 | tf_op jit(solution)/shard_map/ppermute | solution.py:408
  158.4 20.9 %collective-permute-start.37 = (bf16[864,128]{1,0:T(8,128)(2,1)S(1)}, bf16[864,128]{1,0:T(8,128)(2,1)S(1)}, u32[]{:S(2)}, u32[]{:S(2)}) collective-permute-start(bf16[864,128]{1,0:T(8,128)(2,1)S(1)} %get-tuple-element.82), channel_id=1, source_target_pairs={{0,16},{4,20},{8,24},{12,28},{16,0},{20,4},{24,8},{28,12},{1,17},{... | collective-permute-start | bytes 663560 | tf_op jit(solution)/shard_map/ppermute | solution.py:408
  160.7 35.5 %collective-permute-start.38 = (bf16[864,128]{1,0:T(8,128)(2,1)S(1)}, bf16[864,128]{1,0:T(8,128)(2,1)S(1)}, u32[]{:S(2)}, u32[]{:S(2)}) collective-permute-start(bf16[864,128]{1,0:T(8,128)(2,1)S(1)} %get-tuple-element.83), channel_id=1, source_target_pairs={{0,20},{4,16},{8,28},{12,24},{16,4},{20,0},{24,12},{28,8},{1,21},{... | collective-permute-start | bytes 663560 | tf_op jit(solution)/shard_map/ppermute | solution.py:408
  161.9 36.5 %collective-permute-start.21 = (bf16[864,128]{1,0:T(8,128)(2,1)S(1)}, bf16[864,128]{1,0:T(8,128)(2,1)S(1)}, u32[]{:S(2)}, u32[]{:S(2)}) collective-permute-start(bf16[864,128]{1,0:T(8,128)(2,1)S(1)} %get-tuple-element.67), channel_id=1, source_target_pairs={{0,4},{4,0},{8,12},{12,8},{16,20},{20,16},{24,28},{28,24},{1,5},{5... | collective-permute-start | bytes 663560 | tf_op jit(solution)/shard_map/ppermute | solution.py:408
  162.8 35.6 %collective-permute-start.19 = (bf16[864,128]{1,0:T(8,128)(2,1)S(1)}, bf16[864,128]{1,0:T(8,128)(2,1)S(1)}, u32[]{:S(2)}, u32[]{:S(2)}) collective-permute-start(bf16[864,128]{1,0:T(8,128)(2,1)S(1)} %get-tuple-element.64), channel_id=1, source_target_pairs={{0,8},{4,12},{8,0},{12,4},{16,24},{20,28},{24,16},{28,20},{1,9},{5... | collective-permute-start | bytes 663560 | tf_op jit(solution)/shard_map/ppermute | solution.py:408
  164.5 45.3 %collective-permute-start.20 = (bf16[864,128]{1,0:T(8,128)(2,1)S(1)}, bf16[864,128]{1,0:T(8,128)(2,1)S(1)}, u32[]{:S(2)}, u32[]{:S(2)}) collective-permute-start(bf16[864,128]{1,0:T(8,128)(2,1)S(1)} %get-tuple-element.65), channel_id=1, source_target_pairs={{0,12},{4,8},{8,4},{12,0},{16,28},{20,24},{24,20},{28,16},{1,13},{... | collective-permute-start | bytes 663560 | tf_op jit(solution)/shard_map/ppermute | solution.py:408
  179.3 31.6 %collective-permute-start.17 = (bf16[864,128]{1,0:T(8,128)(2,1)S(1)}, bf16[864,128]{1,0:T(8,128)(2,1)S(1)}, u32[]{:S(2)}, u32[]{:S(2)}) collective-permute-start(bf16[864,128]{1,0:T(8,128)(2,1)S(1)} %get-tuple-element.62), channel_id=1, source_target_pairs={{0,24},{4,28},{8,16},{12,20},{16,8},{20,12},{24,0},{28,4},{1,25},{... | collective-permute-start | bytes 663560 | tf_op jit(solution)/shard_map/ppermute | solution.py:408
  196.2 14.6 %collective-permute-start.18 = (bf16[864,128]{1,0:T(8,128)(2,1)S(1)}, bf16[864,128]{1,0:T(8,128)(2,1)S(1)}, u32[]{:S(2)}, u32[]{:S(2)}) collective-permute-start(bf16[864,128]{1,0:T(8,128)(2,1)S(1)} %get-tuple-element.63), channel_id=1, source_target_pairs={{0,28},{4,24},{8,20},{12,16},{16,12},{20,8},{24,4},{28,0},{1,29},{... | collective-permute-start | bytes 663560 | tf_op jit(solution)/shard_map/ppermute | solution.py:408
  198.4 18.7 %collective-permute-start.15 = (bf16[864,128]{1,0:T(8,128)(2,1)S(1)}, bf16[864,128]{1,0:T(8,128)(2,1)S(1)}, u32[]{:S(2)}, u32[]{:S(2)}) collective-permute-start(bf16[864,128]{1,0:T(8,128)(2,1)S(1)} %get-tuple-element.60), channel_id=1, source_target_pairs={{0,16},{4,20},{8,24},{12,28},{16,0},{20,4},{24,8},{28,12},{1,17},{... | collective-permute-start | bytes 663560 | tf_op jit(solution)/shard_map/ppermute | solution.py:408
  198.4 23.0 %collective-permute-start.16 = (bf16[864,128]{1,0:T(8,128)(2,1)S(1)}, bf16[864,128]{1,0:T(8,128)(2,1)S(1)}, u32[]{:S(2)}, u32[]{:S(2)}) collective-permute-start(bf16[864,128]{1,0:T(8,128)(2,1)S(1)} %get-tuple-element.61), channel_id=1, source_target_pairs={{0,20},{4,16},{8,28},{12,24},{16,4},{20,0},{24,12},{28,8},{1,21},{... | collective-permute-start | bytes 663560 | tf_op jit(solution)/shard_map/ppermute | solution.py:408
  (19 other events, 349.6 us)
